TPU v7x, 32 devices: a whole 2x2x4 slice. The times are simulated.
32 devices in a mesh: blocks: 16 (over z, y, x), cross: 2 (over core).
Axes of the slice: x: 2, y: 2, z: 4, core: 2. Of those that a mesh axis runs over, the one named last changes fastest.
Arguments:
- f_home: float32 [1024, 19, 512], P(('blocks', 'cross')), may hold values from -0.5 to 1.5
- levels: int32 [1024], P(('blocks', 'cross')), may hold values from 0 to 1, as said below
- plan: int32 [1024], P(('blocks', 'cross')), may hold values from 0 to 1023, as said below
Outputs:
- f_owner: float32 [1024, 19, 512], P(('blocks', 'cross'))
Inputs may be any that keep to these rules, and one draw needn't show every extreme that they name: `levels`: exactly a quarter of the patches, 8 times the number of devices, have level 1. plan is a permutation of the patch numbers. Of the patches in the slots of one device of f_home, at most 2 have owner slots on one device, and in every draw some device sends exactly 2 to one owner; every device's owner slots receive exactly 8 patches of level 1.
All inputs are finite; a program needn't handle non-finite values.
Results may differ from a plain program's by a relative error of at most 0.0001.
Values sent between devices are 32-bit elements; how exact they have to be, the bound alone decides.
A program may use at most 256 MiB of HBM per device.

v0:
```python
import jax
import jax.numpy as jnp
from jax import lax
from jax.experimental import pallas as pl
from jax.experimental.pallas import tpu as pltpu
from jax.sharding import PartitionSpec as P

SPAN_PATCHES = 4
DEPTH_PATCHES = 8
STEPS = 2
CELLS = 512
VELOCITIES = (
    (0, 0, 0),
    (1, 0, 0),
    (-1, 0, 0),
    (0, 1, 0),
    (0, -1, 0),
    (0, 0, 1),
    (0, 0, -1),
    (1, 1, 0),
    (-1, -1, 0),
    (1, -1, 0),
    (-1, 1, 0),
    (1, 0, 1),
    (-1, 0, -1),
    (1, 0, -1),
    (-1, 0, 1),
    (0, 1, 1),
    (0, -1, -1),
    (0, 1, -1),
    (0, -1, 1),
)
WEIGHTS = (1.0 / 3.0,) + (1.0 / 18.0,) * 6 + (1.0 / 36.0,) * 12
TAU_COARSE = 0.55
TAU_FINE = 2.0 * TAU_COARSE - 0.5
RESCALE = TAU_FINE / (2.0 * TAU_COARSE)
INFLOW = 0.08
MESH = pl.DeviceIdType.MESH
ROWS = 152
MAIN = 16
TAIL = 3
LANES = 128
TILES = CELLS // LANES
Y_UP = [q for q in range(19) if VELOCITIES[q][1] == 1]
Y_DOWN = [q for q in range(19) if VELOCITIES[q][1] == -1]
X_UP = [q for q in range(19) if VELOCITIES[q][0] == 1]
X_DOWN = [q for q in range(19) if VELOCITIES[q][0] == -1]
AROUND = [(dx, dy) for dx in (-1, 0, 1) for dy in (-1, 0, 1) if (dx, dy) != (0, 0)]


def relax_into(load, store, coef):
    f = [load(q) for q in range(19)]
    terms = list(f)
    while len(terms) > 1:
        pairs = [a + b for a, b in zip(terms[::2], terms[1::2])]
        terms = pairs + ([terms[-1]] if len(terms) % 2 else [])
    rho = terms[0]
    inv = 1.0 / rho
    u = []
    for axis in range(3):
        up = [f[q] for q in range(19) if VELOCITIES[q][axis] == 1]
        down = [f[q] for q in range(19) if VELOCITIES[q][axis] == -1]
        d = [a - b for a, b in zip(up, down)]
        u.append((((d[0] + d[1]) + (d[2] + d[3])) + d[4]) * inv)
    base = 1.0 - 1.5 * (u[0] * u[0] + u[1] * u[1] + u[2] * u[2])
    scaled = {w: w * rho for w in set(WEIGHTS)}
    for q in range(19):
        along = None
        for axis in range(3):
            e = VELOCITIES[q][axis]
            if e:
                term = u[axis] if e == 1 else -u[axis]
                along = term if along is None else along + term
        poly = base if along is None else base + along * (3.0 + 4.5 * along)
        balance = scaled[WEIGHTS[q]] * poly
        store(q, balance + coef(q) * (f[q] - balance))


def lattice_kernel(nb, nc, sidx, slot_of, level, f_ref, got_ref, table_ref, st, pb, cq, pm, sent, marks, mark_ref,
                   lev_ref, lv, ys, yr, xs, xr, send_sem, recv_sem, lsend, lrecv, psend, precv,
                   msend, mrecv):
    others = nb * nc - 1
    side = nb * nc // 2
    b = lax.axis_index("blocks")
    c = lax.axis_index("cross")

    def at(dx, dy):
        return (lax.rem(b + dx + nb, nb), lax.rem(c + dy + nc, nc))

    me = b * nc + c
    home_half = me // side
    rank = lax.rem(me, side)

    def peer(k):
        far = (1 - home_half) * side + lax.rem(rank + k, side)
        near = home_half * side + lax.rem(rank + 1 + k, side)
        return jnp.where(k < side, far, near)

    def device(d):
        return (d // nc, lax.rem(d, nc))

    barrier = pltpu.get_barrier_semaphore()

    def greet(k, carry):
        pl.semaphore_signal(barrier, inc=1, device_id=device(peer(k)), device_id_type=MESH)
        return carry

    lax.fori_loop(0, others, greet, 0)

    spot = lax.broadcasted_iota(jnp.int32, (SPAN_PATCHES, 8, LANES), 0) * 8
    spot = spot + lax.broadcasted_iota(jnp.int32, (SPAN_PATCHES, 8, LANES), 1)
    own = jnp.zeros((SPAN_PATCHES, 8, LANES), jnp.float32)
    for p in range(SPAN_PATCHES * 8):
        own = jnp.where(spot == p, level[p].astype(jnp.float32), own)
    lev_ref[...] = own

    def note(d, carry):
        row = lax.broadcasted_iota(jnp.int32, (8, LANES), 0)
        first = slot_of[2 * d].astype(jnp.float32)
        second = slot_of[2 * d + 1].astype(jnp.float32)
        marks[d] = jnp.where(row == 0, first, second)
        return carry

    lax.fori_loop(0, others + 1, note, 0)
    for q in range(19):
        for r in range(SPAN_PATCHES):
            st[q, r] = f_ref[q, r * 8 : r * 8 + 8, :]
    pl.semaphore_wait(barrier, others)

    level_copies = []
    for n, (dx, dy) in enumerate(AROUND):
        copy = pltpu.make_async_remote_copy(
            src_ref=lev_ref, dst_ref=lv.at[n], send_sem=lsend.at[n], recv_sem=lrecv.at[n],
            device_id=at(-dx, -dy), device_id_type=MESH)
        copy.start()
        level_copies.append(copy)

    def mark_copy(k):
        d = peer(k)
        return pltpu.make_async_remote_copy(
            src_ref=marks.at[d], dst_ref=mark_ref.at[me], send_sem=msend.at[k],
            recv_sem=mrecv.at[k], device_id=device(d), device_id_type=MESH)

    def patch_copy(k):
        d = peer(k)
        return pltpu.make_async_remote_copy(
            src_ref=sent.at[d], dst_ref=got_ref.at[me], send_sem=psend.at[k],
            recv_sem=precv.at[k], device_id=device(d), device_id_type=MESH)

    def start_mark(k, carry):
        mark_copy(k).start()
        return carry

    lax.fori_loop(0, others, start_mark, 0)
    mark_ref[me] = marks[me]

    for copy in level_copies:
        copy.wait()

    scale = {(0, 0): jnp.where(own > 0.5, RESCALE, 1.0)}
    for n, key in enumerate(AROUND):
        scale[key] = jnp.where(lv[n] > 0.5, RESCALE, 1.0)
    patch_scale = {}
    for dx in (-1, 0, 1):
        patch_scale[dx, 0] = scale[dx, 0]
        patch_scale[dx, 1] = jnp.concatenate([scale[dx, 0][1:], scale[dx, 1][:1]], axis=0)
        patch_scale[dx, -1] = jnp.concatenate([scale[dx, -1][-1:], scale[dx, 0][:-1]], axis=0)
    gain = jnp.where(own > 0.5, (1.0 - 1.0 / TAU_FINE) / RESCALE, 1.0 - 1.0 / TAU_COARSE)

    def target_scale(dx, dy, dz):
        value = patch_scale[dx, dy]
        return pltpu.roll(value, (-dz) % 8, axis=1) if dz else value

    shape = (SPAN_PATCHES, 8, LANES)
    lane = lax.broadcasted_iota(jnp.int32, shape, 2)
    for q in range(1, 19):
        e = VELOCITIES[q]
        kinds = [{}]
        for axis in range(3):
            if e[axis]:
                kinds = [{**k, axis: v} for k in kinds for v in (0, 1)]
        table = [(k, target_scale(*[e[a] * k.get(a, 0) for a in range(3)])) for k in kinds]
        for tile in range(TILES):
            cell = lane + tile * LANES
            coord = (cell // 64, (cell // 8) % 8, cell % 8)
            result = table[0][1]
            for k, value in table[1:]:
                mask = None
                for axis, on in k.items():
                    if on:
                        hit = coord[axis] == (7 if e[axis] == 1 else 0)
                        mask = hit if mask is None else mask & hit
                result = jnp.where(mask, value, result)
            cq[q - 1, :, :, tile * LANES : (tile + 1) * LANES] = gain * result

    full = (SPAN_PATCHES, 8, CELLS)
    cell = lax.broadcasted_iota(jnp.int32, full, 2)
    coord = (cell // 64, (cell // 8) % 8, cell % 8)
    entry = {
        (axis, e): coord[axis] == (0 if e == 1 else 7) for axis in range(3) for e in (1, -1)
    }
    half = lax.broadcasted_iota(jnp.int32, (2, 8, LANES), 2) < 64
    fine = jnp.broadcast_to(own[:, :, :1] > 0.5, full)

    def roll(v, amount):
        return pltpu.roll(v, amount % CELLS, axis=2)

    def step(s, carry):
        def first(r, tile):
            lanes = slice(tile * LANES, (tile + 1) * LANES)
            plain = jnp.where(lev_ref[r] > 0.5, 1.0 - 1.0 / TAU_FINE, 1.0 - 1.0 / TAU_COARSE)

            def put(q, value):
                pb[q, r, :, lanes] = value

            relax_into(lambda q: st[q, r, :, lanes], put,
                       lambda q: cq[q - 1, r, :, lanes] if q else plain)

        def shift_z(q, rows):
            e = VELOCITIES[q][2]
            if e:
                v = pb[q, rows]
                wrapped = pltpu.roll(roll(v, e - 8 * e), e % 8, axis=1)
                pb[q, rows] = jnp.where(entry[2, e][rows], wrapped, roll(v, e))

        def outer(m, carry):
            for tile in range(TILES):
                first(m * (SPAN_PATCHES - 1), tile)
            return carry

        lax.fori_loop(0, 2, outer, 0)
        for r in (0, SPAN_PATCHES - 1):
            for q in range(19):
                shift_z(q, slice(r, r + 1))
        for n in range(5):
            ys[s, 0, n] = pb[Y_UP[n], SPAN_PATCHES - 1]
            ys[s, 1, n] = pb[Y_DOWN[n], 0]
        y_copies = []
        for way, dy in ((0, 1), (1, -1)):
            copy = pltpu.make_async_remote_copy(
                src_ref=ys.at[s, way], dst_ref=yr.at[s, way], send_sem=send_sem.at[s, way],
                recv_sem=recv_sem.at[s, way], device_id=at(0, dy), device_id_type=MESH)
            copy.start()
            y_copies.append(copy)

        def inner(r, carry):
            for tile in range(TILES):
                first(r, tile)
            return carry

        lax.fori_loop(1, SPAN_PATCHES - 1, inner, 0)
        for q in range(19):
            shift_z(q, slice(1, SPAN_PATCHES - 1))
        st[0] = pb[0]
        st[5] = pb[5]
        st[6] = pb[6]
        def shift_x(wanted):
            for way, e, group in ((0, 1, X_UP), (1, -1, X_DOWN)):
                for n, q in enumerate(group):
                    if (VELOCITIES[q][1] != 0) != wanted:
                        continue
                    v = roll(pb[q], 64 * e)
                    pb[q] = v
                    edge = v[:, :, :LANES] if e == 1 else v[:, :, CELLS - LANES :]
                    turned = pltpu.roll(edge, 64, axis=2)
                    if e == 1:
                        xs[s, way, n] = jnp.where(half, edge[:2], turned[2:])
                    else:
                        xs[s, way, n] = jnp.where(half, turned[:2], edge[2:])

        def shift_y(wanted):
            for way, e, group in ((0, 1, Y_UP), (1, -1, Y_DOWN)):
                for n, q in enumerate(group):
                    if (VELOCITIES[q][0] != 0) != wanted:
                        continue
                    v = pb[q]
                    halo = yr[s, way, n][None]
                    if e == 1:
                        moved = jnp.concatenate([halo, v[:-1]], axis=0)
                    else:
                        moved = jnp.concatenate([v[1:], halo], axis=0)
                    v = jnp.where(entry[1, e], roll(moved, 8 * e - 64 * e), roll(v, 8 * e))
                    if wanted:
                        pb[q] = v
                    else:
                        st[q] = v

        shift_x(False)
        for copy in y_copies:
            copy.wait()
        shift_y(True)
        shift_x(True)
        x_copies = []
        for way, dx in ((0, 1), (1, -1)):
            copy = pltpu.make_async_remote_copy(
                src_ref=xs.at[s, way], dst_ref=xr.at[s, way], send_sem=send_sem.at[s, 2 + way],
                recv_sem=recv_sem.at[s, 2 + way], device_id=at(dx, 0), device_id_type=MESH)
            copy.start()
            x_copies.append(copy)
        shift_y(False)
        for q in X_UP + X_DOWN:
            st[q] = pb[q]

        def again(r, tiles):
            for tile in tiles:
                lanes = slice(tile * LANES, (tile + 1) * LANES)

                def put(q, value):
                    pb[q, r, :, lanes] = value

                relax_into(lambda q: st[q, r, :, lanes], put, lambda q: 1.0 - 1.0 / TAU_FINE)

        def middle(r, carry):
            again(r, range(1, TILES - 1))
            return carry

        lax.fori_loop(0, SPAN_PATCHES, middle, 0)
        for copy in x_copies:
            copy.wait()
        for way, e, group in ((0, 1, X_UP), (1, -1, X_DOWN)):
            outside = b == (0 if e == 1 else nb - 1)
            for n, q in enumerate(group):
                h = xr[s, way, n]
                turned = pltpu.roll(h, 64, axis=2)
                halo = jnp.concatenate([h, turned] if e == 1 else [turned, h], axis=0)
                along = e * INFLOW
                const = WEIGHTS[q] * (1.0 + 3.0 * along + 4.5 * along * along - 1.5 * INFLOW * INFLOW)
                halo = jnp.where(outside, jnp.full(halo.shape, const, jnp.float32), halo)
                if e == 1:
                    st[q, :, :, :LANES] = jnp.where(lane < 64, halo, st[q, :, :, :LANES])
                else:
                    st[q, :, :, CELLS - LANES :] = jnp.where(lane >= 64, halo, st[q, :, :, CELLS - LANES :])

        def ends(r, carry):
            again(r, (0, TILES - 1))
            return carry

        lax.fori_loop(0, SPAN_PATCHES, ends, 0)
        for q in range(19):
            e = VELOCITIES[q]
            take = fine
            for axis in range(3):
                if e[axis]:
                    take = take & ~entry[axis, e[axis]]
            moved = pb[q]
            if q:
                moved = roll(moved, 64 * e[0] + 8 * e[1] + e[2])
            st[q] = jnp.where(take, moved, st[q])
        return carry

    lax.fori_loop(0, STEPS, step, 0)

    for q in range(19):
        for r in range(SPAN_PATCHES):
            pm[r * 8 : r * 8 + 8, q, :] = st[q, r]

    def pack(d):
        for slot in range(2):
            p = sidx[2 * d + slot]
            for tile in range(TILES):
                lanes = slice(tile * LANES, (tile + 1) * LANES)
                at_row = slot * TILES + tile
                sent[d, at_row * MAIN : (at_row + 1) * MAIN, :] = pm[p, :MAIN, lanes]
                low = 2 * TILES * MAIN + at_row * TAIL
                sent[d, low : low + TAIL, :] = pm[p, MAIN:, lanes]

    def post(k, carry):
        pack(peer(k))

        @pl.when(k > 0)
        def _():
            patch_copy(k - 1).start()

        return carry

    lax.fori_loop(0, others, post, 0)
    pack(me)
    patch_copy(others - 1).start()
    got_ref[me] = sent[me]

    def marked(k, carry):
        mark_copy(k).wait()
        return carry

    lax.fori_loop(0, others, marked, 0)
    source = lax.broadcasted_iota(jnp.int32, (others + 1, LANES), 0) * 2
    wanted = lax.broadcasted_iota(jnp.int32, (others + 1, LANES), 1).astype(jnp.float32)
    index = jnp.where(mark_ref[:, 0, :] == wanted, source, 0)
    index = index + jnp.where(mark_ref[:, 1, :] == wanted, source + 1, 0)
    table_ref[...] = jnp.broadcast_to(jnp.sum(index, axis=0, keepdims=True), (8, LANES))

    def finish(k, carry):
        patch_copy(k).wait()
        return carry

    lax.fori_loop(0, others, finish, 0)


def unpack_kernel(ridx, got_ref, out_ref):
    def place(t, carry):
        a = ridx[0, t]
        src = a // 2
        slot = lax.rem(a, 2)
        tail = got_ref[src, 2 * TILES * MAIN : ROWS, :]
        for tile in range(TILES):
            lanes = slice(tile * LANES, (tile + 1) * LANES)
            low = pl.multiple_of((slot * TILES + tile) * MAIN, MAIN)
            out_ref[:MAIN, t, lanes] = got_ref[src, pl.ds(low, MAIN), :]
            other = TAIL * (TILES + tile)
            rest = jnp.where(
                slot == 0, tail[TAIL * tile : TAIL * (tile + 1)], tail[other : other + TAIL]
            )
            out_ref[MAIN:, t, lanes] = rest
        return carry

    for t in range(out_ref.shape[1]):
        place(t, 0)


def body(nb, nc, f_home, levels, plan):
    devices = nb * nc
    patches = f_home.shape[0]
    target = plan // patches
    order = jnp.arange(patches, dtype=jnp.int32)
    earlier = (target[:, None] == target[None, :]) & (order[None, :] < order[:, None])
    place = 2 * target + jnp.sum(earlier.astype(jnp.int32), axis=1)
    hit = place[None, :] == jnp.arange(2 * devices, dtype=jnp.int32)[:, None]
    sidx = jnp.sum(jnp.where(hit, order[None, :], 0), axis=1)
    slot_of = jnp.sum(jnp.where(hit, plan[None, :] % patches + 1, 0), axis=1) - 1
    vmem = pl.BlockSpec(memory_space=pltpu.VMEM)
    smem = pl.BlockSpec(memory_space=pltpu.SMEM)
    state = (19, SPAN_PATCHES, 8, CELLS)
    small = (SPAN_PATCHES, 8, LANES)
    f32 = jnp.float32
    dma = pltpu.SemaphoreType.DMA
    got, ridx = pl.pallas_call(
        lambda *refs: lattice_kernel(nb, nc, *refs),
        out_shape=(
            jax.ShapeDtypeStruct((devices, ROWS, LANES), f32),
            jax.ShapeDtypeStruct((8, LANES), jnp.int32),
        ),
        in_specs=[smem, smem, smem, vmem],
        out_specs=(vmem, vmem),
        scratch_shapes=[
            pltpu.VMEM(state, f32),
            pltpu.VMEM(state, f32),
            pltpu.VMEM((18,) + state[1:], f32),
            pltpu.VMEM((patches, 19, CELLS), f32),
            pltpu.VMEM((devices, ROWS, LANES), f32),
            pltpu.VMEM((devices, 8, LANES), f32),
            pltpu.VMEM((devices, 8, LANES), f32),
            pltpu.VMEM(small, f32),
            pltpu.VMEM((len(AROUND),) + small, f32),
            pltpu.VMEM((STEPS, 2, 5, 8, CELLS), f32),
            pltpu.VMEM((STEPS, 2, 5, 8, CELLS), f32),
            pltpu.VMEM((STEPS, 2, 5, 2, 8, LANES), f32),
            pltpu.VMEM((STEPS, 2, 5, 2, 8, LANES), f32),
            dma((STEPS, 4)),
            dma((STEPS, 4)),
            dma((len(AROUND),)),
            dma((len(AROUND),)),
            dma((devices - 1,)),
            dma((devices - 1,)),
            dma((devices - 1,)),
            dma((devices - 1,)),
        ],
        compiler_params=pltpu.CompilerParams(collective_id=0, has_side_effects=True,
                                             vmem_limit_bytes=60 * 1024 * 1024),
    )(sidx, slot_of, levels, jnp.transpose(f_home, (1, 0, 2)))
    out = pl.pallas_call(
        unpack_kernel,
        out_shape=jax.ShapeDtypeStruct((19, patches, CELLS), f32),
        in_specs=[smem, vmem],
        out_specs=vmem,
        compiler_params=pltpu.CompilerParams(vmem_limit_bytes=40 * 1024 * 1024),
    )(ridx, got)
    return jnp.transpose(out, (1, 0, 2))


def solution(mesh):
    nb, nc = mesh.shape["blocks"], mesh.shape["cross"]
    in_specs = (P(("blocks", "cross"), None, None), P(("blocks", "cross")), P(("blocks", "cross")))
    out_specs = P(("blocks", "cross"), None, None)
    return jax.shard_map(
        lambda f, l, p: body(nb, nc, f, l, p),
        mesh=mesh, in_specs=in_specs, out_specs=out_specs, check_vma=False)
```

profile of v0, /device:TPU:0, one launch (start us, length us, event | category | flops | bytes accessed | tf_op | source)
XLA Modules:
  0.0 93.7 jit_solution(12953955409429898238)
XLA Ops:
  0.0 0.7 and_select_fusion.1
  0.7 0.2 convert_reduce_fusion
  0.9 0.6 select_reduce_fusion
  1.5 0.6 broadcast_add_fusion.refs_1_
  2.1 86.7 %shard_map.37 = (f32[32,152,128]{2,1,0:T(8,128)}, s32[8,128]{1,0:T(8,128)}) custom-call(s32[64]{0:T(128)} %get-tuple-element.10.refs_0_, s32[64]{0:T(128)} %broadcast_add_fusion.refs_1_, s32[32]{0:T(128)} %refs_2_.1, f32[19,32,512]{2,1,0:T(8,128)} %bitcast.2), custom_call_target="tpu_custom_call" | custom-call | tf_op jit(solution)/shard_map/pallas_call | solution.py:436
  88.7 0.0 copy-start
  88.8 1.7 %copy-done = f32[32,152,128]{2,1,0:T(8,128)S(1)} copy-done((f32[32,152,128]{2,1,0:T(8,128)S(1)}, f32[32,152,128]{2,1,0:T(8,128)}, u32[]{:S(2)}) %copy-start) | copy-done | bytes 2490392
  90.4 0.0 copy-start.1
  90.4 0.7 copy-done.1
  91.1 2.6 %shard_map.38 = f32[19,32,512]{2,1,0:T(8,128)} custom-call(s32[8,128]{1,0:T(8,128)S(1)} %copy-done.1, f32[32,152,128]{2,1,0:T(8,128)S(1)} %copy-done), custom_call_target="tpu_custom_call" | custom-call | tf_op jit(solution)/shard_map/pallas_call | solution.py:470
  (1 shorter events, 0.0 us)
Async XLA Ops:
  88.7 1.7 %copy-start = (f32[32,152,128]{2,1,0:T(8,128)S(1)}, f32[32,152,128]{2,1,0:T(8,128)}, u32[]{:S(2)}) copy-start(f32[32,152,128]{2,1,0:T(8,128)} %get-tuple-element.8.got_ref) | copy-start | bytes 7471108
  90.4 0.7 copy-start.1
where the time goes:
time: 94.4 us; the launch traced here: 93.7 us
  Pallas kernels  89.3 us (95%)
  local copies, waits for them, and re-layouts  2.38 us (3%)
  other arithmetic  2.05 us (2%)
    pallas_call x1, Pallas kernels, body(): pl.pallas_call(lambda *refs: lattice_kernel(nb, nc, *refs), out_shape=(ja...  86.7 us
    pallas_call x1, Pallas kernels, body(): pl.pallas_call(unpack_kernel, out_shape=jax.ShapeDtypeStruct((19, patches...  2.6 us
    unnamed x4, local copies, waits for them, and re-layouts  2.38 us

commit v1 on v0

--- a/solution.py
+++ b/solution.py
@@ -88,13 +88,9 @@
         return (lax.rem(b + dx + nb, nb), lax.rem(c + dy + nc, nc))
 
     me = b * nc + c
-    home_half = me // side
-    rank = lax.rem(me, side)
 
     def peer(k):
-        far = (1 - home_half) * side + lax.rem(rank + k, side)
-        near = home_half * side + lax.rem(rank + 1 + k, side)
-        return jnp.where(k < side, far, near)
+        return lax.bitwise_xor(me, jnp.where(k < side, side + k, k - side + 1))
 
     def device(d):
         return (d // nc, lax.rem(d, nc))

time: 94.4 us -> 91.3 us (0.967)
  the two profiles are of different devices: /device:TPU:0 before, /device:TPU:17 now
where the time goes in v1:
time: 91.3 us; the launch traced here: 91.1 us
  Pallas kernels  86.6 us (95%)
  local copies, waits for them, and re-layouts  2.38 us (3%)
  other arithmetic  2.05 us (2%)
    pallas_call x1, Pallas kernels, body(): pl.pallas_call(lambda *refs: lattice_kernel(nb, nc, *refs), out_shape=(ja...  84 us
    pallas_call x1, Pallas kernels, body(): pl.pallas_call(unpack_kernel, out_shape=jax.ShapeDtypeStruct((19, patches...  2.61 us
    unnamed x4, local copies, waits for them, and re-layouts  2.38 us

profile of v1, /device:TPU:17, one launch (start us, length us, event | category | flops | bytes accessed | tf_op | source)
XLA Modules:
  0.0 91.1 jit_solution(12677284560726292004)
XLA Ops:
  0.0 0.7 and_select_fusion.1
  0.7 0.2 convert_reduce_fusion
  0.9 0.6 select_reduce_fusion
  1.5 0.6 broadcast_add_fusion.refs_1_
  2.1 84.0 %shard_map.37 = (f32[32,152,128]{2,1,0:T(8,128)}, s32[8,128]{1,0:T(8,128)}) custom-call(s32[64]{0:T(128)} %get-tuple-element.10.refs_0_, s32[64]{0:T(128)} %broadcast_add_fusion.refs_1_, s32[32]{0:T(128)} %refs_2_.1, f32[19,32,512]{2,1,0:T(8,128)} %bitcast.2), custom_call_target="tpu_custom_call" | custom-call | tf_op jit(solution)/shard_map/pallas_call | solution.py:432
  86.1 0.0 copy-start
  86.1 1.7 %copy-done = f32[32,152,128]{2,1,0:T(8,128)S(1)} copy-done((f32[32,152,128]{2,1,0:T(8,128)S(1)}, f32[32,152,128]{2,1,0:T(8,128)}, u32[]{:S(2)}) %copy-start) | copy-done | bytes 2490392
  87.8 0.0 copy-start.1
  87.8 0.7 copy-done.1
  88.4 2.6 %shard_map.38 = f32[19,32,512]{2,1,0:T(8,128)} custom-call(s32[8,128]{1,0:T(8,128)S(1)} %copy-done.1, f32[32,152,128]{2,1,0:T(8,128)S(1)} %copy-done), custom_call_target="tpu_custom_call" | custom-call | tf_op jit(solution)/shard_map/pallas_call | solution.py:466
  (1 shorter events, 0.0 us)
Async XLA Ops:
  86.1 1.7 %copy-start = (f32[32,152,128]{2,1,0:T(8,128)S(1)}, f32[32,152,128]{2,1,0:T(8,128)}, u32[]{:S(2)}) copy-start(f32[32,152,128]{2,1,0:T(8,128)} %get-tuple-element.8.got_ref) | copy-start | bytes 7471108
  87.8 0.7 copy-start.1

commit v2 on v1

--- a/solution.py
+++ b/solution.py
@@ -36,9 +36,11 @@
 RESCALE = TAU_FINE / (2.0 * TAU_COARSE)
 INFLOW = 0.08
 MESH = pl.DeviceIdType.MESH
-ROWS = 152
 MAIN = 16
 TAIL = 3
+HALF = 40
+MARK = 38
+FLAG = 39
 LANES = 128
 TILES = CELLS // LANES
 Y_UP = [q for q in range(19) if VELOCITIES[q][1] == 1]
@@ -76,9 +78,13 @@
         store(q, balance + coef(q) * (f[q] - balance))
 
 
-def lattice_kernel(nb, nc, sidx, slot_of, level, f_ref, got_ref, table_ref, st, pb, cq, pm, sent, marks, mark_ref,
-                   lev_ref, lv, ys, yr, xs, xr, send_sem, recv_sem, lsend, lrecv, psend, precv,
-                   msend, mrecv):
+def low_row(q, tile):
+    return tile % 2 * MAIN + q if q < MAIN else 2 * MAIN + tile % 2 * TAIL + q - MAIN
+
+
+def lattice_kernel(nb, nc, sidx, slot_of, level, f_ref, got_ref, left_ref, table_ref, st, pb, cq, pm, sent, second,
+                   extra, theirs, lev_ref, lv, ys, yr, xs, xr, send_sem, recv_sem, lsend, lrecv, psend,
+                   precv, esend, erecv, csend, crecv):
     others = nb * nc - 1
     side = nb * nc // 2
     b = lax.axis_index("blocks")
@@ -110,14 +116,6 @@
         own = jnp.where(spot == p, level[p].astype(jnp.float32), own)
     lev_ref[...] = own
 
-    def note(d, carry):
-        row = lax.broadcasted_iota(jnp.int32, (8, LANES), 0)
-        first = slot_of[2 * d].astype(jnp.float32)
-        second = slot_of[2 * d + 1].astype(jnp.float32)
-        marks[d] = jnp.where(row == 0, first, second)
-        return carry
-
-    lax.fori_loop(0, others + 1, note, 0)
     for q in range(19):
         for r in range(SPAN_PATCHES):
             st[q, r] = f_ref[q, r * 8 : r * 8 + 8, :]
@@ -131,24 +129,19 @@
         copy.start()
         level_copies.append(copy)
 
-    def mark_copy(k):
-        d = peer(k)
-        return pltpu.make_async_remote_copy(
-            src_ref=marks.at[d], dst_ref=mark_ref.at[me], send_sem=msend.at[k],
-            recv_sem=mrecv.at[k], device_id=device(d), device_id_type=MESH)
+    count = others + 1
 
     def patch_copy(k):
         d = peer(k)
         return pltpu.make_async_remote_copy(
-            src_ref=sent.at[d], dst_ref=got_ref.at[me], send_sem=psend.at[k],
+            src_ref=sent.at[d], dst_ref=got_ref.at[pl.ds(2 * me, 2)], send_sem=psend.at[k],
             recv_sem=precv.at[k], device_id=device(d), device_id_type=MESH)
 
-    def start_mark(k, carry):
-        mark_copy(k).start()
-        return carry
-
-    lax.fori_loop(0, others, start_mark, 0)
-    mark_ref[me] = marks[me]
+    def extra_copy(k):
+        d = peer(k)
+        return pltpu.make_async_remote_copy(
+            src_ref=extra.at[d], dst_ref=got_ref.at[2 * count + me], send_sem=esend.at[k],
+            recv_sem=erecv.at[k], device_id=device(d), device_id_type=MESH)
 
     for copy in level_copies:
         copy.wait()
@@ -346,19 +339,22 @@
 
     lax.fori_loop(0, STEPS, step, 0)
 
+    pm[:, 2 * MAIN : HALF, :] = jnp.zeros((pm.shape[0], HALF - 2 * MAIN, LANES), jnp.float32)
+    pm[:, HALF + 2 * MAIN :, :] = jnp.zeros((pm.shape[0], HALF - 2 * MAIN, LANES), jnp.float32)
     for q in range(19):
         for r in range(SPAN_PATCHES):
-            pm[r * 8 : r * 8 + 8, q, :] = st[q, r]
+            for tile in range(TILES):
+                row = tile // 2 * HALF + low_row(q, tile)
+                pm[r * 8 : r * 8 + 8, row, :] = st[q, r, :, tile * LANES : (tile + 1) * LANES]
+
+    def tag(value):
+        return jnp.full((1, LANES), value.astype(jnp.float32), jnp.float32)
 
     def pack(d):
-        for slot in range(2):
-            p = sidx[2 * d + slot]
-            for tile in range(TILES):
-                lanes = slice(tile * LANES, (tile + 1) * LANES)
-                at_row = slot * TILES + tile
-                sent[d, at_row * MAIN : (at_row + 1) * MAIN, :] = pm[p, :MAIN, lanes]
-                low = 2 * TILES * MAIN + at_row * TAIL
-                sent[d, low : low + TAIL, :] = pm[p, MAIN:, lanes]
+        p = sidx[2 * d]
+        sent[d, 0] = pm[p, :HALF]
+        sent[d, 1] = pm[p, HALF:]
+        sent[d, 0, MARK : MARK + 1, :] = tag(slot_of[2 * d])
 
     def post(k, carry):
         pack(peer(k))
@@ -371,46 +367,126 @@
 
     lax.fori_loop(0, others, post, 0)
     pack(me)
+
+    def half_rows(which):
+        return pl.ds(pl.multiple_of(which * HALF, HALF), HALF)
+
+    def pack_second(d, carry):
+        second[d] = pm[sidx[2 * d + 1], half_rows(1 - c), :]
+        second[d, MARK : MARK + 1, :] = tag(slot_of[2 * d + 1])
+        return carry
+
+    lax.fori_loop(0, count, pack_second, 0)
     patch_copy(others - 1).start()
-    got_ref[me] = sent[me]
-
-    def marked(k, carry):
-        mark_copy(k).wait()
-        return carry
-
-    lax.fori_loop(0, others, marked, 0)
-    source = lax.broadcasted_iota(jnp.int32, (others + 1, LANES), 0) * 2
-    wanted = lax.broadcasted_iota(jnp.int32, (others + 1, LANES), 1).astype(jnp.float32)
-    index = jnp.where(mark_ref[:, 0, :] == wanted, source, 0)
-    index = index + jnp.where(mark_ref[:, 1, :] == wanted, source + 1, 0)
-    table_ref[...] = jnp.broadcast_to(jnp.sum(index, axis=0, keepdims=True), (8, LANES))
+    got_ref[2 * me] = sent[me, 0]
+    got_ref[2 * me + 1] = sent[me, 1]
+    swap = pltpu.make_async_remote_copy(
+        src_ref=second, dst_ref=theirs, send_sem=csend, recv_sem=crecv,
+        device_id=at(0, 1), device_id_type=MESH)
+    swap.start()
+    swap.wait()
+    both = jnp.where((second[:, MARK, :] > -0.5) & (theirs[:, MARK, :] > -0.5), 1.0, 0.0)
+    flag = jnp.max(both, axis=0, keepdims=True)
+    zero = c == 0
+
+    def pack_extra(d):
+        mine = pm[sidx[2 * d + 1], half_rows(c), :]
+        other = theirs[d]
+        my_tag = tag(slot_of[2 * d + 1])
+        other_tag = other[MARK : MARK + 1]
+        has_mine = my_tag > -0.5
+        has_other = other_tag > -0.5
+        keep = (has_mine & zero) | ~has_other
+        extra[d] = jnp.where(keep, mine, other)
+        extra[d, MARK : MARK + 1, :] = jnp.where(keep, my_tag, other_tag)
+        extra[d, FLAG : FLAG + 1, :] = flag
+        left_ref[d] = jnp.where(zero, other, mine)
+        left_ref[d, MARK : MARK + 1, :] = jnp.where(
+            has_mine & has_other, jnp.where(zero, other_tag, my_tag), -1.0
+        )
+
+    def post_extra(k, carry):
+        pack_extra(peer(k))
+
+        @pl.when(k > 0)
+        def _():
+            extra_copy(k - 1).start()
+
+        return carry
+
+    lax.fori_loop(0, others, post_extra, 0)
+    pack_extra(me)
+    extra_copy(others - 1).start()
+    got_ref[2 * count + me] = extra[me]
 
     def finish(k, carry):
         patch_copy(k).wait()
+        extra_copy(k).wait()
         return carry
 
     lax.fori_loop(0, others, finish, 0)
+    source = lax.broadcasted_iota(jnp.int32, (2 * count, LANES), 0)
+    wanted = lax.broadcasted_iota(jnp.int32, (2 * count, LANES), 1).astype(jnp.float32)
+    first_hit = (got_ref[: 2 * count, MARK, :] == wanted) & (source % 2 == 0)
+    index = jnp.sum(jnp.where(first_hit, source, 0), axis=0, keepdims=True)
+    source = source[:count]
+    extra_hit = (got_ref[2 * count :, MARK, :] == wanted[:count]) & (source % nc == 0)
+    index = index + jnp.sum(jnp.where(extra_hit, source + 2 * count, 0), axis=0, keepdims=True)
+    over = jnp.max(got_ref[2 * count :, FLAG, :], axis=0, keepdims=True)
+    row = lax.broadcasted_iota(jnp.int32, (8, LANES), 0)
+    table_ref[...] = jnp.where(row == 0, index, jnp.where(over > 0.5, 1, 0))
+
+
+def leftover_kernel(nb, nc, left_ref, table_ref, got_ref, new_table_ref, send_sem, recv_sem):
+    count = nb * nc
+    me = lax.axis_index("blocks") * nc + lax.axis_index("cross")
+
+    def device(d):
+        return (d // nc, lax.rem(d, nc))
+
+    barrier = pltpu.get_barrier_semaphore()
+
+    def greet(k, carry):
+        pl.semaphore_signal(barrier, inc=1, device_id=device(lax.bitwise_xor(me, k)), device_id_type=MESH)
+        return carry
+
+    lax.fori_loop(1, count, greet, 0)
+    pl.semaphore_wait(barrier, count - 1)
+
+    def left_copy(k):
+        d = lax.bitwise_xor(me, k)
+        return pltpu.make_async_remote_copy(
+            src_ref=left_ref.at[d], dst_ref=got_ref.at[me], send_sem=send_sem.at[k],
+            recv_sem=recv_sem.at[k], device_id=device(d), device_id_type=MESH)
+
+    def post(k, carry):
+        left_copy(k).start()
+        return carry
+
+    def finish(k, carry):
+        left_copy(k).wait()
+        return carry
+
+    lax.fori_loop(1, count, post, 0)
+    got_ref[me] = left_ref[me]
+    lax.fori_loop(1, count, finish, 0)
+    source = lax.broadcasted_iota(jnp.int32, (count, LANES), 0)
+    wanted = lax.broadcasted_iota(jnp.int32, (count, LANES), 1).astype(jnp.float32)
+    hit = (got_ref[:, MARK, :] == wanted) & (source % nc == 0)
+    index = jnp.sum(jnp.where(hit, source + 3 * count, 0), axis=0, keepdims=True)
+    new_table_ref[...] = table_ref[...] + index
 
 
 def unpack_kernel(ridx, got_ref, out_ref):
-    def place(t, carry):
-        a = ridx[0, t]
-        src = a // 2
-        slot = lax.rem(a, 2)
-        tail = got_ref[src, 2 * TILES * MAIN : ROWS, :]
+    for t in range(out_ref.shape[1]):
+        base = ridx[0, t]
         for tile in range(TILES):
+            block = got_ref.at[base + tile // 2]
             lanes = slice(tile * LANES, (tile + 1) * LANES)
-            low = pl.multiple_of((slot * TILES + tile) * MAIN, MAIN)
-            out_ref[:MAIN, t, lanes] = got_ref[src, pl.ds(low, MAIN), :]
-            other = TAIL * (TILES + tile)
-            rest = jnp.where(
-                slot == 0, tail[TAIL * tile : TAIL * (tile + 1)], tail[other : other + TAIL]
-            )
-            out_ref[MAIN:, t, lanes] = rest
-        return carry
-
-    for t in range(out_ref.shape[1]):
-        place(t, 0)
+            low = low_row(0, tile)
+            out_ref[:MAIN, t, lanes] = block[low : low + MAIN, :]
+            low = low_row(MAIN, tile)
+            out_ref[MAIN:, t, lanes] = block[2 * MAIN :, :][low - 2 * MAIN : low - 2 * MAIN + TAIL]
 
 
 def body(nb, nc, f_home, levels, plan):
@@ -429,22 +505,26 @@
     small = (SPAN_PATCHES, 8, LANES)
     f32 = jnp.float32
     dma = pltpu.SemaphoreType.DMA
-    got, ridx = pl.pallas_call(
+    half = (HALF, LANES)
+    limit = pltpu.CompilerParams(collective_id=0, has_side_effects=True, vmem_limit_bytes=60 * 1024 * 1024)
+    got, left, table = pl.pallas_call(
         lambda *refs: lattice_kernel(nb, nc, *refs),
         out_shape=(
-            jax.ShapeDtypeStruct((devices, ROWS, LANES), f32),
+            jax.ShapeDtypeStruct((3 * devices,) + half, f32),
+            jax.ShapeDtypeStruct((devices,) + half, f32),
             jax.ShapeDtypeStruct((8, LANES), jnp.int32),
         ),
         in_specs=[smem, smem, smem, vmem],
-        out_specs=(vmem, vmem),
+        out_specs=(vmem, vmem, vmem),
         scratch_shapes=[
             pltpu.VMEM(state, f32),
             pltpu.VMEM(state, f32),
             pltpu.VMEM((18,) + state[1:], f32),
-            pltpu.VMEM((patches, 19, CELLS), f32),
-            pltpu.VMEM((devices, ROWS, LANES), f32),
-            pltpu.VMEM((devices, 8, LANES), f32),
-            pltpu.VMEM((devices, 8, LANES), f32),
+            pltpu.VMEM((patches, 2 * HALF, LANES), f32),
+            pltpu.VMEM((devices, 2) + half, f32),
+            pltpu.VMEM((devices,) + half, f32),
+            pltpu.VMEM((devices,) + half, f32),
+            pltpu.VMEM((devices,) + half, f32),
             pltpu.VMEM(small, f32),
             pltpu.VMEM((len(AROUND),) + small, f32),
             pltpu.VMEM((STEPS, 2, 5, 8, CELLS), f32),
@@ -459,17 +539,36 @@
             dma((devices - 1,)),
             dma((devices - 1,)),
             dma((devices - 1,)),
+            dma,
+            dma,
         ],
-        compiler_params=pltpu.CompilerParams(collective_id=0, has_side_effects=True,
-                                             vmem_limit_bytes=60 * 1024 * 1024),
+        compiler_params=limit,
     )(sidx, slot_of, levels, jnp.transpose(f_home, (1, 0, 2)))
-    out = pl.pallas_call(
-        unpack_kernel,
-        out_shape=jax.ShapeDtypeStruct((19, patches, CELLS), f32),
-        in_specs=[smem, vmem],
-        out_specs=vmem,
-        compiler_params=pltpu.CompilerParams(vmem_limit_bytes=40 * 1024 * 1024),
-    )(ridx, got)
+
+    def unpack(table, got):
+        return pl.pallas_call(
+            unpack_kernel,
+            out_shape=jax.ShapeDtypeStruct((19, patches, CELLS), f32),
+            in_specs=[smem, vmem],
+            out_specs=vmem,
+            compiler_params=pltpu.CompilerParams(vmem_limit_bytes=40 * 1024 * 1024),
+        )(table, got)
+
+    def with_leftover(table, got, left):
+        more, table = pl.pallas_call(
+            lambda *refs: leftover_kernel(nb, nc, *refs),
+            out_shape=(
+                jax.ShapeDtypeStruct((devices,) + half, f32),
+                jax.ShapeDtypeStruct((8, LANES), jnp.int32),
+            ),
+            in_specs=[vmem, vmem],
+            out_specs=(vmem, vmem),
+            scratch_shapes=[dma((devices,)), dma((devices,))],
+            compiler_params=pltpu.CompilerParams(collective_id=1, has_side_effects=True),
+        )(left, table)
+        return unpack(table, jnp.concatenate([got, more], axis=0))
+
+    out = lax.cond(table[1, 0] > 0, with_leftover, lambda table, got, left: unpack(table, got), table, got, left)
     return jnp.transpose(out, (1, 0, 2))
 
 

time: 91.3 us -> 77.2 us (0.85)
  the two profiles are of different devices: /device:TPU:17 before, /device:TPU:0 now
where the time goes in v2:
time: 77.2 us; the launch traced here: 76.1 us
  Pallas kernels  71.9 us (93%)
  other arithmetic  2.03 us (3%)
  local copies, waits for them, and re-layouts  1.54 us (2%)
    pallas_call x1, Pallas kernels, body(): pl.pallas_call(lambda *refs: lattice_kernel(nb, nc, *refs), out_shape=(ja...  70.5 us

profile of v2, /device:TPU:0, one launch (start us, length us, event | category | flops | bytes accessed | tf_op | source)
XLA Modules:
  0.0 76.1 jit_solution(13713146250992812966)
XLA Ops:
  0.0 0.7 and_select_fusion.1
  0.7 0.2 convert_reduce_fusion
  0.9 0.6 select_reduce_fusion
  1.5 0.6 broadcast_add_fusion.refs_1_
  2.0 70.5 %shard_map.37 = (f32[96,40,128]{2,1,0:T(8,128)S(1)}, f32[32,40,128]{2,1,0:T(8,128)}, s32[8,128]{1,0:T(8,128)S(1)}) custom-call(s32[64]{0:T(128)} %get-tuple-element.32.refs_0_, s32[64]{0:T(128)} %broadcast_add_fusion.refs_1_, s32[32]{0:T(128)} %refs_2_.1, f32[19,32,512]{2,1,0:T(8,128)} %bitcast.3), custom_call_target="tpu_custom_call" | custom-call | tf_op jit(solution)/shard_map/pallas_call | solution.py:510
  72.5 0.5 slice.3
  73.7 1.4 %conditional.1 = (f32[19,32,512]{2,1,0:T(8,128)S(1)}) conditional(s32[]{:T(128)} %bitcast.1, (s32[8,128]{1,0:T(8,128)S(1)}, f32[96,40,128]{2,1,0:T(8,128)S(1)}) %tuple.11, (f32[32,40,128]{2,1,0:T(8,128)}, s32[8,128]{1,0:T(8,128)S(1)}, f32[96,40,128]{2,1,0:T(8,128)S(1)}) %tuple.12), branch_computations={%region_3.4_spmd, %region_4.5_spmd} | conditional | flops 655360 | bytes 5259300 | solution.py:571
  73.7 1.4 %branch_0_fun.1 = f32[19,32,512]{2,1,0:T(8,128)S(1)} custom-call(s32[8,128]{1,0:T(8,128)S(1)} %get-tuple-element.18.ridx, f32[96,40,128]{2,1,0:T(8,128)S(1)} %get-tuple-element.19.got_ref), custom_call_target="tpu_custom_call" | custom-call | tf_op jit(solution)/shard_map/cond/branch_0_fun/pallas_call | solution.py:549
  75.1 0.0 copy-start.1
  75.1 1.0 %copy-done.1 = f32[19,32,512]{2,1,0:T(8,128)} copy-done((f32[19,32,512]{2,1,0:T(8,128)}, f32[19,32,512]{2,1,0:T(8,128)S(1)}, u32[]{:S(2)}) %copy-start.1) | copy-done | bytes 1245208
  (1 shorter events, 0.0 us)
Async XLA Ops:
  75.1 1.0 %copy-start.1 = (f32[19,32,512]{2,1,0:T(8,128)}, f32[19,32,512]{2,1,0:T(8,128)S(1)}, u32[]{:S(2)}) copy-start(f32[19,32,512]{2,1,0:T(8,128)S(1)} %get-tuple-element.35) | copy-start | bytes 3735556

commit v3 on v2

--- a/solution.py
+++ b/solution.py
@@ -47,6 +47,7 @@
 Y_DOWN = [q for q in range(19) if VELOCITIES[q][1] == -1]
 X_UP = [q for q in range(19) if VELOCITIES[q][0] == 1]
 X_DOWN = [q for q in range(19) if VELOCITIES[q][0] == -1]
+DIAGONAL = [q for q in range(19) if VELOCITIES[q][0] and VELOCITIES[q][1]]
 AROUND = [(dx, dy) for dx in (-1, 0, 1) for dy in (-1, 0, 1) if (dx, dy) != (0, 0)]
 
 
@@ -83,7 +84,7 @@
 
 
 def lattice_kernel(nb, nc, sidx, slot_of, level, f_ref, got_ref, left_ref, table_ref, st, pb, cq, pm, sent, second,
-                   extra, theirs, lev_ref, lv, ys, yr, xs, xr, send_sem, recv_sem, lsend, lrecv, psend,
+                   extra, theirs, lev_ref, lv, ys, yr, xs, xr, ds, dr, send_sem, recv_sem, lsend, lrecv, psend,
                    precv, esend, erecv, csend, crecv):
     others = nb * nc - 1
     side = nb * nc // 2
@@ -188,111 +189,120 @@
     entry = {
         (axis, e): coord[axis] == (0 if e == 1 else 7) for axis in range(3) for e in (1, -1)
     }
+    lower = lane < 64
     half = lax.broadcasted_iota(jnp.int32, (2, 8, LANES), 2) < 64
     fine = jnp.broadcast_to(own[:, :, :1] > 0.5, full)
-
-    def roll(v, amount):
-        return pltpu.roll(v, amount % CELLS, axis=2)
+    in_tile = {
+        (axis, e): (lane // 8 % 8 if axis == 1 else lane % 8) == (0 if e == 1 else 7)
+        for axis in (1, 2) for e in (1, -1)
+    }
+
+    def spin(v, amount):
+        return pltpu.roll(v, amount % LANES, axis=v.ndim - 1)
+
+    def along_z(q, v):
+        e = VELOCITIES[q][2]
+        if not e:
+            return v
+        wrapped = pltpu.roll(spin(v, -7 * e), e % 8, axis=1)
+        return jnp.where(in_tile[2, e][: v.shape[0]], wrapped, spin(v, e))
+
+    def along_y(q, v, halo):
+        e = VELOCITIES[q][1]
+        moved = jnp.concatenate([halo, v[:-1]] if e == 1 else [v[1:], halo], axis=0)
+        return jnp.where(in_tile[1, e], spin(moved, -56 * e), spin(v, 8 * e))
+
+    def lanes_of(tile):
+        return slice(tile * LANES, (tile + 1) * LANES)
 
     def step(s, carry):
-        def first(r, tile):
-            lanes = slice(tile * LANES, (tile + 1) * LANES)
+        def first(r, tiles):
             plain = jnp.where(lev_ref[r] > 0.5, 1.0 - 1.0 / TAU_FINE, 1.0 - 1.0 / TAU_COARSE)
-
-            def put(q, value):
-                pb[q, r, :, lanes] = value
-
-            relax_into(lambda q: st[q, r, :, lanes], put,
-                       lambda q: cq[q - 1, r, :, lanes] if q else plain)
-
-        def shift_z(q, rows):
-            e = VELOCITIES[q][2]
-            if e:
-                v = pb[q, rows]
-                wrapped = pltpu.roll(roll(v, e - 8 * e), e % 8, axis=1)
-                pb[q, rows] = jnp.where(entry[2, e][rows], wrapped, roll(v, e))
+            for tile in tiles:
+                lanes = lanes_of(tile)
+
+                def put(q, value):
+                    pb[q, r, :, lanes] = value
+
+                relax_into(lambda q: st[q, r, :, lanes], put,
+                           lambda q: cq[q - 1, r, :, lanes] if q else plain)
+
+        def faces(r, carry):
+            first(r, (0, TILES - 1))
+            return carry
+
+        lax.fori_loop(0, SPAN_PATCHES, faces, 0)
+        for way, e, group in ((0, 1, X_UP), (1, -1, X_DOWN)):
+            for n, q in enumerate(group):
+                v = along_z(q, pb[q, :, :, lanes_of(TILES - 1 if e == 1 else 0)])
+                turned = spin(v, 64)
+                if e == 1:
+                    xs[s, way, n] = jnp.where(half, turned[:2], v[2:])
+                else:
+                    xs[s, way, n] = jnp.where(half, v[:2], turned[2:])
+                if q in DIAGONAL:
+                    ds[s, DIAGONAL.index(q)] = turned[SPAN_PATCHES - 1 if VELOCITIES[q][1] == 1 else 0]
+        x_copies = []
+
+        def send(src, dst, n, to):
+            copy = pltpu.make_async_remote_copy(
+                src_ref=src, dst_ref=dst, send_sem=send_sem.at[s, n], recv_sem=recv_sem.at[s, n],
+                device_id=to, device_id_type=MESH)
+            copy.start()
+            return copy
 
         def outer(m, carry):
-            for tile in range(TILES):
-                first(m * (SPAN_PATCHES - 1), tile)
+            first(m * (SPAN_PATCHES - 1), range(1, TILES - 1))
             return carry
 
+        def inner(r, carry):
+            first(r, range(1, TILES - 1))
+            return carry
+
+        for way, dx in ((0, 1), (1, -1)):
+            x_copies.append(send(xs.at[s, way], xr.at[s, way], 2 + way, at(dx, 0)))
+        for n, q in enumerate(DIAGONAL):
+            x_copies.append(send(ds.at[s, n], dr.at[s, n], 4 + n, at(*VELOCITIES[q][:2])))
         lax.fori_loop(0, 2, outer, 0)
-        for r in (0, SPAN_PATCHES - 1):
-            for q in range(19):
-                shift_z(q, slice(r, r + 1))
-        for n in range(5):
-            ys[s, 0, n] = pb[Y_UP[n], SPAN_PATCHES - 1]
-            ys[s, 1, n] = pb[Y_DOWN[n], 0]
+        for way, e, group in ((0, 1, Y_UP), (1, -1, Y_DOWN)):
+            r = SPAN_PATCHES - 1 if e == 1 else 0
+            for n, q in enumerate(group):
+                for tile in range(TILES):
+                    ys[s, way, n, :, lanes_of(tile)] = along_z(q, pb[q, r : r + 1, :, lanes_of(tile)])[0]
         y_copies = []
         for way, dy in ((0, 1), (1, -1)):
-            copy = pltpu.make_async_remote_copy(
-                src_ref=ys.at[s, way], dst_ref=yr.at[s, way], send_sem=send_sem.at[s, way],
-                recv_sem=recv_sem.at[s, way], device_id=at(0, dy), device_id_type=MESH)
-            copy.start()
-            y_copies.append(copy)
-
-        def inner(r, carry):
+            y_copies.append(send(ys.at[s, way], yr.at[s, way], way, at(0, dy)))
+        lax.fori_loop(1, SPAN_PATCHES - 1, inner, 0)
+
+        def shift(q):
+            e = VELOCITIES[q]
+            tiles = [along_z(q, pb[q, :, :, lanes_of(tile)]) for tile in range(TILES)]
+            if e[1]:
+                way, group = (0, Y_UP) if e[1] == 1 else (1, Y_DOWN)
+                n = group.index(q)
+                tiles = [along_y(q, v, yr[s, way, n, :, lanes_of(tile)][None]) for tile, v in enumerate(tiles)]
+            if e[0]:
+                turned = [spin(v, 64) for v in tiles]
+                for tile in range(TILES):
+                    if e[0] == 1:
+                        tiles[tile] = jnp.where(lower, turned[tile - 1], turned[tile])
+                    else:
+                        tiles[tile] = jnp.where(lower, turned[tile], turned[(tile + 1) % TILES])
             for tile in range(TILES):
-                first(r, tile)
-            return carry
-
-        lax.fori_loop(1, SPAN_PATCHES - 1, inner, 0)
+                st[q, :, :, lanes_of(tile)] = tiles[tile]
+
         for q in range(19):
-            shift_z(q, slice(1, SPAN_PATCHES - 1))
-        st[0] = pb[0]
-        st[5] = pb[5]
-        st[6] = pb[6]
-        def shift_x(wanted):
-            for way, e, group in ((0, 1, X_UP), (1, -1, X_DOWN)):
-                for n, q in enumerate(group):
-                    if (VELOCITIES[q][1] != 0) != wanted:
-                        continue
-                    v = roll(pb[q], 64 * e)
-                    pb[q] = v
-                    edge = v[:, :, :LANES] if e == 1 else v[:, :, CELLS - LANES :]
-                    turned = pltpu.roll(edge, 64, axis=2)
-                    if e == 1:
-                        xs[s, way, n] = jnp.where(half, edge[:2], turned[2:])
-                    else:
-                        xs[s, way, n] = jnp.where(half, turned[:2], edge[2:])
-
-        def shift_y(wanted):
-            for way, e, group in ((0, 1, Y_UP), (1, -1, Y_DOWN)):
-                for n, q in enumerate(group):
-                    if (VELOCITIES[q][0] != 0) != wanted:
-                        continue
-                    v = pb[q]
-                    halo = yr[s, way, n][None]
-                    if e == 1:
-                        moved = jnp.concatenate([halo, v[:-1]], axis=0)
-                    else:
-                        moved = jnp.concatenate([v[1:], halo], axis=0)
-                    v = jnp.where(entry[1, e], roll(moved, 8 * e - 64 * e), roll(v, 8 * e))
-                    if wanted:
-                        pb[q] = v
-                    else:
-                        st[q] = v
-
-        shift_x(False)
+            if not VELOCITIES[q][1]:
+                shift(q)
         for copy in y_copies:
             copy.wait()
-        shift_y(True)
-        shift_x(True)
-        x_copies = []
-        for way, dx in ((0, 1), (1, -1)):
-            copy = pltpu.make_async_remote_copy(
-                src_ref=xs.at[s, way], dst_ref=xr.at[s, way], send_sem=send_sem.at[s, 2 + way],
-                recv_sem=recv_sem.at[s, 2 + way], device_id=at(dx, 0), device_id_type=MESH)
-            copy.start()
-            x_copies.append(copy)
-        shift_y(False)
-        for q in X_UP + X_DOWN:
-            st[q] = pb[q]
+        for q in range(19):
+            if VELOCITIES[q][1]:
+                shift(q)
 
         def again(r, tiles):
             for tile in tiles:
-                lanes = slice(tile * LANES, (tile + 1) * LANES)
+                lanes = lanes_of(tile)
 
                 def put(q, value):
                     pb[q, r, :, lanes] = value
@@ -310,15 +320,16 @@
             outside = b == (0 if e == 1 else nb - 1)
             for n, q in enumerate(group):
                 h = xr[s, way, n]
-                turned = pltpu.roll(h, 64, axis=2)
+                turned = spin(h, 64)
                 halo = jnp.concatenate([h, turned] if e == 1 else [turned, h], axis=0)
+                if q in DIAGONAL:
+                    halo = along_y(q, halo, dr[s, DIAGONAL.index(q)][None])
                 along = e * INFLOW
                 const = WEIGHTS[q] * (1.0 + 3.0 * along + 4.5 * along * along - 1.5 * INFLOW * INFLOW)
                 halo = jnp.where(outside, jnp.full(halo.shape, const, jnp.float32), halo)
-                if e == 1:
-                    st[q, :, :, :LANES] = jnp.where(lane < 64, halo, st[q, :, :, :LANES])
-                else:
-                    st[q, :, :, CELLS - LANES :] = jnp.where(lane >= 64, halo, st[q, :, :, CELLS - LANES :])
+                lanes = lanes_of(0 if e == 1 else TILES - 1)
+                keep = st[q, :, :, lanes]
+                st[q, :, :, lanes] = jnp.where(lower, halo, keep) if e == 1 else jnp.where(lower, keep, halo)
 
         def ends(r, carry):
             again(r, (0, TILES - 1))
@@ -333,7 +344,7 @@
                     take = take & ~entry[axis, e[axis]]
             moved = pb[q]
             if q:
-                moved = roll(moved, 64 * e[0] + 8 * e[1] + e[2])
+                moved = pltpu.roll(moved, (64 * e[0] + 8 * e[1] + e[2]) % CELLS, axis=2)
             st[q] = jnp.where(take, moved, st[q])
         return carry
 
@@ -531,8 +542,10 @@
             pltpu.VMEM((STEPS, 2, 5, 8, CELLS), f32),
             pltpu.VMEM((STEPS, 2, 5, 2, 8, LANES), f32),
             pltpu.VMEM((STEPS, 2, 5, 2, 8, LANES), f32),
-            dma((STEPS, 4)),
-            dma((STEPS, 4)),
+            pltpu.VMEM((STEPS, len(DIAGONAL), 8, LANES), f32),
+            pltpu.VMEM((STEPS, len(DIAGONAL), 8, LANES), f32),
+            dma((STEPS, 8)),
+            dma((STEPS, 8)),
             dma((len(AROUND),)),
             dma((len(AROUND),)),
             dma((devices - 1,)),

time: 77.2 us -> 74.8 us (0.969)
  Pallas kernels: 71.9 us -> 69.4 us
    pallas_call x1, Pallas kernels: 70.5 us -> 68 us  [body(): pl.pallas_call(lambda *refs: lattice_kernel(nb, nc, *refs), out_shape=(ja...]
where the time goes in v3:
time: 74.8 us; the launch traced here: 73.7 us
  Pallas kernels  69.4 us (93%)
  other arithmetic  2.03 us (3%)
  local copies, waits for them, and re-layouts  1.54 us (2%)
    pallas_call x1, Pallas kernels, body(): pl.pallas_call(lambda *refs: lattice_kernel(nb, nc, *refs), out_shape=(ja...  68 us

profile of v3, /device:TPU:0, one launch (start us, length us, event | category | flops | bytes accessed | tf_op | source)
XLA Modules:
  0.0 73.7 jit_solution(4907875987916608384)
XLA Ops:
  0.0 0.7 and_select_fusion.1
  0.7 0.2 convert_reduce_fusion
  0.9 0.6 select_reduce_fusion
  1.5 0.6 broadcast_add_fusion.refs_1_
  2.0 68.0 %shard_map.37 = (f32[96,40,128]{2,1,0:T(8,128)S(1)}, f32[32,40,128]{2,1,0:T(8,128)}, s32[8,128]{1,0:T(8,128)S(1)}) custom-call(s32[64]{0:T(128)} %get-tuple-element.32.refs_0_, s32[64]{0:T(128)} %broadcast_add_fusion.refs_1_, s32[32]{0:T(128)} %refs_2_.1, f32[19,32,512]{2,1,0:T(8,128)} %bitcast.3), custom_call_target="tpu_custom_call" | custom-call | tf_op jit(solution)/shard_map/pallas_call | solution.py:521
  70.1 0.5 slice.3
  71.2 1.4 %conditional.1 = (f32[19,32,512]{2,1,0:T(8,128)S(1)}) conditional(s32[]{:T(128)} %bitcast.1, (s32[8,128]{1,0:T(8,128)S(1)}, f32[96,40,128]{2,1,0:T(8,128)S(1)}) %tuple.11, (f32[32,40,128]{2,1,0:T(8,128)}, s32[8,128]{1,0:T(8,128)S(1)}, f32[96,40,128]{2,1,0:T(8,128)S(1)}) %tuple.12), branch_computations={%region_3.4_spmd, %region_4.5_spmd} | conditional | flops 655360 | bytes 5259300 | solution.py:584
  71.2 1.4 %branch_0_fun.1 = f32[19,32,512]{2,1,0:T(8,128)S(1)} custom-call(s32[8,128]{1,0:T(8,128)S(1)} %get-tuple-element.18.ridx, f32[96,40,128]{2,1,0:T(8,128)S(1)} %get-tuple-element.19.got_ref), custom_call_target="tpu_custom_call" | custom-call | tf_op jit(solution)/shard_map/cond/branch_0_fun/pallas_call | solution.py:562
  72.6 0.0 copy-start.1
  72.6 1.0 %copy-done.1 = f32[19,32,512]{2,1,0:T(8,128)} copy-done((f32[19,32,512]{2,1,0:T(8,128)}, f32[19,32,512]{2,1,0:T(8,128)S(1)}, u32[]{:S(2)}) %copy-start.1) | copy-done | bytes 1245208
  (1 shorter events, 0.0 us)
Async XLA Ops:
  72.6 1.0 %copy-start.1 = (f32[19,32,512]{2,1,0:T(8,128)}, f32[19,32,512]{2,1,0:T(8,128)S(1)}, u32[]{:S(2)}) copy-start(f32[19,32,512]{2,1,0:T(8,128)S(1)} %get-tuple-element.35) | copy-start | bytes 3735556

commit v4 on v3

--- a/solution.py
+++ b/solution.py
@@ -83,10 +83,11 @@
     return tile % 2 * MAIN + q if q < MAIN else 2 * MAIN + tile % 2 * TAIL + q - MAIN
 
 
-def lattice_kernel(nb, nc, sidx, slot_of, level, f_ref, got_ref, left_ref, table_ref, st, pb, cq, pm, sent, second,
-                   extra, theirs, lev_ref, lv, ys, yr, xs, xr, ds, dr, send_sem, recv_sem, lsend, lrecv, psend,
-                   precv, esend, erecv, csend, crecv):
+def lattice_kernel(nb, nc, level, plan_ref, f_ref, got_ref, left_ref, table_ref, st, pb, cq, pm, sent, second,
+                   extra, theirs, lev_ref, lv, ys, yr, xs, xr, ds, dr, pick, pick_s, tags, send_sem, recv_sem, lsend, lrecv, psend,
+                   precv, esend, erecv, csend, crecv, pick_sem, up_sem, down_sem):
     others = nb * nc - 1
+    rounds = max(2 * STEPS + 1, (nb - 1).bit_length())
     side = nb * nc // 2
     b = lax.axis_index("blocks")
     c = lax.axis_index("cross")
@@ -103,12 +104,59 @@
         return (d // nc, lax.rem(d, nc))
 
     barrier = pltpu.get_barrier_semaphore()
-
-    def greet(k, carry):
-        pl.semaphore_signal(barrier, inc=1, device_id=device(peer(k)), device_id_type=MESH)
-        return carry
-
-    lax.fori_loop(0, others, greet, 0)
+    above = b < nb - 1
+    below = b > 0
+
+    def signal(sem, to):
+        pl.semaphore_signal(sem, inc=1, device_id=to, device_id_type=MESH)
+
+    for k in range(1, nc):
+        signal(barrier, at(0, k))
+    for there, dx in ((above, 1), (below, -1)):
+        @pl.when(there)
+        def _():
+            for k in range(nc):
+                signal(barrier, at(dx, k))
+
+    def tell(k):
+        hop = lax.shift_left(jnp.int32(1), jnp.int32(k))
+
+        @pl.when(b + hop < nb)
+        def _():
+            signal(up_sem.at[k], (b + hop, c))
+
+        @pl.when(b >= hop)
+        def _():
+            signal(down_sem.at[k], (b - hop, c))
+
+    def hear(k):
+        hop = lax.shift_left(jnp.int32(1), jnp.int32(k))
+
+        @pl.when(b >= hop)
+        def _():
+            pl.semaphore_wait(up_sem.at[k], 1)
+
+        @pl.when(b + hop < nb)
+        def _():
+            pl.semaphore_wait(down_sem.at[k], 1)
+
+    patches = f_ref.shape[1]
+    count = nb * nc
+    target = lax.broadcasted_iota(jnp.int32, (count, patches), 0)
+    where = jnp.broadcast_to(plan_ref[...], (count, patches))
+    member = where // patches == target
+    key = lax.broadcasted_iota(jnp.int32, (count, patches), 1) * patches + where % patches
+    low_key = jnp.min(jnp.where(member, key, patches * patches), axis=1, keepdims=True)
+    high_key = jnp.max(jnp.where(member, key, -1), axis=1, keepdims=True)
+    some = high_key >= 0
+    two = high_key > low_key
+    column = lax.broadcasted_iota(jnp.int32, (count, LANES), 1)
+    pick[...] = jnp.where(column == 0, jnp.where(some, low_key // patches, 0),
+                          jnp.where(two, high_key // patches, 0))
+    to_scalars = pltpu.make_async_copy(pick, pick_s, pick_sem)
+    to_scalars.start()
+    tags[0] = jnp.broadcast_to(jnp.where(some, low_key % patches, -1), (count, LANES)).astype(jnp.float32)
+    tags[1] = jnp.broadcast_to(jnp.where(two, high_key % patches, -1), (count, LANES)).astype(jnp.float32)
 
     spot = lax.broadcasted_iota(jnp.int32, (SPAN_PATCHES, 8, LANES), 0) * 8
     spot = spot + lax.broadcasted_iota(jnp.int32, (SPAN_PATCHES, 8, LANES), 1)
@@ -120,17 +168,33 @@
     for q in range(19):
         for r in range(SPAN_PATCHES):
             st[q, r] = f_ref[q, r * 8 : r * 8 + 8, :]
-    pl.semaphore_wait(barrier, others)
+    pl.semaphore_wait(barrier, nc - 1 + nc * (jnp.where(above, 1, 0) + jnp.where(below, 1, 0)))
+    tell(0)
+
+    def start_to(there, copy):
+        if there is None:
+            copy.start()
+        else:
+            pl.when(there)(copy.start)
+
+    def wait_for(outgoing, incoming, copy):
+        if outgoing is None:
+            copy.wait()
+        else:
+            pl.when(outgoing)(copy.wait_send)
+            pl.when(incoming)(copy.wait_recv)
+
+    def ends_of(dx):
+        return {0: (None, None), 1: (above, below), -1: (below, above)}[dx]
 
     level_copies = []
     for n, (dx, dy) in enumerate(AROUND):
         copy = pltpu.make_async_remote_copy(
             src_ref=lev_ref, dst_ref=lv.at[n], send_sem=lsend.at[n], recv_sem=lrecv.at[n],
             device_id=at(-dx, -dy), device_id_type=MESH)
-        copy.start()
-        level_copies.append(copy)
-
-    count = others + 1
+        outgoing, incoming = ends_of(-dx)
+        start_to(outgoing, copy)
+        level_copies.append((outgoing, incoming, copy))
 
     def patch_copy(k):
         d = peer(k)
@@ -145,7 +209,7 @@
             recv_sem=erecv.at[k], device_id=device(d), device_id_type=MESH)
 
     for copy in level_copies:
-        copy.wait()
+        wait_for(*copy)
 
     scale = {(0, 0): jnp.where(own > 0.5, RESCALE, 1.0)}
     for n, key in enumerate(AROUND):
@@ -244,12 +308,13 @@
                     ds[s, DIAGONAL.index(q)] = turned[SPAN_PATCHES - 1 if VELOCITIES[q][1] == 1 else 0]
         x_copies = []
 
-        def send(src, dst, n, to):
+        def send(src, dst, n, dx, dy):
             copy = pltpu.make_async_remote_copy(
                 src_ref=src, dst_ref=dst, send_sem=send_sem.at[s, n], recv_sem=recv_sem.at[s, n],
-                device_id=to, device_id_type=MESH)
-            copy.start()
-            return copy
+                device_id=at(dx, dy), device_id_type=MESH)
+            outgoing, incoming = ends_of(dx)
+            start_to(outgoing, copy)
+            return outgoing, incoming, copy
 
         def outer(m, carry):
             first(m * (SPAN_PATCHES - 1), range(1, TILES - 1))
@@ -260,9 +325,9 @@
             return carry
 
         for way, dx in ((0, 1), (1, -1)):
-            x_copies.append(send(xs.at[s, way], xr.at[s, way], 2 + way, at(dx, 0)))
+            x_copies.append(send(xs.at[s, way], xr.at[s, way], 2 + way, dx, 0))
         for n, q in enumerate(DIAGONAL):
-            x_copies.append(send(ds.at[s, n], dr.at[s, n], 4 + n, at(*VELOCITIES[q][:2])))
+            x_copies.append(send(ds.at[s, n], dr.at[s, n], 4 + n, *VELOCITIES[q][:2]))
         lax.fori_loop(0, 2, outer, 0)
         for way, e, group in ((0, 1, Y_UP), (1, -1, Y_DOWN)):
             r = SPAN_PATCHES - 1 if e == 1 else 0
@@ -271,7 +336,7 @@
                     ys[s, way, n, :, lanes_of(tile)] = along_z(q, pb[q, r : r + 1, :, lanes_of(tile)])[0]
         y_copies = []
         for way, dy in ((0, 1), (1, -1)):
-            y_copies.append(send(ys.at[s, way], yr.at[s, way], way, at(0, dy)))
+            y_copies.append(send(ys.at[s, way], yr.at[s, way], way, 0, dy))
         lax.fori_loop(1, SPAN_PATCHES - 1, inner, 0)
 
         def shift(q):
@@ -295,7 +360,9 @@
             if not VELOCITIES[q][1]:
                 shift(q)
         for copy in y_copies:
-            copy.wait()
+            wait_for(*copy)
+        hear(2 * s)
+        tell(2 * s + 1)
         for q in range(19):
             if VELOCITIES[q][1]:
                 shift(q)
@@ -315,7 +382,9 @@
 
         lax.fori_loop(0, SPAN_PATCHES, middle, 0)
         for copy in x_copies:
-            copy.wait()
+            wait_for(*copy)
+        hear(2 * s + 1)
+        tell(2 * s + 2)
         for way, e, group in ((0, 1, X_UP), (1, -1, X_DOWN)):
             outside = b == (0 if e == 1 else nb - 1)
             for n, q in enumerate(group):
@@ -349,6 +418,11 @@
         return carry
 
     lax.fori_loop(0, STEPS, step, 0)
+    for k in range(2 * STEPS, rounds - 1):
+        hear(k)
+        tell(k + 1)
+    hear(rounds - 1)
+    to_scalars.wait()
 
     pm[:, 2 * MAIN : HALF, :] = jnp.zeros((pm.shape[0], HALF - 2 * MAIN, LANES), jnp.float32)
     pm[:, HALF + 2 * MAIN :, :] = jnp.zeros((pm.shape[0], HALF - 2 * MAIN, LANES), jnp.float32)
@@ -358,14 +432,11 @@
                 row = tile // 2 * HALF + low_row(q, tile)
                 pm[r * 8 : r * 8 + 8, row, :] = st[q, r, :, tile * LANES : (tile + 1) * LANES]
 
-    def tag(value):
-        return jnp.full((1, LANES), value.astype(jnp.float32), jnp.float32)
-
     def pack(d):
-        p = sidx[2 * d]
+        p = pick_s[d, 0]
         sent[d, 0] = pm[p, :HALF]
         sent[d, 1] = pm[p, HALF:]
-        sent[d, 0, MARK : MARK + 1, :] = tag(slot_of[2 * d])
+        sent[d, 0, MARK : MARK + 1, :] = tags[0, pl.ds(d, 1), :]
 
     def post(k, carry):
         pack(peer(k))
@@ -383,8 +454,8 @@
         return pl.ds(pl.multiple_of(which * HALF, HALF), HALF)
 
     def pack_second(d, carry):
-        second[d] = pm[sidx[2 * d + 1], half_rows(1 - c), :]
-        second[d, MARK : MARK + 1, :] = tag(slot_of[2 * d + 1])
+        second[d] = pm[pick_s[d, 1], half_rows(1 - c), :]
+        second[d, MARK : MARK + 1, :] = tags[1, pl.ds(d, 1), :]
         return carry
 
     lax.fori_loop(0, count, pack_second, 0)
@@ -401,9 +472,9 @@
     zero = c == 0
 
     def pack_extra(d):
-        mine = pm[sidx[2 * d + 1], half_rows(c), :]
+        mine = pm[pick_s[d, 1], half_rows(c), :]
         other = theirs[d]
-        my_tag = tag(slot_of[2 * d + 1])
+        my_tag = tags[1, pl.ds(d, 1), :]
         other_tag = other[MARK : MARK + 1]
         has_mine = my_tag > -0.5
         has_other = other_tag > -0.5
@@ -503,13 +574,6 @@
 def body(nb, nc, f_home, levels, plan):
     devices = nb * nc
     patches = f_home.shape[0]
-    target = plan // patches
-    order = jnp.arange(patches, dtype=jnp.int32)
-    earlier = (target[:, None] == target[None, :]) & (order[None, :] < order[:, None])
-    place = 2 * target + jnp.sum(earlier.astype(jnp.int32), axis=1)
-    hit = place[None, :] == jnp.arange(2 * devices, dtype=jnp.int32)[:, None]
-    sidx = jnp.sum(jnp.where(hit, order[None, :], 0), axis=1)
-    slot_of = jnp.sum(jnp.where(hit, plan[None, :] % patches + 1, 0), axis=1) - 1
     vmem = pl.BlockSpec(memory_space=pltpu.VMEM)
     smem = pl.BlockSpec(memory_space=pltpu.SMEM)
     state = (19, SPAN_PATCHES, 8, CELLS)
@@ -517,6 +581,7 @@
     f32 = jnp.float32
     dma = pltpu.SemaphoreType.DMA
     half = (HALF, LANES)
+    rounds = max(2 * STEPS + 1, (nb - 1).bit_length())
     limit = pltpu.CompilerParams(collective_id=0, has_side_effects=True, vmem_limit_bytes=60 * 1024 * 1024)
     got, left, table = pl.pallas_call(
         lambda *refs: lattice_kernel(nb, nc, *refs),
@@ -525,7 +590,7 @@
             jax.ShapeDtypeStruct((devices,) + half, f32),
             jax.ShapeDtypeStruct((8, LANES), jnp.int32),
         ),
-        in_specs=[smem, smem, smem, vmem],
+        in_specs=[smem, vmem, vmem],
         out_specs=(vmem, vmem, vmem),
         scratch_shapes=[
             pltpu.VMEM(state, f32),
@@ -544,6 +609,9 @@
             pltpu.VMEM((STEPS, 2, 5, 2, 8, LANES), f32),
             pltpu.VMEM((STEPS, len(DIAGONAL), 8, LANES), f32),
             pltpu.VMEM((STEPS, len(DIAGONAL), 8, LANES), f32),
+            pltpu.VMEM((devices, LANES), jnp.int32),
+            pltpu.SMEM((devices, LANES), jnp.int32),
+            pltpu.VMEM((2, devices, LANES), f32),
             dma((STEPS, 8)),
             dma((STEPS, 8)),
             dma((len(AROUND),)),
@@ -554,9 +622,12 @@
             dma((devices - 1,)),
             dma,
             dma,
+            dma,
+            pltpu.SemaphoreType.REGULAR((rounds,)),
+            pltpu.SemaphoreType.REGULAR((rounds,)),
         ],
         compiler_params=limit,
-    )(sidx, slot_of, levels, jnp.transpose(f_home, (1, 0, 2)))
+    )(levels, plan[None, :], jnp.transpose(f_home, (1, 0, 2)))
 
     def unpack(table, got):
         return pl.pallas_call(

time: 74.8 us -> 71.6 us (0.957)
  other arithmetic: 2.03 us -> 0 us
  Pallas kernels: 69.4 us -> 68.4 us
    pallas_call x1, Pallas kernels: 68 us -> 67.1 us  [body(): pl.pallas_call(lambda *refs: lattice_kernel(nb, nc, *refs), out_shape=(ja...]
    reduce_sum x2 -> x0, other arithmetic: 0.79 us -> none  [the longest x1 0.61 us: body(): jnp.sum(jnp.where(hit, plan[None, :] % patches + 1, 0), axis=1) - 1]
where the time goes in v4:
time: 71.6 us; the launch traced here: 70.7 us
  Pallas kernels  68.4 us (96%)
  local copies, waits for them, and re-layouts  1.54 us (2%)
    pallas_call x1, Pallas kernels, body(): pl.pallas_call(lambda *refs: lattice_kernel(nb, nc, *refs), out_shape=(ja...  67.1 us

profile of v4, /device:TPU:0, one launch (start us, length us, event | category | flops | bytes accessed | tf_op | source)
XLA Modules:
  0.0 70.7 jit_solution(17904317224650343045)
XLA Ops:
  0.0 67.1 %shard_map.37 = (f32[96,40,128]{2,1,0:T(8,128)S(1)}, f32[32,40,128]{2,1,0:T(8,128)}, s32[8,128]{1,0:T(8,128)S(1)}) custom-call(s32[32]{0:T(128)} %refs_0_.1, s32[1,32]{1,0:T(1,128)} %bitcast.5, f32[19,32,512]{2,1,0:T(8,128)} %bitcast.4), custom_call_target="tpu_custom_call" | custom-call | tf_op jit(solution)/shard_map/pallas_call | solution.py:586
  67.1 0.5 slice.3
  68.2 1.4 %conditional.1 = (f32[19,32,512]{2,1,0:T(8,128)S(1)}) conditional(s32[]{:T(128)} %bitcast.2, (s32[8,128]{1,0:T(8,128)S(1)}, f32[96,40,128]{2,1,0:T(8,128)S(1)}) %tuple.11, (f32[32,40,128]{2,1,0:T(8,128)}, s32[8,128]{1,0:T(8,128)S(1)}, f32[96,40,128]{2,1,0:T(8,128)S(1)}) %tuple.12), branch_computations={%region_0.0_spmd, %region_1.0_spmd} | conditional | flops 655360 | bytes 5259300 | solution.py:655
  68.2 1.4 %branch_0_fun.1 = f32[19,32,512]{2,1,0:T(8,128)S(1)} custom-call(s32[8,128]{1,0:T(8,128)S(1)} %get-tuple-element.18.ridx, f32[96,40,128]{2,1,0:T(8,128)S(1)} %get-tuple-element.19.got_ref), custom_call_target="tpu_custom_call" | custom-call | tf_op jit(solution)/shard_map/cond/branch_0_fun/pallas_call | solution.py:633
  69.6 0.0 copy-start.1
  69.6 1.0 %copy-done.1 = f32[19,32,512]{2,1,0:T(8,128)} copy-done((f32[19,32,512]{2,1,0:T(8,128)}, f32[19,32,512]{2,1,0:T(8,128)S(1)}, u32[]{:S(2)}) %copy-start.1) | copy-done | bytes 1245208
Async XLA Ops:
  69.6 1.0 %copy-start.1 = (f32[19,32,512]{2,1,0:T(8,128)}, f32[19,32,512]{2,1,0:T(8,128)S(1)}, u32[]{:S(2)}) copy-start(f32[19,32,512]{2,1,0:T(8,128)S(1)} %get-tuple-element.31) | copy-start | bytes 3735556

commit v5 on v4

--- a/solution.py
+++ b/solution.py
@@ -40,7 +40,11 @@
 TAIL = 3
 HALF = 40
 MARK = 38
-FLAG = 39
+FIRST = 39
+QUARTER = 20
+TAG = 19
+OVER = 1000.0
+GROUP = 4
 LANES = 128
 TILES = CELLS // LANES
 Y_UP = [q for q in range(19) if VELOCITIES[q][1] == 1]
@@ -83,12 +87,11 @@
     return tile % 2 * MAIN + q if q < MAIN else 2 * MAIN + tile % 2 * TAIL + q - MAIN
 
 
-def lattice_kernel(nb, nc, level, plan_ref, f_ref, got_ref, left_ref, table_ref, st, pb, cq, pm, sent, second,
-                   extra, theirs, lev_ref, lv, ys, yr, xs, xr, ds, dr, pick, pick_s, tags, send_sem, recv_sem, lsend, lrecv, psend,
-                   precv, esend, erecv, csend, crecv, pick_sem, up_sem, down_sem):
+def lattice_kernel(nb, nc, level, plan_ref, f_ref, got_ref, pm, table_ref, st, pb, cq, sent, second, theirs,
+                   away, kept, across, extra, got_extra, lev_ref, lv, ys, yr, xs, xr, ds, dr, pick, pick_s, tags, send_sem, recv_sem, lsend, lrecv, psend,
+                   precv, esend, erecv, csend, crecv, qsend, qrecv, pick_sem, up_sem, down_sem):
     others = nb * nc - 1
     rounds = max(2 * STEPS + 1, (nb - 1).bit_length())
-    side = nb * nc // 2
     b = lax.axis_index("blocks")
     c = lax.axis_index("cross")
 
@@ -98,7 +101,7 @@
     me = b * nc + c
 
     def peer(k):
-        return lax.bitwise_xor(me, jnp.where(k < side, side + k, k - side + 1))
+        return lax.bitwise_xor(me, k)
 
     def device(d):
         return (d // nc, lax.rem(d, nc))
@@ -205,7 +208,7 @@
     def extra_copy(k):
         d = peer(k)
         return pltpu.make_async_remote_copy(
-            src_ref=extra.at[d], dst_ref=got_ref.at[2 * count + me], send_sem=esend.at[k],
+            src_ref=extra.at[d], dst_ref=got_extra.at[me], send_sem=esend.at[k],
             recv_sem=erecv.at[k], device_id=device(d), device_id_type=MESH)
 
     for copy in level_copies:
@@ -432,94 +435,176 @@
                 row = tile // 2 * HALF + low_row(q, tile)
                 pm[r * 8 : r * 8 + 8, row, :] = st[q, r, :, tile * LANES : (tile + 1) * LANES]
 
-    def pack(d):
-        p = pick_s[d, 0]
-        sent[d, 0] = pm[p, :HALF]
-        sent[d, 1] = pm[p, HALF:]
-        sent[d, 0, MARK : MARK + 1, :] = tags[0, pl.ds(d, 1), :]
-
-    def post(k, carry):
-        pack(peer(k))
-
-        @pl.when(k > 0)
+    part = lax.rem(me, GROUP)
+    base = me - part
+    far_chip = part // nc
+    chunks = count // GROUP
+
+    def chunk_at(j):
+        return lax.rem(j + chunks // 2, chunks)
+
+    def rows_of(j):
+        return pl.ds(chunk_at(j) * GROUP, GROUP)
+
+    def swap_copy(j):
+        return pltpu.make_async_remote_copy(
+            src_ref=second.at[rows_of(j)], dst_ref=theirs.at[rows_of(j)], send_sem=csend.at[j],
+            recv_sem=crecv.at[j], device_id=at(0, 1), device_id_type=MESH)
+
+    def shuffle_copy(j):
+        return pltpu.make_async_remote_copy(
+            src_ref=away.at[rows_of(j)], dst_ref=across.at[rows_of(j)], send_sem=qsend.at[j],
+            recv_sem=qrecv.at[j], device_id=device(lax.bitwise_xor(me, nc)), device_id_type=MESH)
+
+    def tag_of(which, d):
+        return tags[which, pl.ds(d, 1), :]
+
+    def pack_second(j, carry):
+        for i in range(GROUP):
+            m = chunk_at(j) * GROUP + i
+            d = lax.bitwise_xor(base, m)
+            p = pick_s[d, 1]
+            second[m, 0] = pm[p, :HALF]
+            second[m, 1] = pm[p, HALF:]
+            second[m, 0, MARK : MARK + 1, :] = tag_of(1, d)
+            second[m, 0, FIRST : FIRST + 1, :] = tag_of(0, d)
+
+        @pl.when(j > 0)
         def _():
-            patch_copy(k - 1).start()
-
-        return carry
-
-    lax.fori_loop(0, others, post, 0)
-    pack(me)
-
-    def half_rows(which):
-        return pl.ds(pl.multiple_of(which * HALF, HALF), HALF)
-
-    def pack_second(d, carry):
-        second[d] = pm[pick_s[d, 1], half_rows(1 - c), :]
-        second[d, MARK : MARK + 1, :] = tags[1, pl.ds(d, 1), :]
-        return carry
-
-    lax.fori_loop(0, count, pack_second, 0)
-    patch_copy(others - 1).start()
+            swap_copy(j - 1).start()
+
+        return carry
+
+    lax.fori_loop(0, chunks, pack_second, 0)
+    swap_copy(chunks - 1).start()
+    zero = c == 0
+
+    def piece(p, m, t):
+        top = pl.multiple_of(t // 2 * HALF + lax.rem(t, 2) * MAIN, 8)
+        low = pl.multiple_of(t // 2 * HALF + 2 * MAIN, 8)
+        their_top = pl.multiple_of(lax.rem(t, 2) * MAIN, 8)
+        return (pm[p, pl.ds(top, MAIN), :], pm[p, pl.ds(low, 8), :],
+                theirs[m, t // 2, pl.ds(their_top, MAIN), :], theirs[m, t // 2, 2 * MAIN : HALF, :])
+
+    def pack_chunk(j):
+        for i in range(GROUP):
+            k = chunk_at(j) * GROUP + i
+            d = peer(k)
+            m = lax.bitwise_xor(k, part)
+            p = pick_s[d, 0]
+            my_first = tag_of(0, d)
+            my_second = tag_of(1, d)
+            their_second = theirs[m, 0, MARK : MARK + 1, :]
+            their_first = theirs[m, 0, FIRST : FIRST + 1, :]
+            own = my_first > -0.5
+            sent[d, 0] = jnp.where(own, pm[p, :HALF], theirs[m, 0])
+            sent[d, 1] = jnp.where(own, pm[p, HALF:], theirs[m, 1])
+            sent[d, 0, MARK : MARK + 1, :] = jnp.where(own, my_first, their_second)
+            mine_extra = (my_second > -0.5) & (their_first > -0.5)
+            their_extra = (their_second > -0.5) & own
+            use_mine = mine_extra & (zero | ~their_extra)
+            tag = jnp.where(use_mine, my_second, jnp.where(their_extra, their_second, -1.0))
+            tag = jnp.where(mine_extra & their_extra, OVER, tag)
+            p = pick_s[d, 1]
+            for ref, t in ((kept, part), (away, lax.bitwise_xor(part, nc))):
+                my_top, my_low, their_top, their_low = piece(p, m, t)
+                ref[m, :MAIN, :] = jnp.where(use_mine, my_top, their_top)
+                low = jnp.where(use_mine, my_low, their_low)
+                low = jnp.where(lax.rem(t, 2) == 1, pltpu.roll(low, 8 - TAIL, axis=0), low)
+                ref[m, MAIN : MAIN + TAIL, :] = low[:TAIL]
+                ref[m, TAG : TAG + 1, :] = tag
+
+    def send_chunk(j):
+        shuffle_copy(j).start()
+        for i in range(GROUP):
+            k = chunk_at(j) * GROUP + i
+
+            @pl.when(k > 0)
+            def _():
+                patch_copy(k).start()
+
+    def post(j, carry):
+        swap_copy(j).wait_recv()
+        pack_chunk(j)
+
+        @pl.when(j > 0)
+        def _():
+            send_chunk(j - 1)
+
+        return carry
+
+    lax.fori_loop(0, chunks, post, 0)
+    send_chunk(chunks - 1)
     got_ref[2 * me] = sent[me, 0]
     got_ref[2 * me + 1] = sent[me, 1]
-    swap = pltpu.make_async_remote_copy(
-        src_ref=second, dst_ref=theirs, send_sem=csend, recv_sem=crecv,
-        device_id=at(0, 1), device_id_type=MESH)
-    swap.start()
-    swap.wait()
-    both = jnp.where((second[:, MARK, :] > -0.5) & (theirs[:, MARK, :] > -0.5), 1.0, 0.0)
-    flag = jnp.max(both, axis=0, keepdims=True)
-    zero = c == 0
+
+    def swapped(j, carry):
+        swap_copy(j).wait_send()
+        shuffle_copy(j).wait()
+        return carry
+
+    lax.fori_loop(0, chunks, swapped, 0)
+    near_tags = kept[:, TAG, :]
+    far_tags = across[:, TAG, :]
+    over = (near_tags > OVER / 2) | (far_tags > OVER / 2) | ((near_tags > -0.5) & (far_tags > -0.5))
+    flag = jnp.max(jnp.where(over, OVER, 0.0), axis=0, keepdims=True)
 
     def pack_extra(d):
-        mine = pm[pick_s[d, 1], half_rows(c), :]
-        other = theirs[d]
-        my_tag = tags[1, pl.ds(d, 1), :]
-        other_tag = other[MARK : MARK + 1]
-        has_mine = my_tag > -0.5
-        has_other = other_tag > -0.5
-        keep = (has_mine & zero) | ~has_other
+        m = lax.bitwise_xor(base, d)
+        mine = kept[m]
+        other = across[m]
+        keep = ((mine[TAG:] > -0.5) & (far_chip == 0)) | ~(other[TAG:] > -0.5)
         extra[d] = jnp.where(keep, mine, other)
-        extra[d, MARK : MARK + 1, :] = jnp.where(keep, my_tag, other_tag)
-        extra[d, FLAG : FLAG + 1, :] = flag
-        left_ref[d] = jnp.where(zero, other, mine)
-        left_ref[d, MARK : MARK + 1, :] = jnp.where(
-            has_mine & has_other, jnp.where(zero, other_tag, my_tag), -1.0
-        )
-
-    def post_extra(k, carry):
-        pack_extra(peer(k))
-
-        @pl.when(k > 0)
+        extra[d, TAG : TAG + 1, :] = jnp.where(keep, mine[TAG:], other[TAG:]) + flag
+
+    def mask_at(i):
+        return lax.rem(i + count // 2, count)
+
+    def post_extra(i, carry):
+        pack_extra(peer(mask_at(i)))
+
+        @pl.when((i > 0) & (mask_at(i - 1) > 0))
         def _():
-            extra_copy(k - 1).start()
-
-        return carry
-
-    lax.fori_loop(0, others, post_extra, 0)
-    pack_extra(me)
-    extra_copy(others - 1).start()
-    got_ref[2 * count + me] = extra[me]
+            extra_copy(mask_at(i - 1)).start()
+
+        return carry
+
+    lax.fori_loop(0, count, post_extra, 0)
+    extra_copy(mask_at(count - 1)).start()
+    got_extra[me] = extra[me]
 
     def finish(k, carry):
         patch_copy(k).wait()
         extra_copy(k).wait()
         return carry
 
-    lax.fori_loop(0, others, finish, 0)
+    lax.fori_loop(1, count, finish, 0)
+
+    def assemble(g, carry):
+        for t in range(TILES):
+            whole = got_ref.at[2 * count + 2 * g + t // 2]
+            block = got_extra.at[g * GROUP + t]
+            whole[t % 2 * MAIN : (t % 2 + 1) * MAIN, :] = block[:MAIN, :]
+            low = 2 * MAIN + t % 2 * TAIL
+            whole[low : low + TAIL, :] = block[MAIN : MAIN + TAIL, :]
+        return carry
+
+    lax.fori_loop(0, chunks, assemble, 0)
     source = lax.broadcasted_iota(jnp.int32, (2 * count, LANES), 0)
     wanted = lax.broadcasted_iota(jnp.int32, (2 * count, LANES), 1).astype(jnp.float32)
     first_hit = (got_ref[: 2 * count, MARK, :] == wanted) & (source % 2 == 0)
     index = jnp.sum(jnp.where(first_hit, source, 0), axis=0, keepdims=True)
     source = source[:count]
-    extra_hit = (got_ref[2 * count :, MARK, :] == wanted[:count]) & (source % nc == 0)
-    index = index + jnp.sum(jnp.where(extra_hit, source + 2 * count, 0), axis=0, keepdims=True)
-    over = jnp.max(got_ref[2 * count :, FLAG, :], axis=0, keepdims=True)
+    extra_tags = got_extra[:, TAG, :]
+    extra_hit = (extra_tags == wanted[:count]) & (source % GROUP == 0)
+    place = source // GROUP * 2 + 2 * count
+    index = index + jnp.sum(jnp.where(extra_hit, place, 0), axis=0, keepdims=True)
+    over = jnp.max(extra_tags, axis=0, keepdims=True)
     row = lax.broadcasted_iota(jnp.int32, (8, LANES), 0)
-    table_ref[...] = jnp.where(row == 0, index, jnp.where(over > 0.5, 1, 0))
-
-
-def leftover_kernel(nb, nc, left_ref, table_ref, got_ref, new_table_ref, send_sem, recv_sem):
+    table_ref[...] = jnp.where(row == 0, index, jnp.where(over > OVER / 2, 1, 0))
+
+
+def full_kernel(nb, nc, sidx, slot_of, pm, got_ref, table_ref, sent, send_sem, recv_sem):
     count = nb * nc
     me = lax.axis_index("blocks") * nc + lax.axis_index("cross")
 
@@ -535,28 +620,40 @@
     lax.fori_loop(1, count, greet, 0)
     pl.semaphore_wait(barrier, count - 1)
 
-    def left_copy(k):
+    def pack(d, carry):
+        for slot in range(2):
+            p = sidx[2 * d + slot]
+            sent[d, 2 * slot] = pm[p, :HALF]
+            sent[d, 2 * slot + 1] = pm[p, HALF:]
+            tag = jnp.full((1, LANES), slot_of[2 * d + slot].astype(jnp.float32), jnp.float32)
+            sent[d, 2 * slot, MARK : MARK + 1, :] = tag
+        return carry
+
+    lax.fori_loop(0, count, pack, 0)
+
+    def copy(k):
         d = lax.bitwise_xor(me, k)
         return pltpu.make_async_remote_copy(
-            src_ref=left_ref.at[d], dst_ref=got_ref.at[me], send_sem=send_sem.at[k],
+            src_ref=sent.at[d], dst_ref=got_ref.at[pl.ds(4 * me, 4)], send_sem=send_sem.at[k],
             recv_sem=recv_sem.at[k], device_id=device(d), device_id_type=MESH)
 
     def post(k, carry):
-        left_copy(k).start()
+        copy(k).start()
         return carry
 
     def finish(k, carry):
-        left_copy(k).wait()
+        copy(k).wait()
         return carry
 
     lax.fori_loop(1, count, post, 0)
-    got_ref[me] = left_ref[me]
+    for i in range(4):
+        got_ref[4 * me + i] = sent[me, i]
     lax.fori_loop(1, count, finish, 0)
-    source = lax.broadcasted_iota(jnp.int32, (count, LANES), 0)
-    wanted = lax.broadcasted_iota(jnp.int32, (count, LANES), 1).astype(jnp.float32)
-    hit = (got_ref[:, MARK, :] == wanted) & (source % nc == 0)
-    index = jnp.sum(jnp.where(hit, source + 3 * count, 0), axis=0, keepdims=True)
-    new_table_ref[...] = table_ref[...] + index
+    source = lax.broadcasted_iota(jnp.int32, (4 * count, LANES), 0)
+    wanted = lax.broadcasted_iota(jnp.int32, (4 * count, LANES), 1).astype(jnp.float32)
+    hit = (got_ref[:, MARK, :] == wanted) & (source % 2 == 0)
+    index = jnp.sum(jnp.where(hit, source, 0), axis=0, keepdims=True)
+    table_ref[...] = jnp.broadcast_to(index, table_ref.shape)
 
 
 def unpack_kernel(ridx, got_ref, out_ref):
@@ -581,13 +678,14 @@
     f32 = jnp.float32
     dma = pltpu.SemaphoreType.DMA
     half = (HALF, LANES)
+    quarter = (QUARTER, LANES)
     rounds = max(2 * STEPS + 1, (nb - 1).bit_length())
     limit = pltpu.CompilerParams(collective_id=0, has_side_effects=True, vmem_limit_bytes=60 * 1024 * 1024)
-    got, left, table = pl.pallas_call(
+    got, packed, table = pl.pallas_call(
         lambda *refs: lattice_kernel(nb, nc, *refs),
         out_shape=(
-            jax.ShapeDtypeStruct((3 * devices,) + half, f32),
-            jax.ShapeDtypeStruct((devices,) + half, f32),
+            jax.ShapeDtypeStruct((2 * devices + 2 * devices // GROUP,) + half, f32),
+            jax.ShapeDtypeStruct((patches, 2 * HALF, LANES), f32),
             jax.ShapeDtypeStruct((8, LANES), jnp.int32),
         ),
         in_specs=[smem, vmem, vmem],
@@ -596,11 +694,14 @@
             pltpu.VMEM(state, f32),
             pltpu.VMEM(state, f32),
             pltpu.VMEM((18,) + state[1:], f32),
-            pltpu.VMEM((patches, 2 * HALF, LANES), f32),
             pltpu.VMEM((devices, 2) + half, f32),
-            pltpu.VMEM((devices,) + half, f32),
-            pltpu.VMEM((devices,) + half, f32),
-            pltpu.VMEM((devices,) + half, f32),
+            pltpu.VMEM((devices, 2) + half, f32),
+            pltpu.VMEM((devices, 2) + half, f32),
+            pltpu.VMEM((devices,) + quarter, f32),
+            pltpu.VMEM((devices,) + quarter, f32),
+            pltpu.VMEM((devices,) + quarter, f32),
+            pltpu.VMEM((devices,) + quarter, f32),
+            pltpu.VMEM((devices,) + quarter, f32),
             pltpu.VMEM(small, f32),
             pltpu.VMEM((len(AROUND),) + small, f32),
             pltpu.VMEM((STEPS, 2, 5, 8, CELLS), f32),
@@ -616,12 +717,14 @@
             dma((STEPS, 8)),
             dma((len(AROUND),)),
             dma((len(AROUND),)),
-            dma((devices - 1,)),
-            dma((devices - 1,)),
-            dma((devices - 1,)),
-            dma((devices - 1,)),
-            dma,
-            dma,
+            dma((devices,)),
+            dma((devices,)),
+            dma((devices,)),
+            dma((devices,)),
+            dma((devices // GROUP,)),
+            dma((devices // GROUP,)),
+            dma((devices // GROUP,)),
+            dma((devices // GROUP,)),
             dma,
             pltpu.SemaphoreType.REGULAR((rounds,)),
             pltpu.SemaphoreType.REGULAR((rounds,)),
@@ -638,21 +741,32 @@
             compiler_params=pltpu.CompilerParams(vmem_limit_bytes=40 * 1024 * 1024),
         )(table, got)
 
-    def with_leftover(table, got, left):
-        more, table = pl.pallas_call(
-            lambda *refs: leftover_kernel(nb, nc, *refs),
+    def in_full(table, got, packed, plan):
+        target = plan // patches
+        order = jnp.arange(patches, dtype=jnp.int32)
+        earlier = (target[:, None] == target[None, :]) & (order[None, :] < order[:, None])
+        place = 2 * target + jnp.sum(earlier.astype(jnp.int32), axis=1)
+        hit = place[None, :] == jnp.arange(2 * devices, dtype=jnp.int32)[:, None]
+        sidx = jnp.sum(jnp.where(hit, order[None, :], 0), axis=1)
+        slot_of = jnp.sum(jnp.where(hit, plan[None, :] % patches + 1, 0), axis=1) - 1
+        got, table = pl.pallas_call(
+            lambda *refs: full_kernel(nb, nc, *refs),
             out_shape=(
-                jax.ShapeDtypeStruct((devices,) + half, f32),
+                jax.ShapeDtypeStruct((4 * devices,) + half, f32),
                 jax.ShapeDtypeStruct((8, LANES), jnp.int32),
             ),
-            in_specs=[vmem, vmem],
+            in_specs=[smem, smem, vmem],
             out_specs=(vmem, vmem),
-            scratch_shapes=[dma((devices,)), dma((devices,))],
-            compiler_params=pltpu.CompilerParams(collective_id=1, has_side_effects=True),
-        )(left, table)
-        return unpack(table, jnp.concatenate([got, more], axis=0))
-
-    out = lax.cond(table[1, 0] > 0, with_leftover, lambda table, got, left: unpack(table, got), table, got, left)
+            scratch_shapes=[
+                pltpu.VMEM((devices, 4) + half, f32), dma((devices,)), dma((devices,))
+            ],
+            compiler_params=pltpu.CompilerParams(collective_id=1, has_side_effects=True,
+                                                 vmem_limit_bytes=48 * 1024 * 1024),
+        )(sidx, slot_of, packed)
+        return unpack(table, got)
+
+    out = lax.cond(table[1, 0] > 0, in_full, lambda table, got, packed, plan: unpack(table, got),
+                   table, got, packed, plan)
     return jnp.transpose(out, (1, 0, 2))
 
 

time: 71.6 us -> 66.5 us (0.929); the launches traced: 70.7 us -> 66.3 us
  Pallas kernels: 68.4 us -> 64.1 us
    pallas_call x1, Pallas kernels: 67.1 us -> 62.7 us  [body(): pl.pallas_call(lambda *refs: lattice_kernel(nb, nc, *refs), out_shape=(ja...]
where the time goes in v5:
time: 66.5 us; the launch traced here: 66.3 us
  Pallas kernels  64.1 us (96%)
  local copies, waits for them, and re-layouts  1.55 us (2%)
  between operations  0.69 us (1%)
    pallas_call x1, Pallas kernels, body(): pl.pallas_call(lambda *refs: lattice_kernel(nb, nc, *refs), out_shape=(ja...  62.7 us
    pallas_call x1, Pallas kernels, unpack(): pl.pallas_call(unpack_kernel, out_shape=jax.ShapeDtypeStruct((19, patches...  1.37 us

profile of v5, /device:TPU:0, one launch (start us, length us, event | category | flops | bytes accessed | tf_op | source)
XLA Modules:
  0.0 66.3 jit_solution(9284811193840229578)
XLA Ops:
  0.0 0.0 copy-start.1
  0.0 62.7 %shard_map.37 = (f32[80,40,128]{2,1,0:T(8,128)S(1)}, f32[32,80,128]{2,1,0:T(8,128)S(1)}, s32[8,128]{1,0:T(8,128)S(1)}) custom-call(s32[32]{0:T(128)} %refs_0_.1, s32[1,32]{1,0:T(1,128)} %bitcast.5, f32[19,32,512]{2,1,0:T(8,128)} %bitcast.4), custom_call_target="tpu_custom_call" | custom-call | tf_op jit(solution)/shard_map/pallas_call | solution.py:684
  62.7 0.5 slice.3
  63.9 0.0 copy-done.1
  63.9 1.4 %conditional.1 = (f32[19,32,512]{2,1,0:T(8,128)S(1)}) conditional(s32[]{:T(128)} %bitcast.2, (s32[8,128]{1,0:T(8,128)S(1)}, f32[80,40,128]{2,1,0:T(8,128)S(1)}) %tuple.11, (s32[32]{0:T(128)S(1)}, f32[32,80,128]{2,1,0:T(8,128)S(1)}) %tuple.17), branch_computations={%region_0.0_spmd, %region_1.5_spmd} | conditional | flops 15968 | bytes 2312 | solution.py:768
  63.9 1.4 %branch_0_fun.1 = f32[19,32,512]{2,1,0:T(8,128)S(1)} custom-call(s32[8,128]{1,0:T(8,128)S(1)} %get-tuple-element.16.ridx, f32[80,40,128]{2,1,0:T(8,128)S(1)} %get-tuple-element.17.got_ref), custom_call_target="tpu_custom_call" | custom-call | tf_op jit(solution)/shard_map/cond/branch_0_fun/pallas_call | solution.py:736
  65.3 0.0 copy-start
  65.3 1.0 %copy-done = f32[19,32,512]{2,1,0:T(8,128)} copy-done((f32[19,32,512]{2,1,0:T(8,128)}, f32[19,32,512]{2,1,0:T(8,128)S(1)}, u32[]{:S(2)}) %copy-start) | copy-done | bytes 1245208
Async XLA Ops:
  0.0 63.9 %copy-start.1 = (s32[32]{0:T(128)S(1)}, s32[32]{0:T(128)}, u32[]{:S(2)}) copy-start(s32[32]{0:T(128)} %param.7) | copy-start | bytes 388
  65.3 1.0 %copy-start = (f32[19,32,512]{2,1,0:T(8,128)}, f32[19,32,512]{2,1,0:T(8,128)S(1)}, u32[]{:S(2)}) copy-start(f32[19,32,512]{2,1,0:T(8,128)S(1)} %get-tuple-element.32) | copy-start | bytes 3735556

commit v6 on v5

--- a/solution.py
+++ b/solution.py
@@ -83,15 +83,24 @@
         store(q, balance + coef(q) * (f[q] - balance))
 
 
+def half_of(tile):
+    return 1 if tile in (0, TILES - 1) else 0
+
+
+def place_of(tile):
+    return tile // 2 if half_of(tile) else tile - 1
+
+
 def low_row(q, tile):
-    return tile % 2 * MAIN + q if q < MAIN else 2 * MAIN + tile % 2 * TAIL + q - MAIN
+    place = place_of(tile)
+    return place * MAIN + q if q < MAIN else 2 * MAIN + place * TAIL + q - MAIN
 
 
 def lattice_kernel(nb, nc, level, plan_ref, f_ref, got_ref, pm, table_ref, st, pb, cq, sent, second, theirs,
                    away, kept, across, extra, got_extra, lev_ref, lv, ys, yr, xs, xr, ds, dr, pick, pick_s, tags, send_sem, recv_sem, lsend, lrecv, psend,
                    precv, esend, erecv, csend, crecv, qsend, qrecv, pick_sem, up_sem, down_sem):
     others = nb * nc - 1
-    rounds = max(2 * STEPS + 1, (nb - 1).bit_length())
+    rounds = max(2 * STEPS, (nb - 1).bit_length())
     b = lax.axis_index("blocks")
     c = lax.axis_index("cross")
 
@@ -199,11 +208,11 @@
         start_to(outgoing, copy)
         level_copies.append((outgoing, incoming, copy))
 
-    def patch_copy(k):
+    def patch_copy(half, k):
         d = peer(k)
         return pltpu.make_async_remote_copy(
-            src_ref=sent.at[d], dst_ref=got_ref.at[pl.ds(2 * me, 2)], send_sem=psend.at[k],
-            recv_sem=precv.at[k], device_id=device(d), device_id_type=MESH)
+            src_ref=sent.at[half, d], dst_ref=got_ref.at[2 * me + half], send_sem=psend.at[half, k],
+            recv_sem=precv.at[half, k], device_id=device(d), device_id_type=MESH)
 
     def extra_copy(k):
         d = peer(k)
@@ -250,15 +259,9 @@
                 result = jnp.where(mask, value, result)
             cq[q - 1, :, :, tile * LANES : (tile + 1) * LANES] = gain * result
 
-    full = (SPAN_PATCHES, 8, CELLS)
-    cell = lax.broadcasted_iota(jnp.int32, full, 2)
-    coord = (cell // 64, (cell // 8) % 8, cell % 8)
-    entry = {
-        (axis, e): coord[axis] == (0 if e == 1 else 7) for axis in range(3) for e in (1, -1)
-    }
     lower = lane < 64
     half = lax.broadcasted_iota(jnp.int32, (2, 8, LANES), 2) < 64
-    fine = jnp.broadcast_to(own[:, :, :1] > 0.5, full)
+    fine = own > 0.5
     in_tile = {
         (axis, e): (lane // 8 % 8 if axis == 1 else lane % 8) == (0 if e == 1 else 7)
         for axis in (1, 2) for e in (1, -1)
@@ -282,7 +285,7 @@
     def lanes_of(tile):
         return slice(tile * LANES, (tile + 1) * LANES)
 
-    def step(s, carry):
+    def step(s, stage=None):
         def first(r, tiles):
             plain = jnp.where(lev_ref[r] > 0.5, 1.0 - 1.0 / TAU_FINE, 1.0 - 1.0 / TAU_COARSE)
             for tile in tiles:
@@ -379,15 +382,52 @@
 
                 relax_into(lambda q: st[q, r, :, lanes], put, lambda q: 1.0 - 1.0 / TAU_FINE)
 
+        def settle(tiles):
+            for q in range(19):
+                e = VELOCITIES[q]
+                amount = 64 * e[0] + 8 * e[1] + e[2]
+                inside = fine
+                for axis in (1, 2):
+                    if e[axis]:
+                        inside = inside & ~in_tile[axis, e[axis]]
+                turned = {}
+
+                def moved_from(tile):
+                    if tile not in turned:
+                        v = pb[q, :, :, lanes_of(tile)]
+                        turned[tile] = spin(v, amount) if amount else v
+                    return turned[tile]
+
+                for tile in tiles:
+                    take = inside
+                    value = moved_from(tile)
+                    if e[0] == 1:
+                        value = jnp.where(lower, moved_from((tile - 1) % TILES), value)
+                        take = take & ~lower if tile == 0 else take
+                    elif e[0] == -1:
+                        value = jnp.where(lower, value, moved_from((tile + 1) % TILES))
+                        take = take & lower if tile == TILES - 1 else take
+                    lanes = lanes_of(tile)
+                    st[q, :, :, lanes] = jnp.where(take, value, st[q, :, :, lanes])
+
         def middle(r, carry):
             again(r, range(1, TILES - 1))
             return carry
 
+        def ends(r, carry):
+            again(r, (0, TILES - 1))
+            return carry
+
         lax.fori_loop(0, SPAN_PATCHES, middle, 0)
+        if stage is not None:
+            lax.fori_loop(0, SPAN_PATCHES, ends, 0)
+            settle(range(1, TILES - 1))
+            stage()
         for copy in x_copies:
             wait_for(*copy)
-        hear(2 * s + 1)
-        tell(2 * s + 2)
+        if stage is None:
+            hear(2 * s + 1)
+            tell(2 * s + 2)
         for way, e, group in ((0, 1, X_UP), (1, -1, X_DOWN)):
             outside = b == (0 if e == 1 else nb - 1)
             for n, q in enumerate(group):
@@ -403,37 +443,17 @@
                 keep = st[q, :, :, lanes]
                 st[q, :, :, lanes] = jnp.where(lower, halo, keep) if e == 1 else jnp.where(lower, keep, halo)
 
-        def ends(r, carry):
-            again(r, (0, TILES - 1))
-            return carry
-
         lax.fori_loop(0, SPAN_PATCHES, ends, 0)
+        settle(range(TILES) if stage is None else (0, TILES - 1))
+
+    def fill(half):
+        pm[:, half * HALF + 2 * MAIN : (half + 1) * HALF, :] = jnp.zeros(
+            (pm.shape[0], HALF - 2 * MAIN, LANES), jnp.float32)
         for q in range(19):
-            e = VELOCITIES[q]
-            take = fine
-            for axis in range(3):
-                if e[axis]:
-                    take = take & ~entry[axis, e[axis]]
-            moved = pb[q]
-            if q:
-                moved = pltpu.roll(moved, (64 * e[0] + 8 * e[1] + e[2]) % CELLS, axis=2)
-            st[q] = jnp.where(take, moved, st[q])
-        return carry
-
-    lax.fori_loop(0, STEPS, step, 0)
-    for k in range(2 * STEPS, rounds - 1):
-        hear(k)
-        tell(k + 1)
-    hear(rounds - 1)
-    to_scalars.wait()
-
-    pm[:, 2 * MAIN : HALF, :] = jnp.zeros((pm.shape[0], HALF - 2 * MAIN, LANES), jnp.float32)
-    pm[:, HALF + 2 * MAIN :, :] = jnp.zeros((pm.shape[0], HALF - 2 * MAIN, LANES), jnp.float32)
-    for q in range(19):
-        for r in range(SPAN_PATCHES):
-            for tile in range(TILES):
-                row = tile // 2 * HALF + low_row(q, tile)
-                pm[r * 8 : r * 8 + 8, row, :] = st[q, r, :, tile * LANES : (tile + 1) * LANES]
+            for r in range(SPAN_PATCHES):
+                for tile in range(TILES):
+                    if half_of(tile) == half:
+                        pm[r * 8 : r * 8 + 8, half * HALF + low_row(q, tile), :] = st[q, r, :, lanes_of(tile)]
 
     part = lax.rem(me, GROUP)
     base = me - part
@@ -446,10 +466,11 @@
     def rows_of(j):
         return pl.ds(chunk_at(j) * GROUP, GROUP)
 
-    def swap_copy(j):
+    def swap_copy(half, j):
         return pltpu.make_async_remote_copy(
-            src_ref=second.at[rows_of(j)], dst_ref=theirs.at[rows_of(j)], send_sem=csend.at[j],
-            recv_sem=crecv.at[j], device_id=at(0, 1), device_id_type=MESH)
+            src_ref=second.at[half, rows_of(j)], dst_ref=theirs.at[half, rows_of(j)],
+            send_sem=csend.at[half, j], recv_sem=crecv.at[half, j], device_id=at(0, 1),
+            device_id_type=MESH)
 
     def shuffle_copy(j):
         return pltpu.make_async_remote_copy(
@@ -459,87 +480,110 @@
     def tag_of(which, d):
         return tags[which, pl.ds(d, 1), :]
 
-    def pack_second(j, carry):
-        for i in range(GROUP):
-            m = chunk_at(j) * GROUP + i
-            d = lax.bitwise_xor(base, m)
-            p = pick_s[d, 1]
-            second[m, 0] = pm[p, :HALF]
-            second[m, 1] = pm[p, HALF:]
-            second[m, 0, MARK : MARK + 1, :] = tag_of(1, d)
-            second[m, 0, FIRST : FIRST + 1, :] = tag_of(0, d)
-
-        @pl.when(j > 0)
-        def _():
-            swap_copy(j - 1).start()
-
-        return carry
-
-    lax.fori_loop(0, chunks, pack_second, 0)
-    swap_copy(chunks - 1).start()
+    def offer(half):
+        def pack_second(j, carry):
+            for i in range(GROUP):
+                m = chunk_at(j) * GROUP + i
+                d = lax.bitwise_xor(base, m)
+                second[half, m] = pm[pick_s[d, 1], half * HALF : (half + 1) * HALF]
+                if half == 0:
+                    second[0, m, MARK : MARK + 1, :] = tag_of(1, d)
+                    second[0, m, FIRST : FIRST + 1, :] = tag_of(0, d)
+
+            @pl.when(j > 0)
+            def _():
+                swap_copy(half, j - 1).start()
+
+            return carry
+
+        lax.fori_loop(0, chunks, pack_second, 0)
+        swap_copy(half, chunks - 1).start()
+
     zero = c == 0
 
-    def piece(p, m, t):
-        top = pl.multiple_of(t // 2 * HALF + lax.rem(t, 2) * MAIN, 8)
-        low = pl.multiple_of(t // 2 * HALF + 2 * MAIN, 8)
-        their_top = pl.multiple_of(lax.rem(t, 2) * MAIN, 8)
-        return (pm[p, pl.ds(top, MAIN), :], pm[p, pl.ds(low, 8), :],
-                theirs[m, t // 2, pl.ds(their_top, MAIN), :], theirs[m, t // 2, 2 * MAIN : HALF, :])
-
-    def pack_chunk(j):
+    def pack_quarters(d, m, my_second, their_second, their_first, own):
+        mine_extra = (my_second > -0.5) & (their_first > -0.5)
+        their_extra = (their_second > -0.5) & own
+        use_mine = mine_extra & (zero | ~their_extra)
+        tag = jnp.where(use_mine, my_second, jnp.where(their_extra, their_second, -1.0))
+        tag = jnp.where(mine_extra & their_extra, OVER, tag)
+        p = pick_s[d, 1]
+        for ref, t in ((kept, part), (away, lax.bitwise_xor(part, nc))):
+            half = lax.rem(t, 2)
+            place = t // 2
+            top = pl.multiple_of(place * MAIN, 8)
+            my_top = pl.multiple_of(half * HALF + place * MAIN, 8)
+            my_low = pl.multiple_of(half * HALF + 2 * MAIN, 8)
+            ref[m, :MAIN, :] = jnp.where(
+                use_mine, pm[p, pl.ds(my_top, MAIN), :], theirs[half, m, pl.ds(top, MAIN), :])
+            low = jnp.where(use_mine, pm[p, pl.ds(my_low, 8), :], theirs[half, m, 2 * MAIN : HALF, :])
+            low = jnp.where(place == 1, pltpu.roll(low, 8 - TAIL, axis=0), low)
+            ref[m, MAIN : MAIN + TAIL, :] = low[:TAIL]
+            ref[m, TAG : TAG + 1, :] = tag
+
+    def pack_chunk(half, j):
         for i in range(GROUP):
             k = chunk_at(j) * GROUP + i
             d = peer(k)
             m = lax.bitwise_xor(k, part)
-            p = pick_s[d, 0]
             my_first = tag_of(0, d)
-            my_second = tag_of(1, d)
-            their_second = theirs[m, 0, MARK : MARK + 1, :]
-            their_first = theirs[m, 0, FIRST : FIRST + 1, :]
+            their_second = theirs[0, m, MARK : MARK + 1, :]
             own = my_first > -0.5
-            sent[d, 0] = jnp.where(own, pm[p, :HALF], theirs[m, 0])
-            sent[d, 1] = jnp.where(own, pm[p, HALF:], theirs[m, 1])
-            sent[d, 0, MARK : MARK + 1, :] = jnp.where(own, my_first, their_second)
-            mine_extra = (my_second > -0.5) & (their_first > -0.5)
-            their_extra = (their_second > -0.5) & own
-            use_mine = mine_extra & (zero | ~their_extra)
-            tag = jnp.where(use_mine, my_second, jnp.where(their_extra, their_second, -1.0))
-            tag = jnp.where(mine_extra & their_extra, OVER, tag)
-            p = pick_s[d, 1]
-            for ref, t in ((kept, part), (away, lax.bitwise_xor(part, nc))):
-                my_top, my_low, their_top, their_low = piece(p, m, t)
-                ref[m, :MAIN, :] = jnp.where(use_mine, my_top, their_top)
-                low = jnp.where(use_mine, my_low, their_low)
-                low = jnp.where(lax.rem(t, 2) == 1, pltpu.roll(low, 8 - TAIL, axis=0), low)
-                ref[m, MAIN : MAIN + TAIL, :] = low[:TAIL]
-                ref[m, TAG : TAG + 1, :] = tag
-
-    def send_chunk(j):
-        shuffle_copy(j).start()
+            sent[half, d] = jnp.where(
+                own, pm[pick_s[d, 0], half * HALF : (half + 1) * HALF], theirs[half, m])
+            if half == 0:
+                sent[0, d, MARK : MARK + 1, :] = jnp.where(own, my_first, their_second)
+            else:
+                pack_quarters(d, m, tag_of(1, d), their_second, theirs[0, m, FIRST : FIRST + 1, :], own)
+
+    def send_chunk(half, j):
+        if half:
+            shuffle_copy(j).start()
         for i in range(GROUP):
             k = chunk_at(j) * GROUP + i
 
             @pl.when(k > 0)
             def _():
-                patch_copy(k).start()
-
-    def post(j, carry):
-        swap_copy(j).wait_recv()
-        pack_chunk(j)
-
-        @pl.when(j > 0)
-        def _():
-            send_chunk(j - 1)
-
+                patch_copy(half, k).start()
+
+    def exchange(half):
+        def post(j, carry):
+            swap_copy(half, j).wait_recv()
+            pack_chunk(half, j)
+
+            @pl.when(j > 0)
+            def _():
+                send_chunk(half, j - 1)
+
+            return carry
+
+        lax.fori_loop(0, chunks, post, 0)
+        send_chunk(half, chunks - 1)
+        got_ref[2 * me + half] = sent[half, me]
+
+    def early():
+        fill(0)
+        to_scalars.wait()
+        offer(0)
+        for k in range(2 * STEPS - 1, rounds):
+            if k > 2 * STEPS - 1:
+                tell(k)
+            hear(k)
+        exchange(0)
+
+    def whole_step(s, carry):
+        step(s)
         return carry
 
-    lax.fori_loop(0, chunks, post, 0)
-    send_chunk(chunks - 1)
-    got_ref[2 * me] = sent[me, 0]
-    got_ref[2 * me + 1] = sent[me, 1]
+    lax.fori_loop(0, STEPS - 1, whole_step, 0)
+    step(STEPS - 1, early)
+    fill(1)
+    offer(1)
+    exchange(1)
 
     def swapped(j, carry):
-        swap_copy(j).wait_send()
+        swap_copy(0, j).wait_send()
+        swap_copy(1, j).wait_send()
         shuffle_copy(j).wait()
         return carry
 
@@ -574,7 +618,8 @@
     got_extra[me] = extra[me]
 
     def finish(k, carry):
-        patch_copy(k).wait()
+        patch_copy(0, k).wait()
+        patch_copy(1, k).wait()
         extra_copy(k).wait()
         return carry
 
@@ -582,10 +627,10 @@
 
     def assemble(g, carry):
         for t in range(TILES):
-            whole = got_ref.at[2 * count + 2 * g + t // 2]
+            whole = got_ref.at[2 * count + 2 * g + t % 2]
             block = got_extra.at[g * GROUP + t]
-            whole[t % 2 * MAIN : (t % 2 + 1) * MAIN, :] = block[:MAIN, :]
-            low = 2 * MAIN + t % 2 * TAIL
+            whole[t // 2 * MAIN : (t // 2 + 1) * MAIN, :] = block[:MAIN, :]
+            low = 2 * MAIN + t // 2 * TAIL
             whole[low : low + TAIL, :] = block[MAIN : MAIN + TAIL, :]
         return carry
 
@@ -660,7 +705,7 @@
     for t in range(out_ref.shape[1]):
         base = ridx[0, t]
         for tile in range(TILES):
-            block = got_ref.at[base + tile // 2]
+            block = got_ref.at[base + half_of(tile)]
             lanes = slice(tile * LANES, (tile + 1) * LANES)
             low = low_row(0, tile)
             out_ref[:MAIN, t, lanes] = block[low : low + MAIN, :]
@@ -679,7 +724,7 @@
     dma = pltpu.SemaphoreType.DMA
     half = (HALF, LANES)
     quarter = (QUARTER, LANES)
-    rounds = max(2 * STEPS + 1, (nb - 1).bit_length())
+    rounds = max(2 * STEPS, (nb - 1).bit_length())
     limit = pltpu.CompilerParams(collective_id=0, has_side_effects=True, vmem_limit_bytes=60 * 1024 * 1024)
     got, packed, table = pl.pallas_call(
         lambda *refs: lattice_kernel(nb, nc, *refs),
@@ -694,9 +739,9 @@
             pltpu.VMEM(state, f32),
             pltpu.VMEM(state, f32),
             pltpu.VMEM((18,) + state[1:], f32),
-            pltpu.VMEM((devices, 2) + half, f32),
-            pltpu.VMEM((devices, 2) + half, f32),
-            pltpu.VMEM((devices, 2) + half, f32),
+            pltpu.VMEM((2, devices) + half, f32),
+            pltpu.VMEM((2, devices) + half, f32),
+            pltpu.VMEM((2, devices) + half, f32),
             pltpu.VMEM((devices,) + quarter, f32),
             pltpu.VMEM((devices,) + quarter, f32),
             pltpu.VMEM((devices,) + quarter, f32),
@@ -717,12 +762,12 @@
             dma((STEPS, 8)),
             dma((len(AROUND),)),
             dma((len(AROUND),)),
+            dma((2, devices)),
+            dma((2, devices)),
             dma((devices,)),
             dma((devices,)),
-            dma((devices,)),
-            dma((devices,)),
-            dma((devices // GROUP,)),
-            dma((devices // GROUP,)),
+            dma((2, devices // GROUP)),
+            dma((2, devices // GROUP)),
             dma((devices // GROUP,)),
             dma((devices // GROUP,)),
             dma,

time: 66.5 us -> 64.5 us (0.970)
  Pallas kernels: 64.1 us -> 62.1 us
    pallas_call x1, Pallas kernels: 62.7 us -> 60.6 us  [body(): pl.pallas_call(lambda *refs: lattice_kernel(nb, nc, *refs), out_shape=(ja...]
where the time goes in v6:
time: 64.5 us; the launch traced here: 64.4 us
  Pallas kernels  62.1 us (96%)
  local copies, waits for them, and re-layouts  1.55 us (2%)
  between operations  0.69 us (1%)
    pallas_call x1, Pallas kernels, body(): pl.pallas_call(lambda *refs: lattice_kernel(nb, nc, *refs), out_shape=(ja...  60.6 us
    pallas_call x1, Pallas kernels, unpack(): pl.pallas_call(unpack_kernel, out_shape=jax.ShapeDtypeStruct((19, patches...  1.54 us

profile of v6, /device:TPU:0, one launch (start us, length us, event | category | flops | bytes accessed | tf_op | source)
XLA Modules:
  0.0 64.4 jit_solution(7757507057507411128)
XLA Ops:
  0.0 0.0 copy-start.1
  0.0 60.6 %shard_map.37 = (f32[80,40,128]{2,1,0:T(8,128)S(1)}, f32[32,80,128]{2,1,0:T(8,128)S(1)}, s32[8,128]{1,0:T(8,128)S(1)}) custom-call(s32[32]{0:T(128)} %refs_0_.1, s32[1,32]{1,0:T(1,128)} %bitcast.5, f32[19,32,512]{2,1,0:T(8,128)} %bitcast.4), custom_call_target="tpu_custom_call" | custom-call | tf_op jit(solution)/shard_map/pallas_call | solution.py:729
  60.6 0.5 slice.3
  61.8 0.0 copy-done.1
  61.8 1.6 %conditional.1 = (f32[19,32,512]{2,1,0:T(8,128)S(1)}) conditional(s32[]{:T(128)} %bitcast.2, (s32[8,128]{1,0:T(8,128)S(1)}, f32[80,40,128]{2,1,0:T(8,128)S(1)}) %tuple.11, (s32[32]{0:T(128)S(1)}, f32[32,80,128]{2,1,0:T(8,128)S(1)}) %tuple.17), branch_computations={%region_0.0_spmd, %region_1.5_spmd} | conditional | flops 15968 | bytes 2312 | solution.py:813
  61.8 1.5 %branch_0_fun.1 = f32[19,32,512]{2,1,0:T(8,128)S(1)} custom-call(s32[8,128]{1,0:T(8,128)S(1)} %get-tuple-element.16.ridx, f32[80,40,128]{2,1,0:T(8,128)S(1)} %get-tuple-element.17.got_ref), custom_call_target="tpu_custom_call" | custom-call | tf_op jit(solution)/shard_map/cond/branch_0_fun/pallas_call | solution.py:781
  63.3 0.0 copy-start
  63.3 1.0 %copy-done = f32[19,32,512]{2,1,0:T(8,128)} copy-done((f32[19,32,512]{2,1,0:T(8,128)}, f32[19,32,512]{2,1,0:T(8,128)S(1)}, u32[]{:S(2)}) %copy-start) | copy-done | bytes 1245208
Async XLA Ops:
  0.0 61.8 %copy-start.1 = (s32[32]{0:T(128)S(1)}, s32[32]{0:T(128)}, u32[]{:S(2)}) copy-start(s32[32]{0:T(128)} %param.7) | copy-start | bytes 388
  63.3 1.0 %copy-start = (f32[19,32,512]{2,1,0:T(8,128)}, f32[19,32,512]{2,1,0:T(8,128)S(1)}, u32[]{:S(2)}) copy-start(f32[19,32,512]{2,1,0:T(8,128)S(1)} %get-tuple-element.32) | copy-start | bytes 3735556

commit v7 on v6

--- a/solution.py
+++ b/solution.py
@@ -52,7 +52,6 @@
 X_UP = [q for q in range(19) if VELOCITIES[q][0] == 1]
 X_DOWN = [q for q in range(19) if VELOCITIES[q][0] == -1]
 DIAGONAL = [q for q in range(19) if VELOCITIES[q][0] and VELOCITIES[q][1]]
-AROUND = [(dx, dy) for dx in (-1, 0, 1) for dy in (-1, 0, 1) if (dx, dy) != (0, 0)]
 
 
 def relax_into(load, store, coef):
@@ -97,7 +96,7 @@
 
 
 def lattice_kernel(nb, nc, level, plan_ref, f_ref, got_ref, pm, table_ref, st, pb, cq, sent, second, theirs,
-                   away, kept, across, extra, got_extra, lev_ref, lv, ys, yr, xs, xr, ds, dr, pick, pick_s, tags, send_sem, recv_sem, lsend, lrecv, psend,
+                   away, kept, across, extra, got_extra, own_ref, lev_ref, lv, ys, yr, xs, xr, ds, dr, pick, pick_s, tags, send_sem, recv_sem, lsend, lrecv, psend,
                    precv, esend, erecv, csend, crecv, qsend, qrecv, pick_sem, up_sem, down_sem):
     others = nb * nc - 1
     rounds = max(2 * STEPS, (nb - 1).bit_length())
@@ -170,13 +169,18 @@
     tags[0] = jnp.broadcast_to(jnp.where(some, low_key % patches, -1), (count, LANES)).astype(jnp.float32)
     tags[1] = jnp.broadcast_to(jnp.where(two, high_key % patches, -1), (count, LANES)).astype(jnp.float32)
 
-    spot = lax.broadcasted_iota(jnp.int32, (SPAN_PATCHES, 8, LANES), 0) * 8
-    spot = spot + lax.broadcasted_iota(jnp.int32, (SPAN_PATCHES, 8, LANES), 1)
-    own = jnp.zeros((SPAN_PATCHES, 8, LANES), jnp.float32)
+    slot = lax.broadcasted_iota(jnp.int32, (8, LANES), 0)
+    slot = slot + 8 * lax.broadcasted_iota(jnp.int32, (8, LANES), 1)
+    brief = jnp.zeros((8, LANES), jnp.float32)
     for p in range(SPAN_PATCHES * 8):
-        own = jnp.where(spot == p, level[p].astype(jnp.float32), own)
-    lev_ref[...] = own
-
+        brief = jnp.where(slot == p, level[p].astype(jnp.float32), brief)
+    lev_ref[...] = brief
+
+    def spread(values, r):
+        return jnp.broadcast_to(values[:, r : r + 1], (8, LANES))[None]
+
+    own = jnp.concatenate([spread(brief, r) for r in range(SPAN_PATCHES)], axis=0)
+    own_ref[...] = own
     for q in range(19):
         for r in range(SPAN_PATCHES):
             st[q, r] = f_ref[q, r * 8 : r * 8 + 8, :]
@@ -200,7 +204,8 @@
         return {0: (None, None), 1: (above, below), -1: (below, above)}[dx]
 
     level_copies = []
-    for n, (dx, dy) in enumerate(AROUND):
+    around = [(dx, dy) for dx in (-1, 0, 1) for dy in range(nc) if (dx, dy) != (0, 0)]
+    for n, (dx, dy) in enumerate(around):
         copy = pltpu.make_async_remote_copy(
             src_ref=lev_ref, dst_ref=lv.at[n], send_sem=lsend.at[n], recv_sem=lrecv.at[n],
             device_id=at(-dx, -dy), device_id_type=MESH)
@@ -210,9 +215,11 @@
 
     def patch_copy(half, k):
         d = peer(k)
+        rows = slice(0, MARK if half else FIRST)
         return pltpu.make_async_remote_copy(
-            src_ref=sent.at[half, d], dst_ref=got_ref.at[2 * me + half], send_sem=psend.at[half, k],
-            recv_sem=precv.at[half, k], device_id=device(d), device_id_type=MESH)
+            src_ref=sent.at[half, d, rows], dst_ref=got_ref.at[2 * me + half, rows],
+            send_sem=psend.at[half, k], recv_sem=precv.at[half, k], device_id=device(d),
+            device_id_type=MESH)
 
     def extra_copy(k):
         d = peer(k)
@@ -223,14 +230,14 @@
     for copy in level_copies:
         wait_for(*copy)
 
-    scale = {(0, 0): jnp.where(own > 0.5, RESCALE, 1.0)}
-    for n, key in enumerate(AROUND):
-        scale[key] = jnp.where(lv[n] > 0.5, RESCALE, 1.0)
     patch_scale = {}
     for dx in (-1, 0, 1):
-        patch_scale[dx, 0] = scale[dx, 0]
-        patch_scale[dx, 1] = jnp.concatenate([scale[dx, 0][1:], scale[dx, 1][:1]], axis=0)
-        patch_scale[dx, -1] = jnp.concatenate([scale[dx, -1][-1:], scale[dx, 0][:-1]], axis=0)
+        rows = [spread(lv[around.index((dx, nc - 1))], SPAN_PATCHES - 1)]
+        rows += [own[r][None] if dx == 0 else spread(lv[around.index((dx, 0))], r) for r in range(SPAN_PATCHES)]
+        rows += [spread(lv[around.index((dx, 1 % nc))], 0)]
+        rows = [jnp.where(value > 0.5, RESCALE, 1.0) for value in rows]
+        for dy in (-1, 0, 1):
+            patch_scale[dx, dy] = jnp.concatenate(rows[1 + dy : 1 + dy + SPAN_PATCHES], axis=0)
     gain = jnp.where(own > 0.5, (1.0 - 1.0 / TAU_FINE) / RESCALE, 1.0 - 1.0 / TAU_COARSE)
 
     def target_scale(dx, dy, dz):
@@ -270,24 +277,24 @@
     def spin(v, amount):
         return pltpu.roll(v, amount % LANES, axis=v.ndim - 1)
 
-    def along_z(q, v):
+    def along_z(q, v, more=0):
         e = VELOCITIES[q][2]
         if not e:
-            return v
-        wrapped = pltpu.roll(spin(v, -7 * e), e % 8, axis=1)
-        return jnp.where(in_tile[2, e][: v.shape[0]], wrapped, spin(v, e))
-
-    def along_y(q, v, halo):
+            return spin(v, more) if more else v
+        wrapped = pltpu.roll(spin(v, more - 7 * e), e % 8, axis=1)
+        return jnp.where(in_tile[2, e][: v.shape[0]], wrapped, spin(v, more + e))
+
+    def along_y(q, v, halo, more=0):
         e = VELOCITIES[q][1]
         moved = jnp.concatenate([halo, v[:-1]] if e == 1 else [v[1:], halo], axis=0)
-        return jnp.where(in_tile[1, e], spin(moved, -56 * e), spin(v, 8 * e))
+        return jnp.where(in_tile[1, e], spin(moved, more - 56 * e), spin(v, more + 8 * e))
 
     def lanes_of(tile):
         return slice(tile * LANES, (tile + 1) * LANES)
 
     def step(s, stage=None):
         def first(r, tiles):
-            plain = jnp.where(lev_ref[r] > 0.5, 1.0 - 1.0 / TAU_FINE, 1.0 - 1.0 / TAU_COARSE)
+            plain = jnp.where(own_ref[r] > 0.5, 1.0 - 1.0 / TAU_FINE, 1.0 - 1.0 / TAU_COARSE)
             for tile in tiles:
                 lanes = lanes_of(tile)
 
@@ -347,13 +354,15 @@
 
         def shift(q):
             e = VELOCITIES[q]
-            tiles = [along_z(q, pb[q, :, :, lanes_of(tile)]) for tile in range(TILES)]
+            half_turn = 64 if e[0] else 0
+            tiles = [along_z(q, pb[q, :, :, lanes_of(tile)], 0 if e[1] else half_turn) for tile in range(TILES)]
             if e[1]:
                 way, group = (0, Y_UP) if e[1] == 1 else (1, Y_DOWN)
                 n = group.index(q)
-                tiles = [along_y(q, v, yr[s, way, n, :, lanes_of(tile)][None]) for tile, v in enumerate(tiles)]
+                tiles = [along_y(q, v, yr[s, way, n, :, lanes_of(tile)][None], half_turn)
+                         for tile, v in enumerate(tiles)]
             if e[0]:
-                turned = [spin(v, 64) for v in tiles]
+                turned = list(tiles)
                 for tile in range(TILES):
                     if e[0] == 1:
                         tiles[tile] = jnp.where(lower, turned[tile - 1], turned[tile])
@@ -446,6 +455,8 @@
         lax.fori_loop(0, SPAN_PATCHES, ends, 0)
         settle(range(TILES) if stage is None else (0, TILES - 1))
 
+    flat = pm.reshape(pm.shape[0] * 2 * HALF, LANES)
+
     def fill(half):
         pm[:, half * HALF + 2 * MAIN : (half + 1) * HALF, :] = jnp.zeros(
             (pm.shape[0], HALF - 2 * MAIN, LANES), jnp.float32)
@@ -453,7 +464,8 @@
             for r in range(SPAN_PATCHES):
                 for tile in range(TILES):
                     if half_of(tile) == half:
-                        pm[r * 8 : r * 8 + 8, half * HALF + low_row(q, tile), :] = st[q, r, :, lanes_of(tile)]
+                        row = r * 8 * 2 * HALF + half * HALF + low_row(q, tile)
+                        flat[pl.ds(row, 8, stride=2 * HALF), :] = st[q, r, :, lanes_of(tile)]
 
     part = lax.rem(me, GROUP)
     base = me - part
@@ -748,7 +760,8 @@
             pltpu.VMEM((devices,) + quarter, f32),
             pltpu.VMEM((devices,) + quarter, f32),
             pltpu.VMEM(small, f32),
-            pltpu.VMEM((len(AROUND),) + small, f32),
+            pltpu.VMEM((8, LANES), f32),
+            pltpu.VMEM((3 * nc - 1, 8, LANES), f32),
             pltpu.VMEM((STEPS, 2, 5, 8, CELLS), f32),
             pltpu.VMEM((STEPS, 2, 5, 8, CELLS), f32),
             pltpu.VMEM((STEPS, 2, 5, 2, 8, LANES), f32),
@@ -760,8 +773,8 @@
             pltpu.VMEM((2, devices, LANES), f32),
             dma((STEPS, 8)),
             dma((STEPS, 8)),
-            dma((len(AROUND),)),
-            dma((len(AROUND),)),
+            dma((3 * nc - 1,)),
+            dma((3 * nc - 1,)),
             dma((2, devices)),
             dma((2, devices)),
             dma((devices,)),

time: 64.5 us -> 62.5 us (0.969)
  Pallas kernels: 62.1 us -> 60.1 us
    pallas_call x1, Pallas kernels: 60.6 us -> 58.5 us  [body(): pl.pallas_call(lambda *refs: lattice_kernel(nb, nc, *refs), out_shape=(ja...]
where the time goes in v7:
time: 62.5 us; the launch traced here: 62.3 us
  Pallas kernels  60.1 us (96%)
  local copies, waits for them, and re-layouts  1.55 us (2%)
  between operations  0.69 us (1%)
    pallas_call x1, Pallas kernels, body(): pl.pallas_call(lambda *refs: lattice_kernel(nb, nc, *refs), out_shape=(ja...  58.5 us
    pallas_call x1, Pallas kernels, unpack(): pl.pallas_call(unpack_kernel, out_shape=jax.ShapeDtypeStruct((19, patches...  1.54 us

profile of v7, /device:TPU:0, one launch (start us, length us, event | category | flops | bytes accessed | tf_op | source)
XLA Modules:
  0.0 62.3 jit_solution(2782962252419465499)
XLA Ops:
  0.0 0.0 copy-start.1
  0.0 58.5 %shard_map.37 = (f32[80,40,128]{2,1,0:T(8,128)S(1)}, f32[32,80,128]{2,1,0:T(8,128)S(1)}, s32[8,128]{1,0:T(8,128)S(1)}) custom-call(s32[32]{0:T(128)} %refs_0_.1, s32[1,32]{1,0:T(1,128)} %bitcast.5, f32[19,32,512]{2,1,0:T(8,128)} %bitcast.4), custom_call_target="tpu_custom_call" | custom-call | tf_op jit(solution)/shard_map/pallas_call | solution.py:741
  58.5 0.5 slice.3
  59.7 0.0 copy-done.1
  59.7 1.6 %conditional.1 = (f32[19,32,512]{2,1,0:T(8,128)S(1)}) conditional(s32[]{:T(128)} %bitcast.2, (s32[8,128]{1,0:T(8,128)S(1)}, f32[80,40,128]{2,1,0:T(8,128)S(1)}) %tuple.11, (s32[32]{0:T(128)S(1)}, f32[32,80,128]{2,1,0:T(8,128)S(1)}) %tuple.17), branch_computations={%region_0.0_spmd, %region_1.5_spmd} | conditional | flops 15968 | bytes 2312 | solution.py:826
  59.7 1.5 %branch_0_fun.1 = f32[19,32,512]{2,1,0:T(8,128)S(1)} custom-call(s32[8,128]{1,0:T(8,128)S(1)} %get-tuple-element.16.ridx, f32[80,40,128]{2,1,0:T(8,128)S(1)} %get-tuple-element.17.got_ref), custom_call_target="tpu_custom_call" | custom-call | tf_op jit(solution)/shard_map/cond/branch_0_fun/pallas_call | solution.py:794
  61.3 0.0 copy-start
  61.3 1.0 %copy-done = f32[19,32,512]{2,1,0:T(8,128)} copy-done((f32[19,32,512]{2,1,0:T(8,128)}, f32[19,32,512]{2,1,0:T(8,128)S(1)}, u32[]{:S(2)}) %copy-start) | copy-done | bytes 1245208
Async XLA Ops:
  0.0 59.7 %copy-start.1 = (s32[32]{0:T(128)S(1)}, s32[32]{0:T(128)}, u32[]{:S(2)}) copy-start(s32[32]{0:T(128)} %param.7) | copy-start | bytes 388
  61.3 1.0 %copy-start = (f32[19,32,512]{2,1,0:T(8,128)}, f32[19,32,512]{2,1,0:T(8,128)S(1)}, u32[]{:S(2)}) copy-start(f32[19,32,512]{2,1,0:T(8,128)S(1)} %get-tuple-element.32) | copy-start | bytes 3735556

commit v8 on v7

--- a/solution.py
+++ b/solution.py
@@ -95,7 +95,7 @@
     return place * MAIN + q if q < MAIN else 2 * MAIN + place * TAIL + q - MAIN
 
 
-def lattice_kernel(nb, nc, level, plan_ref, f_ref, got_ref, pm, table_ref, st, pb, cq, sent, second, theirs,
+def lattice_kernel(nb, nc, level, plan_ref, f_ref, got_ref, pm, table_ref, st, pb, pb2, cq, sent, second, theirs,
                    away, kept, across, extra, got_extra, own_ref, lev_ref, lv, ys, yr, xs, xr, ds, dr, pick, pick_s, tags, send_sem, recv_sem, lsend, lrecv, psend,
                    precv, esend, erecv, csend, crecv, qsend, qrecv, pick_sem, up_sem, down_sem):
     others = nb * nc - 1
@@ -184,6 +184,78 @@
     for q in range(19):
         for r in range(SPAN_PATCHES):
             st[q, r] = f_ref[q, r * 8 : r * 8 + 8, :]
+    gain = jnp.where(own > 0.5, (1.0 - 1.0 / TAU_FINE) / RESCALE, 1.0 - 1.0 / TAU_COARSE)
+    lane = lax.broadcasted_iota(jnp.int32, (SPAN_PATCHES, 8, LANES), 2)
+    lower = lane < 64
+    half = lax.broadcasted_iota(jnp.int32, (2, 8, LANES), 2) < 64
+    fine = own > 0.5
+    in_tile = {
+        (axis, e): (lane // 8 % 8 if axis == 1 else lane % 8) == (0 if e == 1 else 7)
+        for axis in (1, 2) for e in (1, -1)
+    }
+    around = [(dx, dy) for dx in (-1, 0, 1) for dy in range(nc) if (dx, dy) != (0, 0)]
+
+    def targets(far):
+        scales = {}
+        for dx in (-1, 0, 1):
+            rows = [spread(far(dx, nc - 1), SPAN_PATCHES - 1)]
+            rows += [own[r][None] if dx == 0 else spread(far(dx, 0), r) for r in range(SPAN_PATCHES)]
+            rows += [spread(far(dx, 1 % nc), 0)]
+            rows = [jnp.where(value > 0.5, RESCALE, 1.0) for value in rows]
+            for dy in (-1, 0, 1):
+                value = jnp.concatenate(rows[1 + dy : 1 + dy + SPAN_PATCHES], axis=0)
+                for dz in (-1, 0, 1):
+                    scales[dx, dy, dz] = pltpu.roll(value, (-dz) % 8, axis=1) if dz else value
+        return scales
+
+    def coefficient(q, tile, scales, rows):
+        e = VELOCITIES[q]
+        kinds = [{}]
+        for axis in range(3):
+            if e[axis] and (axis or tile == (TILES - 1 if e[0] == 1 else 0)):
+                kinds = [{**k, axis: v} for k in kinds for v in (0, 1)]
+        result = None
+        for k in kinds:
+            value = scales[tuple(e[a] * k.get(a, 0) for a in range(3))][rows]
+            mask = None
+            for axis, on in k.items():
+                if on:
+                    hit = in_tile[axis, -e[axis]] if axis else (~lower if e[0] == 1 else lower)
+                    mask = hit[rows] if mask is None else mask & hit[rows]
+            result = value if result is None else jnp.where(mask, value, result)
+        return gain[rows] * result
+
+    def lanes_of(tile):
+        return slice(tile * LANES, (tile + 1) * LANES)
+
+    everything = slice(0, SPAN_PATCHES)
+    scales = targets(lambda dx, dy: jnp.zeros((8, LANES), jnp.float32))
+    for q in range(1, 19):
+        for tile in range(TILES):
+            cq[q - 1, :, :, lanes_of(tile)] = coefficient(q, tile, scales, everything)
+
+    def first(r, tiles):
+        plain = jnp.where(own_ref[r] > 0.5, 1.0 - 1.0 / TAU_FINE, 1.0 - 1.0 / TAU_COARSE)
+        for tile in tiles:
+            lanes = lanes_of(tile)
+
+            def put(q, value):
+                pb[q, r, :, lanes] = value
+
+            relax_into(lambda q: st[q, r, :, lanes], put,
+                       lambda q: cq[q - 1, r, :, lanes] if q else plain)
+
+    def first_rows(tiles, start, stop, stride=1):
+        def one(n, carry):
+            first(start + stride * n, tiles)
+            return carry
+
+        lax.fori_loop(0, (stop - start + stride - 1) // stride, one, 0)
+
+    end_tiles = (0, TILES - 1)
+    middle_tiles = tuple(range(1, TILES - 1))
+    first_rows(end_tiles, 0, SPAN_PATCHES)
+    first_rows(middle_tiles, 0, SPAN_PATCHES)
     pl.semaphore_wait(barrier, nc - 1 + nc * (jnp.where(above, 1, 0) + jnp.where(below, 1, 0)))
     tell(0)
 
@@ -204,7 +276,6 @@
         return {0: (None, None), 1: (above, below), -1: (below, above)}[dx]
 
     level_copies = []
-    around = [(dx, dy) for dx in (-1, 0, 1) for dy in range(nc) if (dx, dy) != (0, 0)]
     for n, (dx, dy) in enumerate(around):
         copy = pltpu.make_async_remote_copy(
             src_ref=lev_ref, dst_ref=lv.at[n], send_sem=lsend.at[n], recv_sem=lrecv.at[n],
@@ -229,50 +300,26 @@
 
     for copy in level_copies:
         wait_for(*copy)
-
-    patch_scale = {}
-    for dx in (-1, 0, 1):
-        rows = [spread(lv[around.index((dx, nc - 1))], SPAN_PATCHES - 1)]
-        rows += [own[r][None] if dx == 0 else spread(lv[around.index((dx, 0))], r) for r in range(SPAN_PATCHES)]
-        rows += [spread(lv[around.index((dx, 1 % nc))], 0)]
-        rows = [jnp.where(value > 0.5, RESCALE, 1.0) for value in rows]
-        for dy in (-1, 0, 1):
-            patch_scale[dx, dy] = jnp.concatenate(rows[1 + dy : 1 + dy + SPAN_PATCHES], axis=0)
-    gain = jnp.where(own > 0.5, (1.0 - 1.0 / TAU_FINE) / RESCALE, 1.0 - 1.0 / TAU_COARSE)
-
-    def target_scale(dx, dy, dz):
-        value = patch_scale[dx, dy]
-        return pltpu.roll(value, (-dz) % 8, axis=1) if dz else value
-
-    shape = (SPAN_PATCHES, 8, LANES)
-    lane = lax.broadcasted_iota(jnp.int32, shape, 2)
+    scales = targets(lambda dx, dy: lv[around.index((dx, dy))])
+
+    def amend(q, tile, rows):
+        spot = (rows, slice(0, 8), lanes_of(tile))
+        before = cq[(q - 1,) + spot]
+        after = coefficient(q, tile, scales, rows)
+        held = pb[(q,) + spot]
+        pb[(q,) + spot] = held + (after - before) / (1.0 - before) * (st[(q,) + spot] - held)
+        cq[(q - 1,) + spot] = after
+
     for q in range(1, 19):
         e = VELOCITIES[q]
-        kinds = [{}]
-        for axis in range(3):
-            if e[axis]:
-                kinds = [{**k, axis: v} for k in kinds for v in (0, 1)]
-        table = [(k, target_scale(*[e[a] * k.get(a, 0) for a in range(3)])) for k in kinds]
-        for tile in range(TILES):
-            cell = lane + tile * LANES
-            coord = (cell // 64, (cell // 8) % 8, cell % 8)
-            result = table[0][1]
-            for k, value in table[1:]:
-                mask = None
-                for axis, on in k.items():
-                    if on:
-                        hit = coord[axis] == (7 if e[axis] == 1 else 0)
-                        mask = hit if mask is None else mask & hit
-                result = jnp.where(mask, value, result)
-            cq[q - 1, :, :, tile * LANES : (tile + 1) * LANES] = gain * result
-
-    lower = lane < 64
-    half = lax.broadcasted_iota(jnp.int32, (2, 8, LANES), 2) < 64
-    fine = own > 0.5
-    in_tile = {
-        (axis, e): (lane // 8 % 8 if axis == 1 else lane % 8) == (0 if e == 1 else 7)
-        for axis in (1, 2) for e in (1, -1)
-    }
+        outer_tile = {0: None, 1: TILES - 1, -1: 0}[e[0]]
+        if e[0]:
+            amend(q, outer_tile, everything)
+        if e[1]:
+            r = SPAN_PATCHES - 1 if e[1] == 1 else 0
+            for tile in range(TILES):
+                if tile != outer_tile:
+                    amend(q, tile, slice(r, r + 1))
 
     def spin(v, amount):
         return pltpu.roll(v, amount % LANES, axis=v.ndim - 1)
@@ -289,37 +336,8 @@
         moved = jnp.concatenate([halo, v[:-1]] if e == 1 else [v[1:], halo], axis=0)
         return jnp.where(in_tile[1, e], spin(moved, more - 56 * e), spin(v, more + 8 * e))
 
-    def lanes_of(tile):
-        return slice(tile * LANES, (tile + 1) * LANES)
-
     def step(s, stage=None):
-        def first(r, tiles):
-            plain = jnp.where(own_ref[r] > 0.5, 1.0 - 1.0 / TAU_FINE, 1.0 - 1.0 / TAU_COARSE)
-            for tile in tiles:
-                lanes = lanes_of(tile)
-
-                def put(q, value):
-                    pb[q, r, :, lanes] = value
-
-                relax_into(lambda q: st[q, r, :, lanes], put,
-                           lambda q: cq[q - 1, r, :, lanes] if q else plain)
-
-        def faces(r, carry):
-            first(r, (0, TILES - 1))
-            return carry
-
-        lax.fori_loop(0, SPAN_PATCHES, faces, 0)
-        for way, e, group in ((0, 1, X_UP), (1, -1, X_DOWN)):
-            for n, q in enumerate(group):
-                v = along_z(q, pb[q, :, :, lanes_of(TILES - 1 if e == 1 else 0)])
-                turned = spin(v, 64)
-                if e == 1:
-                    xs[s, way, n] = jnp.where(half, turned[:2], v[2:])
-                else:
-                    xs[s, way, n] = jnp.where(half, v[:2], turned[2:])
-                if q in DIAGONAL:
-                    ds[s, DIAGONAL.index(q)] = turned[SPAN_PATCHES - 1 if VELOCITIES[q][1] == 1 else 0]
-        x_copies = []
+        copies = {"x": [], "y": []}
 
         def send(src, dst, n, dx, dy):
             copy = pltpu.make_async_remote_copy(
@@ -327,30 +345,45 @@
                 device_id=at(dx, dy), device_id_type=MESH)
             outgoing, incoming = ends_of(dx)
             start_to(outgoing, copy)
-            return outgoing, incoming, copy
-
-        def outer(m, carry):
-            first(m * (SPAN_PATCHES - 1), range(1, TILES - 1))
-            return carry
-
-        def inner(r, carry):
-            first(r, range(1, TILES - 1))
-            return carry
-
-        for way, dx in ((0, 1), (1, -1)):
-            x_copies.append(send(xs.at[s, way], xr.at[s, way], 2 + way, dx, 0))
-        for n, q in enumerate(DIAGONAL):
-            x_copies.append(send(ds.at[s, n], dr.at[s, n], 4 + n, *VELOCITIES[q][:2]))
-        lax.fori_loop(0, 2, outer, 0)
-        for way, e, group in ((0, 1, Y_UP), (1, -1, Y_DOWN)):
-            r = SPAN_PATCHES - 1 if e == 1 else 0
-            for n, q in enumerate(group):
-                for tile in range(TILES):
-                    ys[s, way, n, :, lanes_of(tile)] = along_z(q, pb[q, r : r + 1, :, lanes_of(tile)])[0]
-        y_copies = []
-        for way, dy in ((0, 1), (1, -1)):
-            y_copies.append(send(ys.at[s, way], yr.at[s, way], way, 0, dy))
-        lax.fori_loop(1, SPAN_PATCHES - 1, inner, 0)
+            copies["x" if dx else "y"].append((outgoing, incoming, copy))
+
+        def send_x():
+            for way, e, group in ((0, 1, X_UP), (1, -1, X_DOWN)):
+                for n, q in enumerate(group):
+                    v = along_z(q, pb[q, :, :, lanes_of(TILES - 1 if e == 1 else 0)])
+                    turned = spin(v, 64)
+                    if e == 1:
+                        xs[s, way, n] = jnp.where(half, turned[:2], v[2:])
+                    else:
+                        xs[s, way, n] = jnp.where(half, v[:2], turned[2:])
+                    if q in DIAGONAL:
+                        ds[s, DIAGONAL.index(q)] = turned[SPAN_PATCHES - 1 if VELOCITIES[q][1] == 1 else 0]
+            for way, dx in ((0, 1), (1, -1)):
+                send(xs.at[s, way], xr.at[s, way], 2 + way, dx, 0)
+            for n, q in enumerate(DIAGONAL):
+                send(ds.at[s, n], dr.at[s, n], 4 + n, *VELOCITIES[q][:2])
+
+        def send_y():
+            for way, e, group in ((0, 1, Y_UP), (1, -1, Y_DOWN)):
+                r = SPAN_PATCHES - 1 if e == 1 else 0
+                for n, q in enumerate(group):
+                    for tile in range(TILES):
+                        ys[s, way, n, :, lanes_of(tile)] = along_z(q, pb[q, r : r + 1, :, lanes_of(tile)])[0]
+            for way, dy in ((0, 1), (1, -1)):
+                send(ys.at[s, way], yr.at[s, way], way, 0, dy)
+
+        if s == 0:
+            send_x()
+            send_y()
+        elif stage is None:
+            first_rows(end_tiles, 0, SPAN_PATCHES)
+            send_x()
+            send_y()
+        else:
+            first_rows(end_tiles, 0, SPAN_PATCHES, SPAN_PATCHES - 1)
+            send_y()
+            first_rows(end_tiles, 1, SPAN_PATCHES - 1)
+            send_x()
 
         def shift(q):
             e = VELOCITIES[q]
@@ -374,7 +407,7 @@
         for q in range(19):
             if not VELOCITIES[q][1]:
                 shift(q)
-        for copy in y_copies:
+        for copy in copies["y"]:
             wait_for(*copy)
         hear(2 * s)
         tell(2 * s + 1)
@@ -387,7 +420,7 @@
                 lanes = lanes_of(tile)
 
                 def put(q, value):
-                    pb[q, r, :, lanes] = value
+                    pb2[q, r, :, lanes] = value
 
                 relax_into(lambda q: st[q, r, :, lanes], put, lambda q: 1.0 - 1.0 / TAU_FINE)
 
@@ -403,7 +436,7 @@
 
                 def moved_from(tile):
                     if tile not in turned:
-                        v = pb[q, :, :, lanes_of(tile)]
+                        v = pb2[q, :, :, lanes_of(tile)]
                         turned[tile] = spin(v, amount) if amount else v
                     return turned[tile]
 
@@ -428,11 +461,13 @@
             return carry
 
         lax.fori_loop(0, SPAN_PATCHES, middle, 0)
-        if stage is not None:
-            lax.fori_loop(0, SPAN_PATCHES, ends, 0)
-            settle(range(1, TILES - 1))
+        lax.fori_loop(0, SPAN_PATCHES, ends, 0)
+        settle(middle_tiles)
+        if stage is None:
+            first_rows(middle_tiles, 0, SPAN_PATCHES)
+        else:
             stage()
-        for copy in x_copies:
+        for copy in copies["x"]:
             wait_for(*copy)
         if stage is None:
             hear(2 * s + 1)
@@ -453,7 +488,7 @@
                 st[q, :, :, lanes] = jnp.where(lower, halo, keep) if e == 1 else jnp.where(lower, keep, halo)
 
         lax.fori_loop(0, SPAN_PATCHES, ends, 0)
-        settle(range(TILES) if stage is None else (0, TILES - 1))
+        settle(end_tiles)
 
     flat = pm.reshape(pm.shape[0] * 2 * HALF, LANES)
 
@@ -583,12 +618,8 @@
             hear(k)
         exchange(0)
 
-    def whole_step(s, carry):
-        step(s)
-        return carry
-
-    lax.fori_loop(0, STEPS - 1, whole_step, 0)
-    step(STEPS - 1, early)
+    for s in range(STEPS):
+        step(s, early if s == STEPS - 1 else None)
     fill(1)
     offer(1)
     exchange(1)
@@ -748,6 +779,7 @@
         in_specs=[smem, vmem, vmem],
         out_specs=(vmem, vmem, vmem),
         scratch_shapes=[
+            pltpu.VMEM(state, f32),
             pltpu.VMEM(state, f32),
             pltpu.VMEM(state, f32),
             pltpu.VMEM((18,) + state[1:], f32),

time: 62.5 us -> 61.6 us (0.986)
  Pallas kernels: 60.1 us -> 59.2 us
    pallas_call x1, Pallas kernels: 58.5 us -> 57.7 us  [body(): pl.pallas_call(lambda *refs: lattice_kernel(nb, nc, *refs), out_shape=(ja...]
where the time goes in v8:
time: 61.6 us; the launch traced here: 61.5 us
  Pallas kernels  59.2 us (96%)
  local copies, waits for them, and re-layouts  1.55 us (3%)
  between operations  0.69 us (1%)
    pallas_call x1, Pallas kernels, body(): pl.pallas_call(lambda *refs: lattice_kernel(nb, nc, *refs), out_shape=(ja...  57.7 us
    pallas_call x1, Pallas kernels, unpack(): pl.pallas_call(unpack_kernel, out_shape=jax.ShapeDtypeStruct((19, patches...  1.54 us

profile of v8, /device:TPU:0, one launch (start us, length us, event | category | flops | bytes accessed | tf_op | source)
XLA Modules:
  0.0 61.5 jit_solution(2332588230931592725)
XLA Ops:
  0.0 0.0 copy-start.1
  0.0 57.7 %shard_map.37 = (f32[80,40,128]{2,1,0:T(8,128)S(1)}, f32[32,80,128]{2,1,0:T(8,128)S(1)}, s32[8,128]{1,0:T(8,128)S(1)}) custom-call(s32[32]{0:T(128)} %refs_0_.1, s32[1,32]{1,0:T(1,128)} %bitcast.5, f32[19,32,512]{2,1,0:T(8,128)} %bitcast.4), custom_call_target="tpu_custom_call" | custom-call | tf_op jit(solution)/shard_map/pallas_call | solution.py:772
  57.7 0.5 slice.3
  58.9 0.0 copy-done.1
  58.9 1.6 %conditional.1 = (f32[19,32,512]{2,1,0:T(8,128)S(1)}) conditional(s32[]{:T(128)} %bitcast.2, (s32[8,128]{1,0:T(8,128)S(1)}, f32[80,40,128]{2,1,0:T(8,128)S(1)}) %tuple.11, (s32[32]{0:T(128)S(1)}, f32[32,80,128]{2,1,0:T(8,128)S(1)}) %tuple.17), branch_computations={%region_0.0_spmd, %region_1.5_spmd} | conditional | flops 15968 | bytes 2312 | solution.py:858
  58.9 1.5 %branch_0_fun.1 = f32[19,32,512]{2,1,0:T(8,128)S(1)} custom-call(s32[8,128]{1,0:T(8,128)S(1)} %get-tuple-element.16.ridx, f32[80,40,128]{2,1,0:T(8,128)S(1)} %get-tuple-element.17.got_ref), custom_call_target="tpu_custom_call" | custom-call | tf_op jit(solution)/shard_map/cond/branch_0_fun/pallas_call | solution.py:826
  60.4 0.0 copy-start
  60.4 1.0 %copy-done = f32[19,32,512]{2,1,0:T(8,128)} copy-done((f32[19,32,512]{2,1,0:T(8,128)}, f32[19,32,512]{2,1,0:T(8,128)S(1)}, u32[]{:S(2)}) %copy-start) | copy-done | bytes 1245208
Async XLA Ops:
  0.0 58.9 %copy-start.1 = (s32[32]{0:T(128)S(1)}, s32[32]{0:T(128)}, u32[]{:S(2)}) copy-start(s32[32]{0:T(128)} %param.7) | copy-start | bytes 388
  60.4 1.0 %copy-start = (f32[19,32,512]{2,1,0:T(8,128)}, f32[19,32,512]{2,1,0:T(8,128)S(1)}, u32[]{:S(2)}) copy-start(f32[19,32,512]{2,1,0:T(8,128)S(1)} %get-tuple-element.32) | copy-start | bytes 3735556

commit v9 on v8

--- a/solution.py
+++ b/solution.py
@@ -281,7 +281,6 @@
             src_ref=lev_ref, dst_ref=lv.at[n], send_sem=lsend.at[n], recv_sem=lrecv.at[n],
             device_id=at(-dx, -dy), device_id_type=MESH)
         outgoing, incoming = ends_of(-dx)
-        start_to(outgoing, copy)
         level_copies.append((outgoing, incoming, copy))
 
     def patch_copy(half, k):
@@ -289,37 +288,36 @@
         rows = slice(0, MARK if half else FIRST)
         return pltpu.make_async_remote_copy(
             src_ref=sent.at[half, d, rows], dst_ref=got_ref.at[2 * me + half, rows],
-            send_sem=psend.at[half, k], recv_sem=precv.at[half, k], device_id=device(d),
+            send_sem=psend.at[half], recv_sem=precv.at[half], device_id=device(d),
             device_id_type=MESH)
 
     def extra_copy(k):
         d = peer(k)
         return pltpu.make_async_remote_copy(
-            src_ref=extra.at[d], dst_ref=got_extra.at[me], send_sem=esend.at[k],
-            recv_sem=erecv.at[k], device_id=device(d), device_id_type=MESH)
-
-    for copy in level_copies:
-        wait_for(*copy)
-    scales = targets(lambda dx, dy: lv[around.index((dx, dy))])
-
-    def amend(q, tile, rows):
-        spot = (rows, slice(0, 8), lanes_of(tile))
-        before = cq[(q - 1,) + spot]
-        after = coefficient(q, tile, scales, rows)
-        held = pb[(q,) + spot]
-        pb[(q,) + spot] = held + (after - before) / (1.0 - before) * (st[(q,) + spot] - held)
-        cq[(q - 1,) + spot] = after
-
-    for q in range(1, 19):
-        e = VELOCITIES[q]
-        outer_tile = {0: None, 1: TILES - 1, -1: 0}[e[0]]
-        if e[0]:
-            amend(q, outer_tile, everything)
-        if e[1]:
-            r = SPAN_PATCHES - 1 if e[1] == 1 else 0
-            for tile in range(TILES):
-                if tile != outer_tile:
-                    amend(q, tile, slice(r, r + 1))
+            src_ref=extra.at[d], dst_ref=got_extra.at[me], send_sem=esend,
+            recv_sem=erecv, device_id=device(d), device_id_type=MESH)
+
+    own_scale = jnp.where(fine, RESCALE, 1.0)
+    kappa = gain / (1.0 - gain)
+
+    def take_levels():
+        for copy in level_copies:
+            wait_for(*copy)
+        scales = targets(lambda dx, dy: lv[around.index((dx, dy))])
+
+        def refresh(q, tile, rows):
+            cq[q - 1, rows, :, lanes_of(tile)] = coefficient(q, tile, scales, rows)
+
+        for q in range(1, 19):
+            e = VELOCITIES[q]
+            outer_tile = {0: None, 1: TILES - 1, -1: 0}[e[0]]
+            if e[0]:
+                refresh(q, outer_tile, everything)
+            if e[1]:
+                r = SPAN_PATCHES - 1 if e[1] == 1 else 0
+                for tile in range(TILES):
+                    if tile != outer_tile:
+                        refresh(q, tile, slice(r, r + 1))
 
     def spin(v, amount):
         return pltpu.roll(v, amount % LANES, axis=v.ndim - 1)
@@ -347,34 +345,65 @@
             start_to(outgoing, copy)
             copies["x" if dx else "y"].append((outgoing, incoming, copy))
 
+        parts = 2 if s == 0 else 1
+
+        def face(q, rows, tile):
+            spot = (q, rows, slice(0, 8), lanes_of(tile))
+            values = [pb[spot]]
+            if s == 0:
+                values.append(kappa[rows] * (st[spot] - values[0]))
+            return [along_z(q, v) for v in values]
+
         def send_x():
             for way, e, group in ((0, 1, X_UP), (1, -1, X_DOWN)):
                 for n, q in enumerate(group):
-                    v = along_z(q, pb[q, :, :, lanes_of(TILES - 1 if e == 1 else 0)])
-                    turned = spin(v, 64)
-                    if e == 1:
-                        xs[s, way, n] = jnp.where(half, turned[:2], v[2:])
-                    else:
-                        xs[s, way, n] = jnp.where(half, v[:2], turned[2:])
-                    if q in DIAGONAL:
-                        ds[s, DIAGONAL.index(q)] = turned[SPAN_PATCHES - 1 if VELOCITIES[q][1] == 1 else 0]
+                    for part_id, v in enumerate(face(q, everything, TILES - 1 if e == 1 else 0)):
+                        turned = spin(v, 64)
+                        if e == 1:
+                            xs[s, way, part_id, n] = jnp.where(half, turned[:2], v[2:])
+                        else:
+                            xs[s, way, part_id, n] = jnp.where(half, v[:2], turned[2:])
+                        if q in DIAGONAL:
+                            edge = turned[SPAN_PATCHES - 1 if VELOCITIES[q][1] == 1 else 0]
+                            ds[s, DIAGONAL.index(q), part_id] = edge
             for way, dx in ((0, 1), (1, -1)):
-                send(xs.at[s, way], xr.at[s, way], 2 + way, dx, 0)
+                send(xs.at[s, way, :parts], xr.at[s, way, :parts], 2 + way, dx, 0)
             for n, q in enumerate(DIAGONAL):
-                send(ds.at[s, n], dr.at[s, n], 4 + n, *VELOCITIES[q][:2])
+                send(ds.at[s, n, :parts], dr.at[s, n, :parts], 4 + n, *VELOCITIES[q][:2])
 
         def send_y():
             for way, e, group in ((0, 1, Y_UP), (1, -1, Y_DOWN)):
                 r = SPAN_PATCHES - 1 if e == 1 else 0
                 for n, q in enumerate(group):
                     for tile in range(TILES):
-                        ys[s, way, n, :, lanes_of(tile)] = along_z(q, pb[q, r : r + 1, :, lanes_of(tile)])[0]
+                        for part_id, v in enumerate(face(q, slice(r, r + 1), tile)):
+                            ys[s, way, part_id, n, :, lanes_of(tile)] = v[0]
             for way, dy in ((0, 1), (1, -1)):
-                send(ys.at[s, way], yr.at[s, way], way, 0, dy)
+                send(ys.at[s, way, :parts], yr.at[s, way, :parts], way, 0, dy)
+
+        def y_halo(e, n, tile):
+            way, r = (0, 0) if e == 1 else (1, SPAN_PATCHES - 1)
+            value = yr[s, way, 0, n, :, lanes_of(tile)]
+            if s == 0:
+                value = value + (own_scale[r] - 1.0) * yr[s, way, 1, n, :, lanes_of(tile)]
+            return value[None]
+
+        def x_halo(way, e, n, q):
+            values = []
+            for part_id in range(parts):
+                h = xr[s, way, part_id, n]
+                turned = spin(h, 64)
+                halo = jnp.concatenate([h, turned] if e == 1 else [turned, h], axis=0)
+                if q in DIAGONAL:
+                    halo = along_y(q, halo, dr[s, DIAGONAL.index(q), part_id][None])
+                values.append(halo)
+            return values[0] + (own_scale - 1.0) * values[1] if s == 0 else values[0]
 
         if s == 0:
             send_x()
             send_y()
+            for outgoing, _, copy in level_copies:
+                start_to(outgoing, copy)
         elif stage is None:
             first_rows(end_tiles, 0, SPAN_PATCHES)
             send_x()
@@ -390,10 +419,8 @@
             half_turn = 64 if e[0] else 0
             tiles = [along_z(q, pb[q, :, :, lanes_of(tile)], 0 if e[1] else half_turn) for tile in range(TILES)]
             if e[1]:
-                way, group = (0, Y_UP) if e[1] == 1 else (1, Y_DOWN)
-                n = group.index(q)
-                tiles = [along_y(q, v, yr[s, way, n, :, lanes_of(tile)][None], half_turn)
-                         for tile, v in enumerate(tiles)]
+                n = (Y_UP if e[1] == 1 else Y_DOWN).index(q)
+                tiles = [along_y(q, v, y_halo(e[1], n, tile), half_turn) for tile, v in enumerate(tiles)]
             if e[0]:
                 turned = list(tiles)
                 for tile in range(TILES):
@@ -463,6 +490,8 @@
         lax.fori_loop(0, SPAN_PATCHES, middle, 0)
         lax.fori_loop(0, SPAN_PATCHES, ends, 0)
         settle(middle_tiles)
+        if s == 0:
+            take_levels()
         if stage is None:
             first_rows(middle_tiles, 0, SPAN_PATCHES)
         else:
@@ -475,11 +504,7 @@
         for way, e, group in ((0, 1, X_UP), (1, -1, X_DOWN)):
             outside = b == (0 if e == 1 else nb - 1)
             for n, q in enumerate(group):
-                h = xr[s, way, n]
-                turned = spin(h, 64)
-                halo = jnp.concatenate([h, turned] if e == 1 else [turned, h], axis=0)
-                if q in DIAGONAL:
-                    halo = along_y(q, halo, dr[s, DIAGONAL.index(q)][None])
+                halo = x_halo(way, e, n, q)
                 along = e * INFLOW
                 const = WEIGHTS[q] * (1.0 + 3.0 * along + 4.5 * along * along - 1.5 * INFLOW * INFLOW)
                 halo = jnp.where(outside, jnp.full(halo.shape, const, jnp.float32), halo)
@@ -516,13 +541,13 @@
     def swap_copy(half, j):
         return pltpu.make_async_remote_copy(
             src_ref=second.at[half, rows_of(j)], dst_ref=theirs.at[half, rows_of(j)],
-            send_sem=csend.at[half, j], recv_sem=crecv.at[half, j], device_id=at(0, 1),
+            send_sem=csend.at[half], recv_sem=crecv.at[half, j], device_id=at(0, 1),
             device_id_type=MESH)
 
     def shuffle_copy(j):
         return pltpu.make_async_remote_copy(
-            src_ref=away.at[rows_of(j)], dst_ref=across.at[rows_of(j)], send_sem=qsend.at[j],
-            recv_sem=qrecv.at[j], device_id=device(lax.bitwise_xor(me, nc)), device_id_type=MESH)
+            src_ref=away.at[rows_of(j)], dst_ref=across.at[rows_of(j)], send_sem=qsend,
+            recv_sem=qrecv, device_id=device(lax.bitwise_xor(me, nc)), device_id_type=MESH)
 
     def tag_of(which, d):
         return tags[which, pl.ds(d, 1), :]
@@ -624,13 +649,14 @@
     offer(1)
     exchange(1)
 
-    def swapped(j, carry):
-        swap_copy(0, j).wait_send()
-        swap_copy(1, j).wait_send()
-        shuffle_copy(j).wait()
-        return carry
-
-    lax.fori_loop(0, chunks, swapped, 0)
+    def waiter(ref, send, recv):
+        return pltpu.make_async_remote_copy(
+            src_ref=ref, dst_ref=ref, send_sem=send, recv_sem=recv, device_id=at(0, 1), device_id_type=MESH)
+
+    for which in range(2):
+        waiter(second.at[which], csend.at[which], csend.at[which]).wait_send()
+    waiter(away, qsend, qrecv).wait_send()
+    waiter(across, qsend, qrecv).wait_recv()
     near_tags = kept[:, TAG, :]
     far_tags = across[:, TAG, :]
     over = (near_tags > OVER / 2) | (far_tags > OVER / 2) | ((near_tags > -0.5) & (far_tags > -0.5))
@@ -660,13 +686,12 @@
     extra_copy(mask_at(count - 1)).start()
     got_extra[me] = extra[me]
 
-    def finish(k, carry):
-        patch_copy(0, k).wait()
-        patch_copy(1, k).wait()
-        extra_copy(k).wait()
-        return carry
-
-    lax.fori_loop(1, count, finish, 0)
+    for which, rows in ((0, FIRST), (1, MARK)):
+        arrived = waiter(sent.at[which, 1:, :rows], psend.at[which], precv.at[which])
+        arrived.wait_send()
+        arrived.wait_recv()
+    waiter(extra.at[1:], esend, erecv).wait_send()
+    waiter(got_extra.at[1:], esend, erecv).wait_recv()
 
     def assemble(g, carry):
         for t in range(TILES):
@@ -794,12 +819,12 @@
             pltpu.VMEM(small, f32),
             pltpu.VMEM((8, LANES), f32),
             pltpu.VMEM((3 * nc - 1, 8, LANES), f32),
-            pltpu.VMEM((STEPS, 2, 5, 8, CELLS), f32),
-            pltpu.VMEM((STEPS, 2, 5, 8, CELLS), f32),
-            pltpu.VMEM((STEPS, 2, 5, 2, 8, LANES), f32),
-            pltpu.VMEM((STEPS, 2, 5, 2, 8, LANES), f32),
-            pltpu.VMEM((STEPS, len(DIAGONAL), 8, LANES), f32),
-            pltpu.VMEM((STEPS, len(DIAGONAL), 8, LANES), f32),
+            pltpu.VMEM((STEPS, 2, 2, 5, 8, CELLS), f32),
+            pltpu.VMEM((STEPS, 2, 2, 5, 8, CELLS), f32),
+            pltpu.VMEM((STEPS, 2, 2, 5, 2, 8, LANES), f32),
+            pltpu.VMEM((STEPS, 2, 2, 5, 2, 8, LANES), f32),
+            pltpu.VMEM((STEPS, len(DIAGONAL), 2, 8, LANES), f32),
+            pltpu.VMEM((STEPS, len(DIAGONAL), 2, 8, LANES), f32),
             pltpu.VMEM((devices, LANES), jnp.int32),
             pltpu.SMEM((devices, LANES), jnp.int32),
             pltpu.VMEM((2, devices, LANES), f32),
@@ -807,14 +832,14 @@
             dma((STEPS, 8)),
             dma((3 * nc - 1,)),
             dma((3 * nc - 1,)),
-            dma((2, devices)),
-            dma((2, devices)),
-            dma((devices,)),
-            dma((devices,)),
+            dma((2,)),
+            dma((2,)),
+            dma,
+            dma,
+            dma((2,)),
             dma((2, devices // GROUP)),
-            dma((2, devices // GROUP)),
-            dma((devices // GROUP,)),
-            dma((devices // GROUP,)),
+            dma,
+            dma,
             dma,
             pltpu.SemaphoreType.REGULAR((rounds,)),
             pltpu.SemaphoreType.REGULAR((rounds,)),

time: 61.6 us -> 59.1 us (0.959)
  Pallas kernels: 59.2 us -> 56.7 us
    pallas_call x1, Pallas kernels: 57.7 us -> 55.2 us  [body(): pl.pallas_call(lambda *refs: lattice_kernel(nb, nc, *refs), out_shape=(ja...]
where the time goes in v9:
time: 59.1 us; the launch traced here: 59 us
  Pallas kernels  56.7 us (96%)
  local copies, waits for them, and re-layouts  1.55 us (3%)
  between operations  0.69 us (1%)
    pallas_call x1, Pallas kernels, body(): pl.pallas_call(lambda *refs: lattice_kernel(nb, nc, *refs), out_shape=(ja...  55.2 us
    pallas_call x1, Pallas kernels, unpack(): pl.pallas_call(unpack_kernel, out_shape=jax.ShapeDtypeStruct((19, patches...  1.54 us

profile of v9, /device:TPU:0, one launch (start us, length us, event | category | flops | bytes accessed | tf_op | source)
XLA Modules:
  0.0 59.0 jit_solution(14856703355476191444)
XLA Ops:
  0.0 0.0 copy-start.1
  0.0 55.2 %shard_map.37 = (f32[80,40,128]{2,1,0:T(8,128)S(1)}, f32[32,80,128]{2,1,0:T(8,128)S(1)}, s32[8,128]{1,0:T(8,128)S(1)}) custom-call(s32[32]{0:T(128)} %refs_0_.1, s32[1,32]{1,0:T(1,128)} %bitcast.5, f32[19,32,512]{2,1,0:T(8,128)} %bitcast.4), custom_call_target="tpu_custom_call" | custom-call | tf_op jit(solution)/shard_map/pallas_call | solution.py:797
  55.2 0.5 slice.3
  56.4 0.0 copy-done.1
  56.4 1.6 %conditional.1 = (f32[19,32,512]{2,1,0:T(8,128)S(1)}) conditional(s32[]{:T(128)} %bitcast.2, (s32[8,128]{1,0:T(8,128)S(1)}, f32[80,40,128]{2,1,0:T(8,128)S(1)}) %tuple.11, (s32[32]{0:T(128)S(1)}, f32[32,80,128]{2,1,0:T(8,128)S(1)}) %tuple.17), branch_computations={%region_0.0_spmd, %region_1.5_spmd} | conditional | flops 15968 | bytes 2312 | solution.py:883
  56.4 1.5 %branch_0_fun.1 = f32[19,32,512]{2,1,0:T(8,128)S(1)} custom-call(s32[8,128]{1,0:T(8,128)S(1)} %get-tuple-element.16.ridx, f32[80,40,128]{2,1,0:T(8,128)S(1)} %get-tuple-element.17.got_ref), custom_call_target="tpu_custom_call" | custom-call | tf_op jit(solution)/shard_map/cond/branch_0_fun/pallas_call | solution.py:851
  57.9 0.0 copy-start
  57.9 1.0 %copy-done = f32[19,32,512]{2,1,0:T(8,128)} copy-done((f32[19,32,512]{2,1,0:T(8,128)}, f32[19,32,512]{2,1,0:T(8,128)S(1)}, u32[]{:S(2)}) %copy-start) | copy-done | bytes 1245208
Async XLA Ops:
  0.0 56.4 %copy-start.1 = (s32[32]{0:T(128)S(1)}, s32[32]{0:T(128)}, u32[]{:S(2)}) copy-start(s32[32]{0:T(128)} %param.7) | copy-start | bytes 388
  57.9 1.0 %copy-start = (f32[19,32,512]{2,1,0:T(8,128)}, f32[19,32,512]{2,1,0:T(8,128)S(1)}, u32[]{:S(2)}) copy-start(f32[19,32,512]{2,1,0:T(8,128)S(1)} %get-tuple-element.32) | copy-start | bytes 3735556

commit v10 on v9

--- a/solution.py
+++ b/solution.py
@@ -275,13 +275,17 @@
     def ends_of(dx):
         return {0: (None, None), 1: (above, below), -1: (below, above)}[dx]
 
+    def waiter(ref, send, recv):
+        return pltpu.make_async_remote_copy(
+            src_ref=ref, dst_ref=ref, send_sem=send, recv_sem=recv, device_id=at(0, 1), device_id_type=MESH)
+
     level_copies = []
     for n, (dx, dy) in enumerate(around):
         copy = pltpu.make_async_remote_copy(
-            src_ref=lev_ref, dst_ref=lv.at[n], send_sem=lsend.at[n], recv_sem=lrecv.at[n],
+            src_ref=lev_ref, dst_ref=lv.at[n], send_sem=lsend.at[dx + 1], recv_sem=lrecv.at[dx + 1],
             device_id=at(-dx, -dy), device_id_type=MESH)
         outgoing, incoming = ends_of(-dx)
-        level_copies.append((outgoing, incoming, copy))
+        level_copies.append((outgoing, copy))
 
     def patch_copy(half, k):
         d = peer(k)
@@ -301,8 +305,9 @@
     kappa = gain / (1.0 - gain)
 
     def take_levels():
-        for copy in level_copies:
-            wait_for(*copy)
+        for dx in (-1, 0, 1):
+            some = nc if dx else nc - 1
+            wait_for(*ends_of(-dx), waiter(lv.at[:some], lsend.at[dx + 1], lrecv.at[dx + 1]))
         scales = targets(lambda dx, dy: lv[around.index((dx, dy))])
 
         def refresh(q, tile, rows):
@@ -335,15 +340,15 @@
         return jnp.where(in_tile[1, e], spin(moved, more - 56 * e), spin(v, more + 8 * e))
 
     def step(s, stage=None):
-        copies = {"x": [], "y": []}
-
-        def send(src, dst, n, dx, dy):
+        def send(src, dst, dx, dy):
             copy = pltpu.make_async_remote_copy(
-                src_ref=src, dst_ref=dst, send_sem=send_sem.at[s, n], recv_sem=recv_sem.at[s, n],
+                src_ref=src, dst_ref=dst, send_sem=send_sem.at[s, dx + 1], recv_sem=recv_sem.at[s, dx + 1],
                 device_id=at(dx, dy), device_id_type=MESH)
-            outgoing, incoming = ends_of(dx)
-            start_to(outgoing, copy)
-            copies["x" if dx else "y"].append((outgoing, incoming, copy))
+            start_to(ends_of(dx)[0], copy)
+
+        def await_halos(dx):
+            ref = pb2.at[: 3 * parts, :, :, :LANES] if dx else ys.at[s, :, :parts]
+            wait_for(*ends_of(dx), waiter(ref, send_sem.at[s, dx + 1], recv_sem.at[s, dx + 1]))
 
         parts = 2 if s == 0 else 1
 
@@ -367,9 +372,9 @@
                             edge = turned[SPAN_PATCHES - 1 if VELOCITIES[q][1] == 1 else 0]
                             ds[s, DIAGONAL.index(q), part_id] = edge
             for way, dx in ((0, 1), (1, -1)):
-                send(xs.at[s, way, :parts], xr.at[s, way, :parts], 2 + way, dx, 0)
+                send(xs.at[s, way, :parts], xr.at[s, way, :parts], dx, 0)
             for n, q in enumerate(DIAGONAL):
-                send(ds.at[s, n, :parts], dr.at[s, n, :parts], 4 + n, *VELOCITIES[q][:2])
+                send(ds.at[s, n, :parts], dr.at[s, n, :parts], *VELOCITIES[q][:2])
 
         def send_y():
             for way, e, group in ((0, 1, Y_UP), (1, -1, Y_DOWN)):
@@ -379,7 +384,7 @@
                         for part_id, v in enumerate(face(q, slice(r, r + 1), tile)):
                             ys[s, way, part_id, n, :, lanes_of(tile)] = v[0]
             for way, dy in ((0, 1), (1, -1)):
-                send(ys.at[s, way, :parts], yr.at[s, way, :parts], way, 0, dy)
+                send(ys.at[s, way, :parts], yr.at[s, way, :parts], 0, dy)
 
         def y_halo(e, n, tile):
             way, r = (0, 0) if e == 1 else (1, SPAN_PATCHES - 1)
@@ -402,7 +407,7 @@
         if s == 0:
             send_x()
             send_y()
-            for outgoing, _, copy in level_copies:
+            for outgoing, copy in level_copies:
                 start_to(outgoing, copy)
         elif stage is None:
             first_rows(end_tiles, 0, SPAN_PATCHES)
@@ -434,8 +439,7 @@
         for q in range(19):
             if not VELOCITIES[q][1]:
                 shift(q)
-        for copy in copies["y"]:
-            wait_for(*copy)
+        await_halos(0)
         hear(2 * s)
         tell(2 * s + 1)
         for q in range(19):
@@ -496,8 +500,8 @@
             first_rows(middle_tiles, 0, SPAN_PATCHES)
         else:
             stage()
-        for copy in copies["x"]:
-            wait_for(*copy)
+        await_halos(1)
+        await_halos(-1)
         if stage is None:
             hear(2 * s + 1)
             tell(2 * s + 2)
@@ -538,10 +542,15 @@
     def rows_of(j):
         return pl.ds(chunk_at(j) * GROUP, GROUP)
 
+    def whole_swap():
+        return pltpu.make_async_remote_copy(
+            src_ref=second.at[1], dst_ref=theirs.at[1], send_sem=csend.at[1],
+            recv_sem=crecv.at[chunks], device_id=at(0, 1), device_id_type=MESH)
+
     def swap_copy(half, j):
         return pltpu.make_async_remote_copy(
             src_ref=second.at[half, rows_of(j)], dst_ref=theirs.at[half, rows_of(j)],
-            send_sem=csend.at[half], recv_sem=crecv.at[half, j], device_id=at(0, 1),
+            send_sem=csend.at[half], recv_sem=crecv.at[j], device_id=at(0, 1),
             device_id_type=MESH)
 
     def shuffle_copy(j):
@@ -562,14 +571,18 @@
                     second[0, m, MARK : MARK + 1, :] = tag_of(1, d)
                     second[0, m, FIRST : FIRST + 1, :] = tag_of(0, d)
 
-            @pl.when(j > 0)
-            def _():
-                swap_copy(half, j - 1).start()
+            if half == 0:
+                @pl.when(j > 0)
+                def _():
+                    swap_copy(half, j - 1).start()
 
             return carry
 
         lax.fori_loop(0, chunks, pack_second, 0)
-        swap_copy(half, chunks - 1).start()
+        if half == 0:
+            swap_copy(half, chunks - 1).start()
+        else:
+            whole_swap().start()
 
     zero = c == 0
 
@@ -619,8 +632,12 @@
                 patch_copy(half, k).start()
 
     def exchange(half):
+        if half:
+            whole_swap().wait_recv()
+
         def post(j, carry):
-            swap_copy(half, j).wait_recv()
+            if half == 0:
+                swap_copy(half, j).wait_recv()
             pack_chunk(half, j)
 
             @pl.when(j > 0)
@@ -649,10 +666,6 @@
     offer(1)
     exchange(1)
 
-    def waiter(ref, send, recv):
-        return pltpu.make_async_remote_copy(
-            src_ref=ref, dst_ref=ref, send_sem=send, recv_sem=recv, device_id=at(0, 1), device_id_type=MESH)
-
     for which in range(2):
         waiter(second.at[which], csend.at[which], csend.at[which]).wait_send()
     waiter(away, qsend, qrecv).wait_send()
@@ -703,13 +716,13 @@
         return carry
 
     lax.fori_loop(0, chunks, assemble, 0)
-    source = lax.broadcasted_iota(jnp.int32, (2 * count, LANES), 0)
-    wanted = lax.broadcasted_iota(jnp.int32, (2 * count, LANES), 1).astype(jnp.float32)
-    first_hit = (got_ref[: 2 * count, MARK, :] == wanted) & (source % 2 == 0)
-    index = jnp.sum(jnp.where(first_hit, source, 0), axis=0, keepdims=True)
-    source = source[:count]
+    source = lax.broadcasted_iota(jnp.int32, (count, LANES), 0)
+    wanted = lax.broadcasted_iota(jnp.int32, (count, LANES), 1).astype(jnp.float32)
+    arrived_flat = got_ref.reshape(got_ref.shape[0] * HALF, LANES)
+    first_hit = arrived_flat[pl.ds(MARK, count, stride=2 * HALF), :] == wanted
+    index = jnp.sum(jnp.where(first_hit, 2 * source, 0), axis=0, keepdims=True)
     extra_tags = got_extra[:, TAG, :]
-    extra_hit = (extra_tags == wanted[:count]) & (source % GROUP == 0)
+    extra_hit = (extra_tags == wanted) & (source % GROUP == 0)
     place = source // GROUP * 2 + 2 * count
     index = index + jnp.sum(jnp.where(extra_hit, place, 0), axis=0, keepdims=True)
     over = jnp.max(extra_tags, axis=0, keepdims=True)
@@ -770,15 +783,20 @@
 
 
 def unpack_kernel(ridx, got_ref, out_ref):
-    for t in range(out_ref.shape[1]):
+    groups = out_ref.shape[1]
+    flat = out_ref.reshape(19 * groups * TILES * 8, LANES)
+    stride = groups * TILES * 8
+    for t in range(groups * 8):
         base = ridx[0, t]
         for tile in range(TILES):
             block = got_ref.at[base + half_of(tile)]
-            lanes = slice(tile * LANES, (tile + 1) * LANES)
-            low = low_row(0, tile)
-            out_ref[:MAIN, t, lanes] = block[low : low + MAIN, :]
-            low = low_row(MAIN, tile)
-            out_ref[MAIN:, t, lanes] = block[2 * MAIN :, :][low - 2 * MAIN : low - 2 * MAIN + TAIL]
+            row = (t // 8 * TILES + tile) * 8 + t % 8
+            place = place_of(tile)
+            for q in range(0, MAIN, 8):
+                flat[pl.ds(row + q * stride, 8, stride=stride), :] = block[place * MAIN + q : place * MAIN + q + 8, :]
+            low = place * TAIL
+            rest = block[2 * MAIN :, :][low : low + TAIL]
+            flat[pl.ds(row + MAIN * stride, TAIL, stride=stride), :] = rest
 
 
 def body(nb, nc, f_home, levels, plan):
@@ -828,16 +846,16 @@
             pltpu.VMEM((devices, LANES), jnp.int32),
             pltpu.SMEM((devices, LANES), jnp.int32),
             pltpu.VMEM((2, devices, LANES), f32),
-            dma((STEPS, 8)),
-            dma((STEPS, 8)),
-            dma((3 * nc - 1,)),
-            dma((3 * nc - 1,)),
+            dma((STEPS, 3)),
+            dma((STEPS, 3)),
+            dma((3,)),
+            dma((3,)),
             dma((2,)),
             dma((2,)),
             dma,
             dma,
             dma((2,)),
-            dma((2, devices // GROUP)),
+            dma((devices // GROUP + 1,)),
             dma,
             dma,
             dma,
@@ -850,7 +868,7 @@
     def unpack(table, got):
         return pl.pallas_call(
             unpack_kernel,
-            out_shape=jax.ShapeDtypeStruct((19, patches, CELLS), f32),
+            out_shape=jax.ShapeDtypeStruct((19, patches // 8, TILES, 8, LANES), f32),
             in_specs=[smem, vmem],
             out_specs=vmem,
             compiler_params=pltpu.CompilerParams(vmem_limit_bytes=40 * 1024 * 1024),
@@ -882,7 +900,7 @@
 
     out = lax.cond(table[1, 0] > 0, in_full, lambda table, got, packed, plan: unpack(table, got),
                    table, got, packed, plan)
-    return jnp.transpose(out, (1, 0, 2))
+    return jnp.transpose(out, (1, 3, 0, 2, 4)).reshape(f_home.shape)
 
 
 def solution(mesh):

time: 59.1 us -> 59 us (level)
  no operation moved by 1% of the time
where the time goes in v10:
time: 59 us; the launch traced here: 58.8 us
  Pallas kernels  56.6 us (96%)
  local copies, waits for them, and re-layouts  1.55 us (3%)
  between operations  0.69 us (1%)
    pallas_call x1, Pallas kernels, body(): pl.pallas_call(lambda *refs: lattice_kernel(nb, nc, *refs), out_shape=(ja...  54.9 us
    pallas_call x1, Pallas kernels, unpack(): pl.pallas_call(unpack_kernel, out_shape=jax.ShapeDtypeStruct((19, patches...  1.65 us

profile of v10, /device:TPU:0, one launch (start us, length us, event | category | flops | bytes accessed | tf_op | source)
XLA Modules:
  0.0 58.8 jit_solution(7522544545736783832)
XLA Ops:
  0.0 0.0 copy-start.1
  0.0 54.9 %shard_map.37 = (f32[80,40,128]{2,1,0:T(8,128)S(1)}, f32[32,80,128]{2,1,0:T(8,128)S(1)}, s32[8,128]{1,0:T(8,128)S(1)}) custom-call(s32[32]{0:T(128)} %refs_0_.1, s32[1,32]{1,0:T(1,128)} %bitcast.7, f32[19,32,512]{2,1,0:T(8,128)} %bitcast.6), custom_call_target="tpu_custom_call" | custom-call | tf_op jit(solution)/shard_map/pallas_call | solution.py:815
  54.9 0.5 slice.3
  56.1 0.0 copy-done.1
  56.1 1.7 %conditional.1 = (f32[19,4,4,8,128]{4,3,2,1,0:T(8,128)S(1)}) conditional(s32[]{:T(128)} %bitcast.2, (s32[8,128]{1,0:T(8,128)S(1)}, f32[80,40,128]{2,1,0:T(8,128)S(1)}) %tuple.11, (s32[32]{0:T(128)S(1)}, f32[32,80,128]{2,1,0:T(8,128)S(1)}) %tuple.17), branch_computations={%region_0.0_spmd, %region_1.5_spmd} | conditional | flops 15968 | bytes 2312 | solution.py:901
  56.1 1.7 %branch_0_fun.1 = f32[19,4,4,8,128]{4,3,2,1,0:T(8,128)S(1)} custom-call(s32[8,128]{1,0:T(8,128)S(1)} %get-tuple-element.16.ridx, f32[80,40,128]{2,1,0:T(8,128)S(1)} %get-tuple-element.17.got_ref), custom_call_target="tpu_custom_call" | custom-call | tf_op jit(solution)/shard_map/cond/branch_0_fun/pallas_call | solution.py:869
  57.8 0.0 copy-start
  57.8 1.0 %copy-done = f32[19,4,4,8,128]{4,3,2,1,0:T(8,128)} copy-done((f32[19,4,4,8,128]{4,3,2,1,0:T(8,128)}, f32[19,4,4,8,128]{4,3,2,1,0:T(8,128)S(1)}, u32[]{:S(2)}) %copy-start) | copy-done | bytes 1245208
Async XLA Ops:
  0.0 56.1 %copy-start.1 = (s32[32]{0:T(128)S(1)}, s32[32]{0:T(128)}, u32[]{:S(2)}) copy-start(s32[32]{0:T(128)} %param.7) | copy-start | bytes 388
  57.8 1.0 %copy-start = (f32[19,4,4,8,128]{4,3,2,1,0:T(8,128)}, f32[19,4,4,8,128]{4,3,2,1,0:T(8,128)S(1)}, u32[]{:S(2)}) copy-start(f32[19,4,4,8,128]{4,3,2,1,0:T(8,128)S(1)} %get-tuple-element.32) | copy-start | bytes 3735556

commit v11 on v10

--- a/solution.py
+++ b/solution.py
@@ -783,20 +783,15 @@
 
 
 def unpack_kernel(ridx, got_ref, out_ref):
-    groups = out_ref.shape[1]
-    flat = out_ref.reshape(19 * groups * TILES * 8, LANES)
-    stride = groups * TILES * 8
-    for t in range(groups * 8):
+    for t in range(out_ref.shape[1]):
         base = ridx[0, t]
         for tile in range(TILES):
             block = got_ref.at[base + half_of(tile)]
-            row = (t // 8 * TILES + tile) * 8 + t % 8
-            place = place_of(tile)
-            for q in range(0, MAIN, 8):
-                flat[pl.ds(row + q * stride, 8, stride=stride), :] = block[place * MAIN + q : place * MAIN + q + 8, :]
-            low = place * TAIL
-            rest = block[2 * MAIN :, :][low : low + TAIL]
-            flat[pl.ds(row + MAIN * stride, TAIL, stride=stride), :] = rest
+            lanes = slice(tile * LANES, (tile + 1) * LANES)
+            low = low_row(0, tile)
+            out_ref[:MAIN, t, lanes] = block[low : low + MAIN, :]
+            low = low_row(MAIN, tile)
+            out_ref[MAIN:, t, lanes] = block[2 * MAIN :, :][low - 2 * MAIN : low - 2 * MAIN + TAIL]
 
 
 def body(nb, nc, f_home, levels, plan):
@@ -868,7 +863,7 @@
     def unpack(table, got):
         return pl.pallas_call(
             unpack_kernel,
-            out_shape=jax.ShapeDtypeStruct((19, patches // 8, TILES, 8, LANES), f32),
+            out_shape=jax.ShapeDtypeStruct((19, patches, CELLS), f32),
             in_specs=[smem, vmem],
             out_specs=vmem,
             compiler_params=pltpu.CompilerParams(vmem_limit_bytes=40 * 1024 * 1024),
@@ -900,7 +895,7 @@
 
     out = lax.cond(table[1, 0] > 0, in_full, lambda table, got, packed, plan: unpack(table, got),
                    table, got, packed, plan)
-    return jnp.transpose(out, (1, 3, 0, 2, 4)).reshape(f_home.shape)
+    return jnp.transpose(out, (1, 0, 2))
 
 
 def solution(mesh):

time: 59 us -> 58.9 us (level)
  no operation moved by 1% of the time
where the time goes in v11:
time: 58.9 us; the launch traced here: 58.7 us
  Pallas kernels  56.5 us (96%)
  local copies, waits for them, and re-layouts  1.55 us (3%)
  between operations  0.69 us (1%)
    pallas_call x1, Pallas kernels, body(): pl.pallas_call(lambda *refs: lattice_kernel(nb, nc, *refs), out_shape=(ja...  54.9 us
    pallas_call x1, Pallas kernels, unpack(): pl.pallas_call(unpack_kernel, out_shape=jax.ShapeDtypeStruct((19, patches...  1.54 us

profile of v11, /device:TPU:0, one launch (start us, length us, event | category | flops | bytes accessed | tf_op | source)
XLA Modules:
  0.0 58.7 jit_solution(1605719571230227112)
XLA Ops:
  0.0 0.0 copy-start.1
  0.0 54.9 %shard_map.37 = (f32[80,40,128]{2,1,0:T(8,128)S(1)}, f32[32,80,128]{2,1,0:T(8,128)S(1)}, s32[8,128]{1,0:T(8,128)S(1)}) custom-call(s32[32]{0:T(128)} %refs_0_.1, s32[1,32]{1,0:T(1,128)} %bitcast.5, f32[19,32,512]{2,1,0:T(8,128)} %bitcast.4), custom_call_target="tpu_custom_call" | custom-call | tf_op jit(solution)/shard_map/pallas_call | solution.py:810
  54.9 0.5 slice.3
  56.1 0.0 copy-done.1
  56.1 1.6 %conditional.1 = (f32[19,32,512]{2,1,0:T(8,128)S(1)}) conditional(s32[]{:T(128)} %bitcast.2, (s32[8,128]{1,0:T(8,128)S(1)}, f32[80,40,128]{2,1,0:T(8,128)S(1)}) %tuple.11, (s32[32]{0:T(128)S(1)}, f32[32,80,128]{2,1,0:T(8,128)S(1)}) %tuple.17), branch_computations={%region_0.0_spmd, %region_1.5_spmd} | conditional | flops 15968 | bytes 2312 | solution.py:896
  56.1 1.5 %branch_0_fun.1 = f32[19,32,512]{2,1,0:T(8,128)S(1)} custom-call(s32[8,128]{1,0:T(8,128)S(1)} %get-tuple-element.16.ridx, f32[80,40,128]{2,1,0:T(8,128)S(1)} %get-tuple-element.17.got_ref), custom_call_target="tpu_custom_call" | custom-call | tf_op jit(solution)/shard_map/cond/branch_0_fun/pallas_call | solution.py:864
  57.7 0.0 copy-start
  57.7 1.0 %copy-done = f32[19,32,512]{2,1,0:T(8,128)} copy-done((f32[19,32,512]{2,1,0:T(8,128)}, f32[19,32,512]{2,1,0:T(8,128)S(1)}, u32[]{:S(2)}) %copy-start) | copy-done | bytes 1245208
Async XLA Ops:
  0.0 56.1 %copy-start.1 = (s32[32]{0:T(128)S(1)}, s32[32]{0:T(128)}, u32[]{:S(2)}) copy-start(s32[32]{0:T(128)} %param.7) | copy-start | bytes 388
  57.7 1.0 %copy-start = (f32[19,32,512]{2,1,0:T(8,128)}, f32[19,32,512]{2,1,0:T(8,128)S(1)}, u32[]{:S(2)}) copy-start(f32[19,32,512]{2,1,0:T(8,128)S(1)} %get-tuple-element.32) | copy-start | bytes 3735556

commit v12 on v11

--- a/solution.py
+++ b/solution.py
@@ -715,7 +715,7 @@
             whole[low : low + TAIL, :] = block[MAIN : MAIN + TAIL, :]
         return carry
 
-    lax.fori_loop(0, chunks, assemble, 0)
+    lax.fori_loop(0, chunks, assemble, 0, unroll=True)
     source = lax.broadcasted_iota(jnp.int32, (count, LANES), 0)
     wanted = lax.broadcasted_iota(jnp.int32, (count, LANES), 1).astype(jnp.float32)
     arrived_flat = got_ref.reshape(got_ref.shape[0] * HALF, LANES)

time: 58.9 us -> 58.8 us (level)
  no operation moved by 1% of the time
where the time goes in v12:
time: 58.8 us; the launch traced here: 58.7 us
  Pallas kernels  56.4 us (96%)
  local copies, waits for them, and re-layouts  1.55 us (3%)
  between operations  0.69 us (1%)
    pallas_call x1, Pallas kernels, body(): pl.pallas_call(lambda *refs: lattice_kernel(nb, nc, *refs), out_shape=(ja...  54.9 us
    pallas_call x1, Pallas kernels, unpack(): pl.pallas_call(unpack_kernel, out_shape=jax.ShapeDtypeStruct((19, patches...  1.54 us

profile of v12, /device:TPU:0, one launch (start us, length us, event | category | flops | bytes accessed | tf_op | source)
XLA Modules:
  0.0 58.7 jit_solution(5183552385101439403)
XLA Ops:
  0.0 0.0 copy-start.1
  0.0 54.9 %shard_map.37 = (f32[80,40,128]{2,1,0:T(8,128)S(1)}, f32[32,80,128]{2,1,0:T(8,128)S(1)}, s32[8,128]{1,0:T(8,128)S(1)}) custom-call(s32[32]{0:T(128)} %refs_0_.1, s32[1,32]{1,0:T(1,128)} %bitcast.5, f32[19,32,512]{2,1,0:T(8,128)} %bitcast.4), custom_call_target="tpu_custom_call" | custom-call | tf_op jit(solution)/shard_map/pallas_call | solution.py:810
  54.9 0.5 slice.3
  56.1 0.0 copy-done.1
  56.1 1.6 %conditional.1 = (f32[19,32,512]{2,1,0:T(8,128)S(1)}) conditional(s32[]{:T(128)} %bitcast.2, (s32[8,128]{1,0:T(8,128)S(1)}, f32[80,40,128]{2,1,0:T(8,128)S(1)}) %tuple.11, (s32[32]{0:T(128)S(1)}, f32[32,80,128]{2,1,0:T(8,128)S(1)}) %tuple.17), branch_computations={%region_0.0_spmd, %region_1.5_spmd} | conditional | flops 15968 | bytes 2312 | solution.py:896
  56.1 1.5 %branch_0_fun.1 = f32[19,32,512]{2,1,0:T(8,128)S(1)} custom-call(s32[8,128]{1,0:T(8,128)S(1)} %get-tuple-element.16.ridx, f32[80,40,128]{2,1,0:T(8,128)S(1)} %get-tuple-element.17.got_ref), custom_call_target="tpu_custom_call" | custom-call | tf_op jit(solution)/shard_map/cond/branch_0_fun/pallas_call | solution.py:864
  57.6 0.0 copy-start
  57.7 1.0 %copy-done = f32[19,32,512]{2,1,0:T(8,128)} copy-done((f32[19,32,512]{2,1,0:T(8,128)}, f32[19,32,512]{2,1,0:T(8,128)S(1)}, u32[]{:S(2)}) %copy-start) | copy-done | bytes 1245208
Async XLA Ops:
  0.0 56.1 %copy-start.1 = (s32[32]{0:T(128)S(1)}, s32[32]{0:T(128)}, u32[]{:S(2)}) copy-start(s32[32]{0:T(128)} %param.7) | copy-start | bytes 388
  57.6 1.0 %copy-start = (f32[19,32,512]{2,1,0:T(8,128)}, f32[19,32,512]{2,1,0:T(8,128)S(1)}, u32[]{:S(2)}) copy-start(f32[19,32,512]{2,1,0:T(8,128)S(1)} %get-tuple-element.32) | copy-start | bytes 3735556
